TPU v7x, 32 devices: a whole 2x2x4 slice. The times are simulated.
32 devices in a mesh: client: 4 (over z), tensor: 4 (over x, core), sdata: 2 (over y).
Axes of the slice: x: 2, y: 2, z: 4, core: 2. Of those that a mesh axis runs over, the one named last changes fastest.
Arguments:
- client_input: bfloat16 [3072, 2048], P(('client', 'sdata')), may hold values from -6 to 6
- client_gain: bfloat16 [4, 2048], P('client'), may hold values from 0.5 to 1.5
- query_weight: bfloat16 [4, 2048, 2048], P('client', None, 'tensor'), as said below
- key_weight: bfloat16 [4, 2048, 512], P('client', None, 'tensor'), as said below
- client_value_weight: bfloat16 [4, 2048, 512], P('client', None, 'tensor'), may hold values from -0.125 to 0.125
- output_weight: bfloat16 [4, 2048, 2048], P('client', None, 'tensor'), may hold values from -0.125 to 0.125
- server_gain: bfloat16 [2, 2048], P('sdata'), may hold values from 0.5 to 1.5
- server_gate: bfloat16 [2, 2048, 4096], P('sdata', None, 'tensor'), may hold values from -0.125 to 0.125
- server_up: bfloat16 [2, 2048, 4096], P('sdata', None, 'tensor'), may hold values from -0.125 to 0.125
- server_down: bfloat16 [2, 4096, 2048], P('sdata', 'tensor'), may hold values from -0.09375 to 0.09375
- upstream: bfloat16 [3072, 2048], P(('client', 'sdata')), may hold values from -6 to 6
- assignment: int32 [4], replicated, may hold values from 0 to 1, as said below
Outputs:
- query_update: bfloat16 [2048, 2048], P(('client', 'sdata'), 'tensor')
- key_update: bfloat16 [2048, 512], P(('client', 'sdata'), 'tensor')
- value_update: bfloat16 [2048, 512], P(('client', 'sdata'), 'tensor')
- output_update: bfloat16 [2048, 2048], P(('client', 'sdata'), 'tensor')
Inputs may be any that keep to these rules, and one draw needn't show every extreme that they name: `assignment`: each of the 2 server groups is named by exactly 2 clients. `query_weight`: independent entries with a spread of about 2048 ** -0.5. `key_weight`: entries with a spread of about 2048 ** -0.5 or more.
All inputs are finite; a program needn't handle non-finite values.
Results may differ from a plain program's by a relative error of at most 0.038.
The roundings to bfloat16 on the way count: a program that leaves them out, or rounds other values in their place, can miss the bound.
Values may be sent and summed in bfloat16 or wider, within the bound.
A program may use at most 128 MiB of HBM per device.

v0:
```python
from functools import partial
import math

import jax
import jax.numpy as jnp
from jax import lax
from jax.experimental import pallas as pl
from jax.experimental.pallas import tpu as pltpu
from jax.sharding import PartitionSpec as P

HEAD_DIM = 64
MESH = pl.DeviceIdType.MESH
CORES = 2
BF16 = jnp.bfloat16
F32 = jnp.float32


def rotary_tables(length):
    halfway = HEAD_DIM // 2
    positions = jnp.arange(length).astype(jnp.float32)
    exponents = jnp.arange(halfway).astype(jnp.float32) * (2.0 / HEAD_DIM)
    frequencies = jnp.exp(-math.log(500000.0) * exponents)
    angles = positions[:, None] * frequencies[None, :]
    cosine_table = jnp.concatenate([jnp.cos(angles), jnp.cos(angles)], 1)
    sine_table = jnp.concatenate([jnp.sin(angles), jnp.sin(angles)], 1)
    return (cosine_table, sine_table)


def rotary(heads_in, cosine_table, sine_table):
    halfway = heads_in.shape[-1] // 2
    turned = jnp.concatenate([-heads_in[..., halfway:], heads_in[..., :halfway]], -1)
    return heads_in * cosine_table[:, None, :] + turned * sine_table[:, None, :]


def normalize(rows_in, gain):
    rows_float = rows_in.astype(jnp.float32)
    inv_rms = lax.rsqrt(jnp.mean(rows_float * rows_float, -1, keepdims=True) + 1e-05)
    return (rows_float * inv_rms * gain.astype(jnp.float32)).astype(jnp.bfloat16)


def attention_part(normed, query_matrix, client_key_matrix, value_matrix, output_matrix):
    length = normed.shape[0]
    query_count = query_matrix.shape[1] // HEAD_DIM
    shared_count = client_key_matrix.shape[1] // HEAD_DIM
    group_size = query_count // shared_count
    cosine_table, sine_table = rotary_tables(length)
    queries = jnp.dot(normed, query_matrix, preferred_element_type=jnp.float32).reshape(
        length, query_count, HEAD_DIM
    )
    queries = (
        rotary(queries, cosine_table, sine_table)
        .astype(jnp.bfloat16)
        .reshape(length, shared_count, group_size, HEAD_DIM)
    )
    key_heads = jnp.dot(normed, client_key_matrix, preferred_element_type=jnp.float32).reshape(
        length, shared_count, HEAD_DIM
    )
    key_heads = rotary(key_heads, cosine_table, sine_table).astype(jnp.bfloat16)
    value_heads = (
        jnp.dot(normed, value_matrix, preferred_element_type=jnp.float32)
        .astype(jnp.bfloat16)
        .reshape(length, shared_count, HEAD_DIM)
    )
    scores = jnp.einsum(
        "qgrd,kgd->grqk", queries.astype(jnp.float32), key_heads.astype(jnp.float32)
    ) * HEAD_DIM ** (-0.5)
    row_ids = lax.broadcasted_iota(jnp.int32, (length, length), 0)
    col_ids = lax.broadcasted_iota(jnp.int32, (length, length), 1)
    scores = jnp.where(col_ids <= row_ids, scores, -1e30)
    highest = lax.stop_gradient(jnp.max(scores, -1, keepdims=True))
    exponent = jnp.exp(scores - highest)
    weights = (exponent / jnp.sum(exponent, -1, keepdims=True)).astype(jnp.bfloat16)
    context = jnp.einsum(
        "grqk,kgd->qgrd", weights.astype(jnp.float32), value_heads.astype(jnp.float32)
    )
    context = context.astype(jnp.bfloat16).reshape(length, query_count * HEAD_DIM)
    return lax.dot_general(
        context, output_matrix, (((1,), (1,)), ((), ())), preferred_element_type=jnp.float32
    )


def server_kernel(
    rows_ref, upstream_ref, gain_ref, gate_ref, up_ref, down_ref, out_ref, normed_ref, total_ref
):
    step = pl.program_id(0)

    def inverse_rms(rows_float):
        return lax.rsqrt(jnp.mean(rows_float * rows_float, -1, keepdims=True) + 1e-05)

    @pl.when(step == 0)
    def _():
        rows_float = rows_ref[...].astype(F32)
        normed_ref[...] = (
            rows_float * inverse_rms(rows_float) * gain_ref[...].astype(F32)
        ).astype(BF16)

    gate, up = gate_ref[...], up_ref[...]
    crossed = (((1,), (1,)), ((), ()))
    gate_value = jnp.dot(normed_ref[...], gate, preferred_element_type=F32)
    up_value = jnp.dot(normed_ref[...], up, preferred_element_type=F32)
    pulled = lax.dot_general(
        upstream_ref[...], down_ref[...], crossed, preferred_element_type=F32
    )
    sigmoid_gate = jax.nn.sigmoid(gate_value)
    gate_grad = (
        pulled * up_value * sigmoid_gate * (1.0 + gate_value * (1.0 - sigmoid_gate))
    ).astype(BF16)
    up_grad = (pulled * gate_value * sigmoid_gate).astype(BF16)
    normed_grad = lax.dot_general(
        gate_grad, gate, crossed, preferred_element_type=F32
    ) + lax.dot_general(up_grad, up, crossed, preferred_element_type=F32)

    @pl.when(step == 0)
    def _():
        total_ref[...] = normed_grad

    @pl.when(step > 0)
    def _():
        total_ref[...] += normed_grad

    @pl.when(step == pl.num_programs(0) - 1)
    def _():
        rows_float = rows_ref[...].astype(F32)
        inv_rms = inverse_rms(rows_float)
        weighted = total_ref[...] * gain_ref[...].astype(F32)
        out_ref[...] = (
            inv_rms * weighted
            - rows_float * inv_rms**3 * jnp.mean(weighted * rows_float, -1, keepdims=True)
        ).astype(BF16)


def server_pull(rows_in, upstream_rows, gain, gate_matrix, up_matrix, down_matrix):
    length, breadth = rows_in.shape
    hidden = gate_matrix.shape[1]
    block = next(b for b in (256, 128, hidden) if hidden % b == 0)
    whole = pl.BlockSpec((length, breadth), lambda i: (0, 0))
    tall = pl.BlockSpec((breadth, block), lambda i: (0, i))
    return pl.pallas_call(
        server_kernel,
        grid=(hidden // block,),
        out_shape=jax.ShapeDtypeStruct((length, breadth), BF16),
        in_specs=[
            whole,
            whole,
            pl.BlockSpec((1, breadth), lambda i: (0, 0)),
            tall,
            tall,
            pl.BlockSpec((block, breadth), lambda i: (i, 0)),
        ],
        out_specs=whole,
        scratch_shapes=[pltpu.VMEM((length, breadth), BF16), pltpu.VMEM((length, breadth), F32)],
        compiler_params=pltpu.CompilerParams(vmem_limit_bytes=48 * 2**20),
        name="server_pull",
    )(rows_in, upstream_rows, gain[None], gate_matrix, up_matrix, down_matrix)


def greet(others):
    barrier = pltpu.get_barrier_semaphore()
    for other in others:
        pl.semaphore_signal(barrier, inc=1, device_id=other, device_id_type=MESH)
    pl.semaphore_wait(barrier, len(others))


def send(source, target, send_sem, recv_sem, device):
    copy = pltpu.make_async_remote_copy(
        src_ref=source,
        dst_ref=target,
        send_sem=send_sem,
        recv_sem=recv_sem,
        device_id=device,
        device_id_type=MESH,
    )
    copy.start()
    return copy


def place():
    tensor_at = lax.axis_index("tensor")
    return tensor_at // CORES, lax.rem(tensor_at, CORES)


def turned(index, step, count):
    return lax.rem(index + step, count)


def columns_of(chip, core, width):
    return pl.ds(pl.multiple_of((chip * CORES + core) * width, width), width)


def partners(chips, client_count, group_count):
    chip, core = place()
    client, group = lax.axis_index("client"), lax.axis_index("sdata")
    others = [{"tensor": chip * CORES + 1 - core}]
    others += [{"tensor": turned(chip, k, chips) * CORES + core} for k in range(1, chips)]
    others += [{"client": turned(client, k, client_count)} for k in range(1, client_count)]
    others += [{"sdata": turned(group, k, group_count)} for k in range(1, group_count)]
    return others


class ShareSum:
    def __init__(self, part, pair, relay, landed, sems, chunks, chips):
        self.part, self.pair, self.relay, self.landed = part, pair, relay, landed
        self.pair_send, self.pair_recv, self.chip_send, self.chip_recv = sems
        self.chips, self.width = chips, part.shape[-1] // (CORES * chips)
        self.chip, self.core = place()
        self.copies = []
        self.pair_copies = {}
        self.chip_copies = {}
        for n, q in enumerate(chunks):
            for k in list(range(1, chips)) + [0]:
                to = turned(self.chip, k, chips)
                copy = send(
                    part.at[q, :, columns_of(to, 1 - self.core, self.width)],
                    pair.at[k, q],
                    self.pair_send.at[k, n],
                    self.pair_recv.at[k, n],
                    {"tensor": self.chip * CORES + 1 - self.core},
                )
                self.pair_copies[k, n] = copy
        for n, q in enumerate(chunks):
            for k in range(1, chips):
                to = turned(self.chip, k, chips)
                self.pair_copies[k, n].wait_recv()
                relay[k, q] = (
                    part[q, :, columns_of(to, self.core, self.width)].astype(F32)
                    + pair[k, q].astype(F32)
                ).astype(BF16)
                self.chip_copies[k, n] = send(
                    relay.at[k, q],
                    landed.at[k, q],
                    self.chip_send.at[k, n],
                    self.chip_recv.at[k, n],
                    {"tensor": to * CORES + self.core},
                )

    def get(self, n, q):
        self.pair_copies[0, n].wait_recv()
        total = self.part[q, :, columns_of(self.chip, self.core, self.width)].astype(
            F32
        ) + self.pair[0, q].astype(F32)
        for k in range(1, self.chips):
            self.chip_copies[k, n].wait_recv()
            total = total + self.landed[k, q].astype(F32)
        return total

    def finish(self):
        for copy in list(self.pair_copies.values()) + list(self.chip_copies.values()):
            copy.wait_send()


class Widen:
    def __init__(self, out, sems, chips):
        self.out, self.chips = out, chips
        self.chip_send, self.chip_recv, self.pair_send, self.pair_recv = sems
        self.chip, self.core = place()
        self.width = out.shape[-1] // (CORES * chips)
        self.started, self.forwarded, self.chip_copies = [], [], {}

    def pair_copy(self, source, k, n, q):
        cols = columns_of(turned(self.chip, self.chips - k, self.chips), self.core, self.width)
        self.forwarded.append(
            send(
                source,
                self.out.at[q, :, cols],
                self.pair_send.at[k, n],
                self.pair_recv.at[k, n],
                {"tensor": self.chip * CORES + 1 - self.core},
            )
        )

    def start(self, source, n, q):
        cols = columns_of(self.chip, self.core, self.width)
        for k in range(1, self.chips):
            self.chip_copies[k, n] = send(
                source,
                self.out.at[q, :, cols],
                self.chip_send.at[k, n],
                self.chip_recv.at[k, n],
                {"tensor": turned(self.chip, k, self.chips) * CORES + self.core},
            )
        self.pair_copy(source, 0, n, q)
        self.out[q, :, cols] = source[...]

    def forward(self, n, q):
        for k in range(1, self.chips):
            self.chip_copies[k, n].wait_recv()
            cols = columns_of(turned(self.chip, self.chips - k, self.chips), self.core, self.width)
            self.pair_copy(self.out.at[q, :, cols], k, n, q)

    def finish(self):
        for copy in self.forwarded:
            copy.wait_recv()
        for copy in self.forwarded + list(self.chip_copies.values()):
            copy.wait_send()


def out_kernel(
    chips, client_count, group_count,
    order, part, inputs, upstream,
    cut_out, up_out, up_own,
    pair, relay, landed, cut_from, cut_at, up_at, cut_put, up_put, cut_own,
    tp_sems, z_sems, y_sems, wide_sems,
):
    client, group = lax.axis_index("client"), lax.axis_index("sdata")
    chip, core = place()
    share = client_count // group_count
    width = part.shape[-1] // (CORES * chips)
    cols = columns_of(chip, core, width)
    greet(partners(chips, client_count, group_count))
    steps = list(range(1, client_count)) + [0]
    targets = [turned(client, k, client_count) for k in steps]
    up_z = []
    sums = ShareSum(part, pair, relay, landed, [tp_sems.at[i] for i in range(4)], targets, chips)
    for k in range(1, client_count):
        to = turned(client, k, client_count)
        up_z.append(
            send(
                upstream.at[to, :, cols], up_at.at[client],
                z_sems.at[0, k], z_sems.at[1, k], {"client": to},
            )
        )
    up_at[client] = upstream[client, :, cols]
    cut_z = []
    for n, (k, to) in enumerate(zip(steps, targets)):
        block = (sums.get(n, to) + inputs[to, :, cols].astype(F32)).astype(BF16)
        if k == 0:
            cut_at[client] = block
        else:
            cut_from[k] = block
            cut_z.append(
                send(
                    cut_from.at[k], cut_at.at[client],
                    z_sems.at[2, k], z_sems.at[3, k], {"client": to},
                )
            )
    widens = [
        Widen(up_out, [wide_sems.at[i] for i in range(4)], chips),
        Widen(cut_out, [wide_sems.at[i] for i in range(4, 8)], chips),
    ]
    rounds = []
    for which, (z_copies, at, put, own) in enumerate(
        ((up_z, up_at, up_put, up_own), (cut_z, cut_at, cut_put, cut_own))
    ):
        for copy in z_copies:
            copy.wait_recv()
        y_copies = []
        for d in range(1, group_count):
            to = turned(group, d, group_count)
            for i in range(share):
                put[d, i] = at[order[to * share + i]]
                y_copies.append(
                    (
                        send(
                            put.at[d, i], own.at[group * share + i],
                            y_sems.at[2 * which, d, i], y_sems.at[2 * which + 1, d, i],
                            {"sdata": to},
                        ),
                        turned(group, group_count - d, group_count) * share + i,
                    )
                )
        n = 0
        for i in range(share):
            q = group * share + i
            own[q] = at[order[group * share + i]]
            widens[which].start(own.at[q], n, q)
            rounds.append((which, n, q))
            n += 1
        for copy, q in y_copies:
            copy.wait_recv()
            widens[which].start(own.at[q], n, q)
            rounds.append((which, n, q))
            n += 1
        for copy, q in y_copies:
            copy.wait_send()
    for which, n, q in rounds:
        widens[which].forward(n, q)
    for widen in widens:
        widen.finish()
    sums.finish()
    for copy in up_z + cut_z:
        copy.wait_send()


def back_kernel(
    chips, client_count, group_count,
    inverse, part, up_own,
    grad_out,
    pair, relay, landed, y_from, y_at, z_from, own,
    tp_sems, y_sems, z_sems, wide_sems,
):
    client, group = lax.axis_index("client"), lax.axis_index("sdata")
    share = client_count // group_count
    greet(partners(chips, client_count, group_count))
    steps = [(d, i) for d in list(range(1, group_count)) + [0] for i in range(share)]
    chunks = [turned(group, d, group_count) * share + i for d, i in steps]
    sums = ShareSum(part, pair, relay, landed, [tp_sems.at[i] for i in range(4)], chunks, chips)
    y_copies = []
    for n, ((d, i), q) in enumerate(zip(steps, chunks)):
        block = (sums.get(n, q) + up_own[q].astype(F32)).astype(BF16)
        if d == 0:
            y_at[group * share + i] = block
        else:
            y_from[d, i] = block
            y_copies.append(
                send(
                    y_from.at[d, i], y_at.at[group * share + i],
                    y_sems.at[0, d, i], y_sems.at[1, d, i],
                    {"sdata": turned(group, d, group_count)},
                )
            )
    for copy in y_copies:
        copy.wait_recv()
    widen = Widen(grad_out, [wide_sems.at[i] for i in range(4)], chips)
    z_copies = []
    for k in list(range(1, client_count)):
        to = turned(client, k, client_count)
        z_from[k] = y_at[inverse[to]]
        z_copies.append(
            send(
                z_from.at[k], own.at[client], z_sems.at[0, k], z_sems.at[1, k], {"client": to}
            )
        )
    own[client] = y_at[inverse[client]]
    widen.start(own.at[client], 0, client)
    for k, copy in enumerate(z_copies, 1):
        copy.wait_recv()
        source = turned(client, client_count - k, client_count)
        widen.start(own.at[source], k, source)
    for k in range(client_count):
        widen.forward(k, turned(client, client_count - k, client_count))
    widen.finish()
    sums.finish()
    for copy in y_copies + z_copies:
        copy.wait_send()


def average_kernel(client_count, group_count, count, *refs):
    early, grads, outs = refs[0], refs[1 : count + 1], refs[count + 1 : 2 * count + 1]
    refs = refs[1:]
    y_at, z_from, z_at = (refs[(2 + i) * count : (3 + i) * count] for i in range(3))
    y_sems, z_sems = refs[5 * count :]
    client, group = lax.axis_index("client"), lax.axis_index("sdata")
    others = [{"client": turned(client, k, client_count)} for k in range(1, client_count)]
    others += [{"sdata": turned(group, k, group_count)} for k in range(1, group_count)]
    greet(others)
    middle = client_count // 2
    steps = [(middle + k) % client_count for k in range(client_count)]
    steps = [k for k in steps if k != 0] + [0]
    y_copies = {}
    for k in steps:
        to = turned(client, k, client_count)
        for a in range(1, count):
            for d in range(1, group_count):
                y_copies[k, a, d] = send(
                    grads[a].at[to, turned(group, d, group_count)], y_at[a].at[d, to],
                    y_sems.at[0, a, d, k], y_sems.at[1, a, d, k],
                    {"sdata": turned(group, d, group_count)},
                )
    z_copies = []
    rows = outs[0].shape[0]
    block = next(b for b in (64, 32, 16, rows) if rows % b == 0)
    for k, a in [(k, 0) for k in steps] + [(k, a) for k in steps for a in range(1, count)]:
            to = turned(client, k, client_count)
            for d in range(1, group_count if a else 1):
                y_copies[k, a, d].wait_recv()
            for r in range(0, rows, block):
                at = pl.ds(r, block)
                total = grads[a][to, group, at, :].astype(F32)
                for d in range(1, group_count):
                    other = y_at[a][d, to, at, :] if a else early[d - 1, to, at, :]
                    total = total + other.astype(F32)
                z_from[a][k, at, :] = total.astype(BF16)
            if k != 0:
                z_copies.append(
                    send(
                        z_from[a].at[k], z_at[a].at[k],
                        z_sems.at[0, a, k], z_sems.at[1, a, k], {"client": to},
                    )
                )
    for copy in z_copies:
        copy.wait_recv()
    for a in range(count):
        for r in range(0, rows, block):
            at = pl.ds(r, block)
            total = z_from[a][0, at, :].astype(F32)
            for k in range(1, client_count):
                total = total + z_at[a][k, at, :].astype(F32)
            outs[a][at, :] = (total * (1.0 / client_count)).astype(BF16)
    for copy in list(y_copies.values()) + z_copies:
        copy.wait_send()


VMEM_SPEC = pl.BlockSpec(memory_space=pltpu.VMEM)
SMEM_SPEC = pl.BlockSpec(memory_space=pltpu.SMEM)


def params(number):
    return pltpu.CompilerParams(
        collective_id=number, has_side_effects=True, vmem_limit_bytes=48 * 2**20
    )


def axis_counts():
    return lax.axis_size("tensor") // CORES, lax.axis_size("client"), lax.axis_size("sdata")


def relay_out(order, attended, rows_in, upstream):
    chips, client_count, group_count = axis_counts()
    length, breadth = rows_in.shape
    chunk, width = length // client_count, breadth // (CORES * chips)
    share = client_count // group_count
    full = (client_count, chunk, breadth)
    own = (client_count, chunk, width)
    dma = pltpu.SemaphoreType.DMA
    vmem = lambda shape: pltpu.VMEM(shape, BF16)
    cut, up, up_own = pl.pallas_call(
        partial(out_kernel, chips, client_count, group_count),
        out_shape=(
            jax.ShapeDtypeStruct(full, BF16),
            jax.ShapeDtypeStruct(full, BF16),
            jax.ShapeDtypeStruct(own, BF16),
        ),
        in_specs=[SMEM_SPEC, VMEM_SPEC, VMEM_SPEC, VMEM_SPEC],
        out_specs=(VMEM_SPEC,) * 3,
        scratch_shapes=[
            vmem((chips,) + own), vmem((chips,) + own), vmem((chips,) + own),
            vmem(own), vmem(own), vmem(own),
            vmem((group_count, share, chunk, width)), vmem((group_count, share, chunk, width)),
            vmem(own),
            dma((4, chips, client_count)), dma((4, client_count)),
            dma((4, group_count, share)), dma((8, chips, client_count)),
        ],
        compiler_params=params(1),
        name="relay_out",
    )(order, attended.reshape(full), rows_in.reshape(full), upstream.reshape(full))
    return cut.reshape(length, breadth), up.reshape(length, breadth), up_own


def relay_back(inverse, pulled, up_own):
    chips, client_count, group_count = axis_counts()
    length, breadth = pulled.shape
    chunk, width = length // client_count, breadth // (CORES * chips)
    share = client_count // group_count
    full = (client_count, chunk, breadth)
    own = (client_count, chunk, width)
    dma = pltpu.SemaphoreType.DMA
    vmem = lambda shape: pltpu.VMEM(shape, BF16)
    grad = pl.pallas_call(
        partial(back_kernel, chips, client_count, group_count),
        out_shape=jax.ShapeDtypeStruct(full, BF16),
        in_specs=[SMEM_SPEC, VMEM_SPEC, VMEM_SPEC],
        out_specs=VMEM_SPEC,
        scratch_shapes=[
            vmem((chips,) + own), vmem((chips,) + own), vmem((chips,) + own),
            vmem((group_count, share, chunk, width)), vmem(own), vmem(own), vmem(own),
            dma((4, chips, client_count)), dma((2, group_count, share)),
            dma((2, client_count)), dma((4, chips, client_count)),
        ],
        compiler_params=params(2),
        name="relay_back",
    )(inverse, pulled.reshape(full), up_own)
    return grad.reshape(length, breadth)


def send_early(grad):
    unused, client_count, group_count = axis_counts()
    group = lax.axis_index("sdata")
    blocks = grad.reshape(client_count, group_count, -1, grad.shape[1])
    arrived = []
    for d in range(1, group_count):
        block = lax.dynamic_index_in_dim(blocks, turned(group, d, group_count), 1, False)
        ring = [(g, (g + d) % group_count) for g in range(group_count)]
        arrived.append(lax.ppermute(block, "sdata", ring))
    return jnp.stack(arrived)


def average(early, grads):
    unused, client_count, group_count = axis_counts()
    count = len(grads)
    rows = grads[0].shape[0] // (client_count * group_count)
    widths = [grad.shape[1] for grad in grads]
    dma = pltpu.SemaphoreType.DMA
    return pl.pallas_call(
        partial(average_kernel, client_count, group_count, count),
        out_shape=tuple(jax.ShapeDtypeStruct((rows, width), BF16) for width in widths),
        in_specs=[VMEM_SPEC] * (count + 1),
        out_specs=(VMEM_SPEC,) * count,
        scratch_shapes=[
            pltpu.VMEM((group_count, client_count, rows, w) if n else (16, 128), BF16)
            for n, w in enumerate(widths)
        ]
        + [pltpu.VMEM((client_count, rows, w), BF16) for w in widths]
        + [pltpu.VMEM((client_count, rows, w), BF16) for w in widths]
        + [dma((2, count, group_count, client_count)), dma((2, count, client_count))],
        compiler_params=params(3),
        name="average",
    )(early, *[grad.reshape(client_count, group_count, rows, grad.shape[1]) for grad in grads])


def local(
    client_input,
    client_gain,
    query_weight,
    key_weight,
    client_value_weight,
    output_weight,
    server_gain,
    server_gate,
    server_up,
    server_down,
    upstream,
    assignment,
):
    client_count = lax.axis_size("client")
    normed = normalize(client_input, client_gain[0])
    attended, pullback = jax.vjp(
        partial(attention_part, normed),
        query_weight[0],
        key_weight[0],
        client_value_weight[0],
        output_weight[0],
    )
    ids = jnp.arange(client_count).astype(jnp.int32)
    ahead = (assignment[None, :] < assignment[:, None]) | (
        (assignment[None, :] == assignment[:, None]) & (ids[None, :] < ids[:, None])
    )
    inverse = jnp.sum(ahead.astype(jnp.int32), 1)
    group_order = jnp.sum(jnp.where(inverse[None, :] == ids[:, None], ids[None, :], 0), 1)
    cut_rows, up_rows, up_own = relay_out(
        group_order, attended.astype(BF16), client_input, upstream
    )
    pulled = server_pull(
        cut_rows, up_rows, server_gain[0], server_gate[0], server_up[0], server_down[0]
    )
    arriving_grad = relay_back(inverse, pulled, up_own)
    query_grad, key_grad, value_grad, output_grad = pullback(arriving_grad.astype(jnp.float32))
    output_update, query_update, key_update, value_update = average(
        send_early(output_grad), [output_grad, query_grad, key_grad, value_grad]
    )
    return (query_update, key_update, value_update, output_update)


def solution(mesh):
    placed = (
        P(("client", "sdata"), None),
        P("client", None),
        P("client", None, "tensor"),
        P("client", None, "tensor"),
        P("client", None, "tensor"),
        P("client", None, "tensor"),
        P("sdata", None),
        P("sdata", None, "tensor"),
        P("sdata", None, "tensor"),
        P("sdata", "tensor", None),
        P(("client", "sdata"), None),
        P(),
    )
    return jax.shard_map(
        local,
        mesh=mesh,
        in_specs=placed,
        out_specs=(
            P(("client", "sdata"), "tensor"),
            P(("client", "sdata"), "tensor"),
            P(("client", "sdata"), "tensor"),
            P(("client", "sdata"), "tensor"),
        ),
        check_vma=False,
    )
```

profile of v0, /device:TPU:8, one launch (start us, length us, event | category | flops | bytes accessed | tf_op | source)
XLA Modules:
  0.0 211.7 jit_solution(6918875920300330697)
XLA Ops:
  0.7 1.0 convert_reduce_fusion.inverse
  1.8 1.8 fusion.8
  3.6 0.7 mul.209
  4.4 1.2 copy.26
  5.6 3.0 %convolution_convert_fusion.8 = bf16[384,128]{0,1:T(8,128)(2,1)} fusion(bf16[1,2048,128]{2,1,0:T(8,128)(2,1)} %param.16, bf16[384,2048]{1,0:T(8,128)(2,1)} %param.12, f32[2048]{0:T(1024)S(1)} %bitcast.174, f32[384]{0:T(512)S(1)} %add_rsqrt_fusion), kind=kOutput, calls=%fused_computation.41 | convolution fusion | flops 204521472 | bytes 2205184 | tf_op jit(solution)/shard_map/jvp()/dot_general | solution.py:60
  8.6 0.7 fusion.17
  9.4 4.0 %copy.27 = bf16[1,2048,512]{1,2,0:T(8,128)(2,1)} copy(bf16[1,2048,512]{2,1,0:T(8,128)(2,1)} %param.14) | data formatting | bytes 4194304 | tf_op args[2]
  13.3 3.4 %fusion.15 = f32[384,8,64]{0,2,1:T(8,128)S(1)} fusion(bf16[8,64,2048]{2,1,0:T(8,128)(2,1)} %bitcast.160, bf16[384,2048]{1,0:T(8,128)(2,1)} %param.12, f32[2048]{0:T(1024)S(1)} %bitcast.176, f32[384]{0:T(512)S(1)} %add_rsqrt_fusion), kind=kOutput, calls=%fused_computation.28 | convolution fusion | flops 808452096 | bytes 4466176 | tf_op jit(solution)/shard_map/jvp()/dot_general | solution.py:47
  17.3 0.9 fusion.7
  18.2 1.0 fusion.11
  19.3 1.1 divide_convert_fusion
  21.0 1.0 convolution_convert_fusion.2
  22.1 42.2 %relay_out.1 = (bf16[4,96,2048]{2,1,0:T(8,128)(2,1)S(1)}, bf16[4,96,2048]{2,1,0:T(8,128)(2,1)S(1)}, bf16[4,96,512]{2,1,0:T(8,128)(2,1)S(1)}) custom-call(s32[4]{0:T(128)S(1)} %select_reduce_fusion.order, bf16[4,96,2048]{2,1,0:T(8,128)(2,1)S(1)} %bitcast.143, bf16[4,96,2048]{2,1,0:T(8,128)(2,1)} %bitcast.153, bf16[4,96,2048]{2,1,0:T(8,128)(2,1)} %bitcast.161), custom_call_target="tpu_custom_call" | custom-call | tf_op jit(solution)/shard_map/relay_out/pallas_call | solution.py:516
  64.3 20.6 %server_pull.1 = bf16[384,2048]{1,0:T(8,128)(2,1)S(1)} custom-call(bf16[384,2048]{1,0:T(8,128)(2,1)S(1)} %bitcast.146, bf16[384,2048]{1,0:T(8,128)(2,1)S(1)} %bitcast.147, bf16[1,2048]{1,0:T(2,128)(2,1)S(1)} %copy-done.3, bf16[2048,1024]{1,0:T(8,128)(2,1)} %bitcast.154, bf16[2048,1024]{1,0:T(8,128)(2,1)} %bitcast.155, bf16[1024,2048]{1,0:T(8,128)(2,1)} %bitcast.156), custom_call_target="tpu_custom_call" | custom-call | tf_op jit(solution)/shard_map/server_pull/pallas_call | solution.py:138
  84.9 28.8 %relay_back.1 = bf16[4,96,2048]{2,1,0:T(8,128)(2,1)S(1)} custom-call(s32[4]{0:T(128)S(1)} %convert_reduce_fusion.inverse, bf16[4,96,2048]{2,1,0:T(8,128)(2,1)S(1)} %bitcast.140, bf16[4,96,512]{2,1,0:T(8,128)(2,1)S(1)} %get-tuple-element.13.up_own), custom_call_target="tpu_custom_call" | custom-call | tf_op jit(solution)/shard_map/relay_back/pallas_call | solution.py:548
  113.7 1.1 copy-done.2
  114.8 2.7 %convolution_convert_fusion.1 = bf16[2048,512]{1,0:T(8,128)(2,1)} fusion(bf16[384,2048]{1,0:T(8,128)(2,1)S(1)} %bitcast.144, bf16[384,512]{0,1:T(8,128)(2,1)S(1)} %bitcast.166), kind=kOutput, calls=%fused_computation.19 | convolution fusion | flops 806354944 | bytes 4063232 | tf_op jit(solution)/shard_map/transpose(jvp())/dot_general | solution.py:77
  117.5 2.3 %dynamic-slice_bitcast_fusion = bf16[4,256,512]{2,1,0:T(8,128)(2,1)} fusion(bf16[4,2,256,512]{3,2,1,0:T(8,128)(2,1)} %bitcast.141, s32[]{:T(128)S(6)} %select_n.22), kind=kLoop, calls=%fused_computation.42 | loop fusion | bytes 2097156 | tf_op jit(solution)/shard_map/jit(dynamic_index_in_dim)/squeeze | solution.py:571
  119.8 1.3 collective-permute-start
  121.7 3.1 %fusion.19 = bf16[384,512]{1,0:T(8,128)(2,1)} fusion(bf16[384,2048]{1,0:T(8,128)(2,1)} %bitcast.145, bf16[1,2048,512]{2,1,0:T(8,128)(2,1)S(1)} %copy-done), kind=kOutput, calls=%fused_computation.32 | convolution fusion | flops 805502976 | bytes 4063232 | tf_op jit(solution)/shard_map/transpose(jvp())/dot_general | solution.py:77
  124.9 1.9 copy.29
  126.8 2.8 %fusion.25 = bf16[2,64,384]{2,1,0:T(8,128)(2,1)S(1)} fusion(bf16[2,64,4,384]{3,1,2,0:T(8,128)(2,1)} %bitcast.162, bf16[2,4,384,384]{2,3,1,0:T(8,128)(2,1)} %copy-done.5), kind=kOutput, calls=%fused_computation.40 | convolution fusion | flops 151044096 | bytes 2850816 | tf_op jit(solution)/shard_map/transpose(jvp(grqk,kgd->qgrd))/dot_general | solution.py:73
  129.6 4.2 %fusion.6 = (f32[2,4,384]{2,1,0:T(4,128)S(1)}, bf16[2,4,384,384]{2,3,1,0:T(8,128)(2,1)S(1)}) fusion(f32[2,384,384,4]{2,1,3,0:T(8,128)} %copy-done.4, f32[2,4,384]{2,1,0:T(4,128)S(1)} %multiply_divide_fusion, f32[2,4,384]{2,1,0:T(4,128)S(1)} %get-tuple-element.28, pred[384,384]{0,1:T(8,128)(4,1)S(1)} %iota_compare_fusion.1, ...), kind=kOutput, calls=%fused_computation.8 | convolution fusion | flops 160429056 | bytes 7753728 | tf_op jit(solution)/shard_map/transpose(jvp(grqk,kgd->qgrd))/dot_general | solution.py:73
  133.9 2.2 %fusion.4 = bf16[2,384,384,4]{2,1,3,0:T(8,128)(2,1)S(1)} fusion(bf16[2,4,384,384]{2,3,1,0:T(8,128)(2,1)S(1)} %get-tuple-element.31, f32[2,384,384,4]{2,1,3,0:T(8,128)S(1)} %bitcast.152, f32[2,384,4]{1,2,0:T(4,128)S(1)} %bitcast.168, f32[2,384,4]{1,2,0:T(4,128)S(1)} %negate_bitcast_fusion, f32[2,384,4]{1,2,0:T(4,128)S(1)} %bitcast.169, ...), kind=kLoop, calls=%fused_computation.6 | loop fusion | flops 11796480 | bytes 9621504 | tf_op jit(solution)/shard_map/transpose(jvp())/mul | solution.py:64
  136.0 0.8 fusion.24
  137.8 1.1 copy-done.7
  138.9 0.8 convolution_convert_fusion.3
  139.6 0.8 convolution_convert_fusion.4
  140.4 2.8 %convolution_convert_fusion = bf16[2048,512]{1,0:T(8,128)(2,1)} fusion(bf16[384,512]{0,1:T(8,128)(2,1)S(1)} %bitcast.167, bf16[384,2048]{1,0:T(8,128)(2,1)S(1)} %copy-done.7, f32[2048]{0:T(1024)S(1)} %bitcast.179, f32[384]{0:T(512)S(1)} %add_rsqrt_fusion), kind=kOutput, calls=%fused_computation.18 | convolution fusion | flops 808452096 | bytes 4072960 | tf_op jit(solution)/shard_map/transpose(jvp())/dot_general | solution.py:47
  143.2 2.2 %collective-permute-done = bf16[4,256,512]{2,1,0:T(8,128)(2,1)S(1)} collective-permute-done((bf16[4,256,512]{2,1,0:T(8,128)(2,1)}, bf16[4,256,512]{2,1,0:T(8,128)(2,1)S(1)}, u32[]{:S(2)}, u32[]{:S(2)}) %collective-permute-start) | collective-permute-done | bytes 1048608 | tf_op jit(solution)/shard_map/ppermute | solution.py:573
  145.4 63.6 %average.1 = (bf16[256,512]{1,0:T(8,128)(2,1)S(1)}, bf16[256,512]{1,0:T(8,128)(2,1)S(1)}, bf16[256,128]{1,0:T(8,128)(2,1)S(1)}, bf16[256,128]{1,0:T(8,128)(2,1)S(1)}) custom-call(bf16[1,4,256,512]{3,2,1,0:T(8,128)(2,1)S(1)} %bitcast.148, bf16[4,2,256,512]{3,2,1,0:T(8,128)(2,1)S(1)} %bitcast.142, bf16[4,2,256,512]{3,2,1,0:T(8,128)(2,1)} %bitcast.159, ...), custom_call_target="tpu_custom_call" | custom-call | tf_op jit(solution)/shard_map/average/pallas_call | solution.py:583
  209.0 0.7 copy.41
  (56 shorter events, 4.9 us)
Async XLA Ops:
  0.6 20.4 %copy-start = (bf16[1,2048,512]{2,1,0:T(8,128)(2,1)S(1)}, bf16[1,2048,512]{2,1,0:T(8,128)(2,1)}, u32[]{:S(2)}) copy-start(bf16[1,2048,512]{2,1,0:T(8,128)(2,1)} %param.17) | copy-start | bytes 6291460
  5.6 3.0 %copy-start.6 = (bf16[384,2048]{1,0:T(8,128)(2,1)S(1)}, bf16[384,2048]{1,0:T(8,128)(2,1)}, u32[]{:S(2)}) copy-start(bf16[384,2048]{1,0:T(8,128)(2,1)} %param.12) | copy-start | bytes 4718596
  17.1 1.1 copy-start.10
  17.3 1.9 copy-start.8
  18.2 2.2 %copy-start.4 = (f32[2,384,384,4]{2,1,3,0:T(8,128)}, f32[2,384,384,4]{2,1,3,0:T(8,128)S(1)}, u32[]{:S(2)}) copy-start(f32[2,384,384,4]{2,1,3,0:T(8,128)S(1)} %get-tuple-element.29) | copy-start | bytes 14155780
  19.3 1.2 copy-start.13
  20.4 1.6 copy-start.5
  22.1 42.3 %copy-start.3 = (bf16[1,2048]{1,0:T(2,128)(2,1)S(1)}, bf16[1,2048]{1,0:T(2,128)(2,1)}, u32[]{:S(2)}) copy-start(bf16[1,2048]{1,0:T(2,128)(2,1)} %gain_ref.1) | copy-start | bytes 12292
  113.7 1.2 copy-start.2
  119.8 25.6 %collective-permute-start = (bf16[4,256,512]{2,1,0:T(8,128)(2,1)}, bf16[4,256,512]{2,1,0:T(8,128)(2,1)S(1)}, u32[]{:S(2)}, u32[]{:S(2)}) collective-permute-start(bf16[4,256,512]{2,1,0:T(8,128)(2,1)} %dynamic-slice_bitcast_fusion), channel_id=1, source_target_pairs={{0,1},{1,0},{2,3},{3,2},{4,5},{5,4},{6,7},{7,6},{8,9},{9,8},{10,11... | collective-permute-start | bytes 3145736 | tf_op jit(solution)/shard_map/ppermute | solution.py:573
  126.8 7.0 %slice-start = ((s8[4718592]{0:T(1024)(128)(4,1)}), s8[4194304]{0:T(1024)(128)(4,1)S(1)}, s32[]{:S(2)}) async-start(s8[4718592]{0:T(1024)(128)(4,1)} %bitcast.151), calls=%async_computation | async-start | bytes 8388608
  129.6 4.3 %slice-start.1 = ((s8[4718592]{0:T(1024)(128)(4,1)}), s8[524288]{0:T(1024)(128)(4,1)S(1)}, s32[]{:S(2)}) async-start(s8[4718592]{0:T(1024)(128)(4,1)} %bitcast.151), calls=%async_computation.1 | async-start | bytes 1048576
  129.6 4.3 %copy-start.12 = (pred[384,384]{1,0:T(8,128)(4,1)S(1)}, pred[384,384]{1,0:T(8,128)(4,1)}, u32[]{:S(2)}) copy-start(pred[384,384]{1,0:T(8,128)(4,1)} %iota_compare_fusion) | copy-start | bytes 442372
  133.9 2.2 %copy-start.9 = (bf16[384,8,64]{0,2,1:T(8,128)(2,1)S(1)}, bf16[384,8,64]{0,2,1:T(8,128)(2,1)}, u32[]{:S(2)}) copy-start(bf16[384,8,64]{0,2,1:T(8,128)(2,1)} %copy-done.8) | copy-start | bytes 1179652
  133.9 3.0 %copy-start.11 = (bf16[384,2,64,1]{0,2,3,1:T(8,128)(2,1)S(1)}, bf16[384,2,64,1]{0,2,3,1:T(8,128)(2,1)}, u32[]{:S(2)}) copy-start(bf16[384,2,64,1]{0,2,3,1:T(8,128)(2,1)} %copy-done.10) | copy-start | bytes 294916
  137.4 1.4 copy-start.7
  140.4 5.0 %copy-start.1 = (bf16[2048,512]{1,0:T(8,128)(2,1)S(1)}, bf16[2048,512]{1,0:T(8,128)(2,1)}, u32[]{:S(2)}) copy-start(bf16[2048,512]{1,0:T(8,128)(2,1)} %convolution_convert_fusion.1) | copy-start | bytes 6291460
where the time goes:
time: 212 us
  Pallas kernels  155 us (73%)
  matrix products  28 us (13%)
  local copies, waits for them, and re-layouts  14.4 us (7%)
  other arithmetic  9.55 us (5%)
  waiting for transfers between devices  2.25 us (1%)
    pallas_call x1, Pallas kernels, average(): pl.pallas_call(partial(average_kernel, client_count, group_count, count),...  63.6 us
    pallas_call x1, Pallas kernels, relay_out(): pl.pallas_call(partial(out_kernel, chips, client_count, group_count), out...  42.2 us
    pallas_call x1, Pallas kernels, relay_back(): pl.pallas_call(partial(back_kernel, chips, client_count, group_count), ou...  28.8 us
    pallas_call x1, Pallas kernels, server_pull(): pl.pallas_call(server_kernel, grid=(hidden // block,), out_shape=jax.Shap...  20.6 us
    unnamed x38, local copies, waits for them, and re-layouts  10.2 us
    dot_general x3, matrix products, attention_part(): jnp.einsum('grqk,kgd->qgrd', weights.astype(jnp.float32), value_heads.ast...  7.52 us
    dot_general x3, matrix products, attention_part(): lax.dot_general(context, output_matrix, (((1,), (1,)), ((), ())), preferr...  6.86 us
    dot_general x2, matrix products, attention_part(): jnp.dot(normed, query_matrix, preferred_element_type=jnp.float32)  6.19 us
  transfers between devices with their start and end apart: 1, of which 1 were waited for; matrix products, arithmetic and copies ran while one was open for 10% of the time, Pallas kernels for 0%

commit v1 on v0

--- a/solution.py
+++ b/solution.py
@@ -11,72 +11,140 @@
 HEAD_DIM = 64
 MESH = pl.DeviceIdType.MESH
 CORES = 2
+LANES = 128
 BF16 = jnp.bfloat16
 F32 = jnp.float32
 
 
-def rotary_tables(length):
-    halfway = HEAD_DIM // 2
-    positions = jnp.arange(length).astype(jnp.float32)
-    exponents = jnp.arange(halfway).astype(jnp.float32) * (2.0 / HEAD_DIM)
-    frequencies = jnp.exp(-math.log(500000.0) * exponents)
-    angles = positions[:, None] * frequencies[None, :]
-    cosine_table = jnp.concatenate([jnp.cos(angles), jnp.cos(angles)], 1)
-    sine_table = jnp.concatenate([jnp.sin(angles), jnp.sin(angles)], 1)
-    return (cosine_table, sine_table)
-
-
-def rotary(heads_in, cosine_table, sine_table):
-    halfway = heads_in.shape[-1] // 2
-    turned = jnp.concatenate([-heads_in[..., halfway:], heads_in[..., :halfway]], -1)
-    return heads_in * cosine_table[:, None, :] + turned * sine_table[:, None, :]
-
-
-def normalize(rows_in, gain):
-    rows_float = rows_in.astype(jnp.float32)
+def lane_tile(flag_ref=None):
+    return lax.broadcasted_iota(jnp.int32, (1, LANES), 1)
+
+
+def swap_halves(tile):
+    low = lax.rem(lane_tile(), HEAD_DIM) < HEAD_DIM // 2
+    ahead = pltpu.roll(tile, LANES - HEAD_DIM // 2, 1)
+    behind = pltpu.roll(tile, HEAD_DIM // 2, 1)
+    return jnp.where(low, ahead, behind)
+
+
+def paired(tile, at):
+    low = lane_tile() < HEAD_DIM
+    moved = pltpu.roll(tile, HEAD_DIM, 1)
+    first, second = (tile, moved) if at == 0 else (moved, tile)
+    zero = jnp.zeros_like(tile)
+    return jnp.where(low, first, zero).astype(BF16), jnp.where(low, zero, second).astype(BF16)
+
+
+CROSSED = (((1,), (1,)), ((), ()))
+TALL = (((0,), (0,)), ((), ()))
+
+
+def forward_kernel(
+    kv_count, sends_half,
+    rows_ref, gain_ref, cosine_ref, sine_ref, query_hbm, key_hbm, value_hbm, output_hbm,
+    normed_out, theirs_out, query_out, key_out, value_out, context_out, weights_out, attended_out,
+    query_mat, key_mat, value_mat, output_mat, scores, key_pair, value_turn, sems,
+):
+    length = rows_ref.shape[0]
+    copies = []
+    for i, (source, target) in enumerate(
+        ((query_hbm, query_mat), (key_hbm, key_mat), (value_hbm, value_mat), (output_hbm, output_mat))
+    ):
+        copies.append(pltpu.make_async_copy(source, target, sems.at[i]))
+        copies[-1].start()
+    rows_float = rows_ref[...].astype(F32)
     inv_rms = lax.rsqrt(jnp.mean(rows_float * rows_float, -1, keepdims=True) + 1e-05)
-    return (rows_float * inv_rms * gain.astype(jnp.float32)).astype(jnp.bfloat16)
-
-
-def attention_part(normed, query_matrix, client_key_matrix, value_matrix, output_matrix):
-    length = normed.shape[0]
-    query_count = query_matrix.shape[1] // HEAD_DIM
-    shared_count = client_key_matrix.shape[1] // HEAD_DIM
-    group_size = query_count // shared_count
-    cosine_table, sine_table = rotary_tables(length)
-    queries = jnp.dot(normed, query_matrix, preferred_element_type=jnp.float32).reshape(
-        length, query_count, HEAD_DIM
-    )
-    queries = (
-        rotary(queries, cosine_table, sine_table)
-        .astype(jnp.bfloat16)
-        .reshape(length, shared_count, group_size, HEAD_DIM)
-    )
-    key_heads = jnp.dot(normed, client_key_matrix, preferred_element_type=jnp.float32).reshape(
-        length, shared_count, HEAD_DIM
-    )
-    key_heads = rotary(key_heads, cosine_table, sine_table).astype(jnp.bfloat16)
-    value_heads = (
-        jnp.dot(normed, value_matrix, preferred_element_type=jnp.float32)
-        .astype(jnp.bfloat16)
-        .reshape(length, shared_count, HEAD_DIM)
-    )
-    scores = jnp.einsum(
-        "qgrd,kgd->grqk", queries.astype(jnp.float32), key_heads.astype(jnp.float32)
-    ) * HEAD_DIM ** (-0.5)
-    row_ids = lax.broadcasted_iota(jnp.int32, (length, length), 0)
-    col_ids = lax.broadcasted_iota(jnp.int32, (length, length), 1)
-    scores = jnp.where(col_ids <= row_ids, scores, -1e30)
-    highest = lax.stop_gradient(jnp.max(scores, -1, keepdims=True))
-    exponent = jnp.exp(scores - highest)
-    weights = (exponent / jnp.sum(exponent, -1, keepdims=True)).astype(jnp.bfloat16)
-    context = jnp.einsum(
-        "grqk,kgd->qgrd", weights.astype(jnp.float32), value_heads.astype(jnp.float32)
-    )
-    context = context.astype(jnp.bfloat16).reshape(length, query_count * HEAD_DIM)
-    return lax.dot_general(
-        context, output_matrix, (((1,), (1,)), ((), ())), preferred_element_type=jnp.float32
-    )
+    normed_out[...] = (rows_float * inv_rms * gain_ref[...].astype(F32)).astype(BF16)
+    if sends_half:
+        blocks, unused, wide = theirs_out.shape
+        other = 1 - lax.axis_index("sdata")
+        for d in range(blocks):
+            theirs_out[d] = normed_out[:, pl.ds(pl.multiple_of((2 * d + other) * wide, wide), wide)]
+    normed = normed_out[...]
+
+    def turn(tile):
+        return tile * cosine_ref[...] + swap_halves(tile) * sine_ref[...]
+
+    copies[0].wait()
+    wide = 2 * LANES
+    for at in range(0, query_mat.shape[1], wide):
+        part = jnp.dot(normed, query_mat[:, at : at + wide], preferred_element_type=F32)
+        for side in (0, LANES):
+            query_out[:, at + side : at + side + LANES] = turn(part[:, side : side + LANES]).astype(BF16)
+    copies[1].wait()
+    keys = turn(jnp.dot(normed, key_mat[...], preferred_element_type=F32)).astype(BF16)
+    key_out[...] = keys
+    copies[2].wait()
+    values = jnp.dot(normed, value_mat[...], preferred_element_type=F32).astype(BF16)
+    value_out[...] = values
+    keys_float, values_float = keys.astype(F32), values.astype(F32)
+    values_turned = values_float.T.astype(BF16)
+    value_turn[...] = jnp.zeros_like(value_turn)
+    for g in range(kv_count):
+        key_pair[g, :length], key_pair[g, length:] = paired(keys_float, g)
+        mine = values_turned[g * HEAD_DIM : (g + 1) * HEAD_DIM]
+        value_turn[g, :HEAD_DIM, :length] = mine
+        value_turn[g, HEAD_DIM:, length:] = mine
+    tiles = query_mat.shape[1] // LANES
+    step = LANES
+    for t in range(tiles):
+        g = t * kv_count // tiles
+        scores[...] = lax.dot_general(
+            key_pair[g], query_out[:, t * LANES : (t + 1) * LANES], CROSSED, preferred_element_type=F32
+        )
+        for head in range(2):
+            base = head * length
+            for i in range(0, length, step):
+                deep = i + step
+                block = scores[base : base + deep, i : i + step] * HEAD_DIM ** (-0.5)
+                key_ids = lax.broadcasted_iota(jnp.int32, (deep, step), 0)
+                query_ids = lax.broadcasted_iota(jnp.int32, (deep, step), 1) + i
+                block = jnp.where(key_ids <= query_ids, block, -1e30)
+                exponent = jnp.exp(block - jnp.max(block, 0, keepdims=True))
+                share = 1.0 / jnp.sum(exponent, 0, keepdims=True)
+                weights_out[t, base : base + deep, i : i + step] = (exponent * share).astype(BF16)
+                if deep < length:
+                    weights_out[t, base + deep : base + length, i : i + step] = jnp.zeros(
+                        (length - deep, step), BF16
+                    )
+        turned_context = jnp.dot(value_turn[g], weights_out[t], preferred_element_type=F32)
+        context_out[:, t * LANES : (t + 1) * LANES] = turned_context.T.astype(BF16)
+    copies[3].wait()
+    context = context_out[...]
+    wide = next(b for b in (512, 256, 128) if attended_out.shape[1] % b == 0)
+    for at in range(0, attended_out.shape[1], wide):
+        attended_out[:, at : at + wide] = lax.dot_general(
+            context, output_mat[at : at + wide, :], CROSSED, preferred_element_type=F32
+        ).astype(BF16)
+
+
+def forward(rows_in, gain, tables, matrices, kv_count, blocks):
+    length, breadth = rows_in.shape
+    features, shared = matrices[0].shape[1], matrices[1].shape[1]
+    tiles = features // LANES
+    rows = breadth // (2 * blocks)
+    sends_half = rows % LANES == 0
+    shape = lambda *sizes: jax.ShapeDtypeStruct(sizes, BF16)
+    theirs = shape(blocks, length, rows) if sends_half else shape(16, LANES)
+    return pl.pallas_call(
+        partial(forward_kernel, kv_count, sends_half),
+        out_shape=(
+            shape(length, breadth), theirs, shape(length, features), shape(length, shared),
+            shape(length, shared), shape(length, features), shape(tiles, 2 * length, length),
+            shape(length, breadth),
+        ),
+        in_specs=[VMEM_SPEC] * 4 + [ANY_SPEC] * 4,
+        out_specs=(VMEM_SPEC,) * 8,
+        scratch_shapes=[pltpu.VMEM(m.shape, BF16) for m in matrices]
+        + [
+            pltpu.VMEM((2 * length, length), F32),
+            pltpu.VMEM((kv_count, 2 * length, LANES), BF16),
+            pltpu.VMEM((kv_count, LANES, 2 * length), BF16),
+            pltpu.SemaphoreType.DMA((4,)),
+        ],
+        compiler_params=pltpu.CompilerParams(vmem_limit_bytes=48 * 2**20),
+        name="forward",
+    )(rows_in, gain, *tables, *matrices)
 
 
 def server_kernel(
@@ -434,63 +502,319 @@
         copy.wait_send()
 
 
-def average_kernel(client_count, group_count, count, *refs):
-    early, grads, outs = refs[0], refs[1 : count + 1], refs[count + 1 : 2 * count + 1]
-    refs = refs[1:]
-    y_at, z_from, z_at = (refs[(2 + i) * count : (3 + i) * count] for i in range(3))
-    y_sems, z_sems = refs[5 * count :]
+class Chain:
+    def __init__(self, own, forth, back, sems, count):
+        self.own, self.forth, self.back, self.count = own, forth, back, count
+        self.sems = sems
+        self.at = lax.axis_index("client")
+
+    def copy(self, way, j, d):
+        landing = self.forth if way == 0 else self.back
+        to = self.at + 1 if way == 0 else self.at - 1
+        return pltpu.make_async_remote_copy(
+            src_ref=self.own.at[d],
+            dst_ref=landing.at[j],
+            send_sem=self.sems.at[2 * way, j],
+            recv_sem=self.sems.at[2 * way + 1, j],
+            device_id={"client": lax.rem(to + self.count, self.count)},
+            device_id_type=MESH,
+        )
+
+    def legs(self):
+        for j in range(self.count - 1):
+            for way in (0, 1):
+                d = self.count - 1 - j if way == 0 else j
+                end = 0 if way == 0 else self.count - 1
+                beyond = self.at < d if way == 0 else self.at > d
+                yield way, j, d, end, beyond
+
+    def open(self, d, way):
+        j = self.count - 1 - d if way == 0 else d
+        if j < self.count - 1:
+            end = 0 if way == 0 else self.count - 1
+
+            @pl.when(self.at == end)
+            def _():
+                self.copy(way, j, d).start()
+
+    def relay(self):
+        for way, j, d, end, beyond in self.legs():
+            landing = self.forth if way == 0 else self.back
+
+            @pl.when(beyond & (self.at != end))
+            def _(way=way, j=j, d=d, landing=landing):
+                self.copy(way, j, d).wait_recv()
+                self.own[d] = (self.own[d].astype(F32) + landing[j].astype(F32)).astype(BF16)
+                self.copy(way, j, d).start()
+
+    def total(self, out_refs):
+        last = self.count - 1
+        for way, end, j in ((0, 0, last - self.at), (1, last, self.at)):
+            landing = self.forth if way == 0 else self.back
+
+            @pl.when(self.at != end)
+            def _(way=way, j=j, landing=landing):
+                self.copy(way, j, 0).wait_recv()
+                self.own[self.at] = (
+                    self.own[self.at].astype(F32) + landing[j].astype(F32)
+                ).astype(BF16)
+
+        result = (self.own[self.at].astype(F32) * (1.0 / self.count)).astype(BF16)
+        at = 0
+        for out in out_refs:
+            out[...] = result[:, at : at + out.shape[1]]
+            at += out.shape[1]
+
+    def finish(self):
+        for way, j, d, end, beyond in self.legs():
+
+            @pl.when(beyond)
+            def _(way=way, j=j, d=d):
+                self.copy(way, j, d).wait_send()
+
+
+def learn_kernel(
+    kv_count, count, aligned,
+    cut_ref, output_ref, query_ref, key_ref, value_ref, context_ref, weights_ref, normed_ref,
+    far_normed, far_context, cosine_ref, sine_ref, *refs,
+):
+    if not aligned:
+        near_cut, give_cut, near_normed, refs = refs[0], refs[1], refs[2], refs[3:]
+    query_out, key_out, value_out, output_out = refs[:4]
+    (
+        pulled, pair, key_turn, value_pair, weight_grad, score_grad, query_grad, shared_grad,
+        far_cut, far_query, far_shared,
+        output_own, output_forth, output_back, shared_own, shared_forth, shared_back,
+        query_own, query_forth, query_back,
+        cut_sems, core_sems, give_sems, output_sems, shared_sems, query_sems,
+    ) = refs[4:]
+    length = cut_ref.shape[0]
+    rows = far_cut.shape[2]
     client, group = lax.axis_index("client"), lax.axis_index("sdata")
-    others = [{"client": turned(client, k, client_count)} for k in range(1, client_count)]
-    others += [{"sdata": turned(group, k, group_count)} for k in range(1, group_count)]
-    greet(others)
-    middle = client_count // 2
-    steps = [(middle + k) % client_count for k in range(client_count)]
-    steps = [k for k in steps if k != 0] + [0]
-    y_copies = {}
-    for k in steps:
-        to = turned(client, k, client_count)
-        for a in range(1, count):
-            for d in range(1, group_count):
-                y_copies[k, a, d] = send(
-                    grads[a].at[to, turned(group, d, group_count)], y_at[a].at[d, to],
-                    y_sems.at[0, a, d, k], y_sems.at[1, a, d, k],
-                    {"sdata": turned(group, d, group_count)},
-                )
-    z_copies = []
-    rows = outs[0].shape[0]
-    block = next(b for b in (64, 32, 16, rows) if rows % b == 0)
-    for k, a in [(k, 0) for k in steps] + [(k, a) for k in steps for a in range(1, count)]:
-            to = turned(client, k, client_count)
-            for d in range(1, group_count if a else 1):
-                y_copies[k, a, d].wait_recv()
-            for r in range(0, rows, block):
-                at = pl.ds(r, block)
-                total = grads[a][to, group, at, :].astype(F32)
-                for d in range(1, group_count):
-                    other = y_at[a][d, to, at, :] if a else early[d - 1, to, at, :]
-                    total = total + other.astype(F32)
-                z_from[a][k, at, :] = total.astype(BF16)
-            if k != 0:
-                z_copies.append(
-                    send(
-                        z_from[a].at[k], z_at[a].at[k],
-                        z_sems.at[0, a, k], z_sems.at[1, a, k], {"client": to},
-                    )
-                )
-    for copy in z_copies:
-        copy.wait_recv()
-    for a in range(count):
-        for r in range(0, rows, block):
-            at = pl.ds(r, block)
-            total = z_from[a][0, at, :].astype(F32)
-            for k in range(1, client_count):
-                total = total + z_at[a][k, at, :].astype(F32)
-            outs[a][at, :] = (total * (1.0 / client_count)).astype(BF16)
-    for copy in list(y_copies.values()) + z_copies:
-        copy.wait_send()
+    tensor_at = lax.axis_index("tensor")
+    core = lax.rem(tensor_at, CORES)
+    sibling = {"tensor": tensor_at + 1 - 2 * core}
+    across = {"sdata": 1 - group}
+    ahead = {"client": lax.rem(client + 1, count)}
+    behind = {"client": lax.rem(client + count - 1, count)}
+    greet([sibling, across, ahead, behind])
+    order = []
+    for j in range((count + 1) // 2):
+        order += [count - 1 - j, j]
+
+    def columns(d, side):
+        return pl.ds(pl.multiple_of((2 * d + side) * rows, rows), rows)
+
+    def cut_copy(n, d):
+        source = cut_ref.at[:, columns(d, 1 - group)] if aligned else give_cut.at[d]
+        return pltpu.make_async_remote_copy(
+            src_ref=source, dst_ref=far_cut.at[d],
+            send_sem=cut_sems.at[0, n], recv_sem=cut_sems.at[1, n],
+            device_id=across, device_id_type=MESH,
+        )
+
+    def core_copy(n, d):
+        return pltpu.make_async_remote_copy(
+            src_ref=far_cut.at[d], dst_ref=far_cut.at[d],
+            send_sem=core_sems.at[0, n], recv_sem=core_sems.at[1, n],
+            device_id=sibling, device_id_type=MESH,
+        )
+
+    halves = count // CORES
+    picks = [order[CORES * n] + core * (order[CORES * n + 1] - order[CORES * n]) for n in range(halves)]
+    others = [
+        order[CORES * n + 1] + core * (order[CORES * n] - order[CORES * n + 1]) for n in range(halves)
+    ]
+    for n in range(halves):
+        cut_copy(n, picks[n]).start()
+
+    width = 2 * LANES if query_ref.shape[1] % (2 * LANES) == 0 else LANES
+    for at in range(0, query_ref.shape[1], width):
+        pulled[:, at : at + width] = jnp.dot(
+            cut_ref[...], output_ref[:, at : at + width], preferred_element_type=F32
+        ).astype(BF16)
+    keys_float, values_float = key_ref[...].astype(F32), value_ref[...].astype(F32)
+    keys_turned = keys_float.T.astype(BF16)
+    key_turn[...] = jnp.zeros_like(key_turn)
+    score_grad[...] = jnp.zeros_like(score_grad)
+    for g in range(kv_count):
+        value_pair[g, :length], value_pair[g, length:] = paired(values_float, g)
+        mine = keys_turned[g * HEAD_DIM : (g + 1) * HEAD_DIM]
+        key_turn[g, :HEAD_DIM, :length] = mine
+        key_turn[g, HEAD_DIM:, length:] = mine
+
+    def unturn(tile):
+        return tile * cosine_ref[...] - swap_halves(tile) * sine_ref[...]
+
+    tiles = query_ref.shape[1] // LANES
+    low = lane_tile() < HEAD_DIM
+    key_sum, value_sum = [None] * kv_count, [None] * kv_count
+    for t in range(tiles):
+        g = t * kv_count // tiles
+        span = slice(t * LANES, (t + 1) * LANES)
+        weight_grad[...] = lax.dot_general(
+            value_pair[g], pulled[:, span], CROSSED, preferred_element_type=F32
+        )
+        for head in range(2):
+            base = head * length
+            for i in range(0, length, LANES):
+                deep = i + LANES
+                grad = weight_grad[base : base + deep, i : i + LANES].astype(BF16).astype(F32)
+                weight = weights_ref[t, base : base + deep, i : i + LANES].astype(F32)
+                both = grad * weight
+                drift = jnp.sum(both, 0, keepdims=True)
+                score_grad[base : base + deep, i : i + LANES] = (
+                    (both - weight * drift) * HEAD_DIM ** (-0.5)
+                ).astype(BF16)
+        back_query = jnp.dot(key_turn[g], score_grad[...], preferred_element_type=F32)
+        query_grad[:, span] = unturn(back_query.T.astype(BF16).astype(F32)).astype(BF16)
+        back_key = jnp.dot(score_grad[...], query_ref[:, span], preferred_element_type=F32)
+        back_value = jnp.dot(weights_ref[t], pulled[:, span], preferred_element_type=F32)
+        first = key_sum[g] is None
+        key_sum[g] = back_key if first else key_sum[g] + back_key
+        value_sum[g] = back_value if first else value_sum[g] + back_value
+
+    def folded(sums):
+        whole = None
+        for g, both in enumerate(sums):
+            upper, lower = both[:length], both[length:]
+            if g == 0:
+                whole = upper + pltpu.roll(lower, HEAD_DIM, 1)
+            else:
+                whole = jnp.where(low, whole, pltpu.roll(upper, HEAD_DIM, 1) + lower)
+        return whole.astype(BF16)
+
+    shared_grad[:, :LANES] = unturn(folded(key_sum).astype(F32)).astype(BF16)
+    shared_grad[:, LANES:] = folded(value_sum)
+
+    def give(source, target, i):
+        return pltpu.make_async_remote_copy(
+            src_ref=source, dst_ref=target, send_sem=give_sems.at[0, i], recv_sem=give_sems.at[1, i],
+            device_id=across, device_id_type=MESH,
+        )
+
+    gifts = [give(shared_grad, far_shared, 0), give(query_grad, far_query, 1)]
+    for gift in gifts:
+        gift.start()
+    chains = [
+        Chain(output_own, output_forth, output_back, output_sems, count),
+        Chain(shared_own, shared_forth, shared_back, shared_sems, count),
+        Chain(query_own, query_forth, query_back, query_sems, count),
+    ]
+
+    def near(d, from_cut):
+        if aligned:
+            return (cut_ref if from_cut else normed_ref)[:, columns(d, group)]
+        return near_cut[d] if from_cut else near_normed[d]
+
+    def product(chain, d, left, right, far_left, far_right):
+        chain.own[d] = (
+            lax.dot_general(left, right, TALL, preferred_element_type=F32)
+            + lax.dot_general(far_left, far_right, TALL, preferred_element_type=F32)
+        ).astype(BF16)
+
+    for n in range(halves):
+        cut_copy(n, picks[n]).wait_recv()
+        core_copy(n, picks[n]).start()
+        core_copy(n, others[n]).wait_recv()
+        for i in range(CORES):
+            d = order[CORES * n + i]
+            product(chains[0], d, near(d, True), context_ref[...], far_cut[d], far_context[...])
+            for way in (0, 1):
+                chains[0].open(d, way)
+
+    def spread(chain, grad, far_grad):
+        for d in order:
+            product(chain, d, near(d, False), grad[...], far_normed[d], far_grad[...])
+            for way in (0, 1):
+                chain.open(d, way)
+
+    gifts[0].wait_recv()
+    spread(chains[1], shared_grad, far_shared)
+    chains[0].relay()
+    gifts[1].wait_recv()
+    spread(chains[2], query_grad, far_query)
+    chains[1].relay()
+    chains[2].relay()
+    chains[0].total([output_out])
+    chains[1].total([key_out, value_out])
+    chains[2].total([query_out])
+    for n in range(halves):
+        cut_copy(n, picks[n]).wait_send()
+        core_copy(n, picks[n]).wait_send()
+    for gift in gifts:
+        gift.wait_send()
+    for chain in chains:
+        chain.finish()
+
+
+def learn(cut_grad, output_matrix, saved, normed, far_normed, far_context, tables, kv_count):
+    unused, count, group_count = axis_counts()
+    queries, keys, values, context, weights = saved
+    length, breadth = cut_grad.shape
+    features = queries.shape[1]
+    rows = breadth // (count * group_count)
+    aligned = rows % LANES == 0
+    dma = pltpu.SemaphoreType.DMA
+    shape = lambda *sizes: jax.ShapeDtypeStruct(sizes, BF16)
+    vmem = lambda *sizes: pltpu.VMEM(sizes, BF16)
+    operands = [cut_grad, output_matrix, queries, keys, values, context, weights, normed]
+    operands += [far_normed, far_context, *tables]
+    if not aligned:
+        group = lax.axis_index("sdata")
+        operands += [
+            half_of(cut_grad, count, group), half_of(cut_grad, count, 1 - group),
+            half_of(normed, count, group),
+        ]
+    chain = lambda wide: [
+        vmem(count, rows, wide), vmem(count - 1, rows, wide), vmem(count - 1, rows, wide)
+    ]
+    return pl.pallas_call(
+        partial(learn_kernel, kv_count, count, aligned),
+        out_shape=(
+            shape(rows, features), shape(rows, LANES), shape(rows, LANES), shape(rows, features)
+        ),
+        in_specs=[VMEM_SPEC] * len(operands),
+        out_specs=(VMEM_SPEC,) * 4,
+        scratch_shapes=[
+            vmem(length, features), vmem(16, LANES), vmem(kv_count, LANES, 2 * length),
+            vmem(kv_count, 2 * length, LANES), pltpu.VMEM((2 * length, length), F32),
+            vmem(2 * length, length), vmem(length, features), vmem(length, 2 * LANES),
+            vmem(count, length, rows), vmem(length, features), vmem(length, 2 * LANES),
+        ]
+        + chain(features) + chain(2 * LANES) + chain(features)
+        + [dma((2, count // CORES)), dma((2, count // CORES)), dma((2, 2))]
+        + [dma((4, count - 1))] * 3,
+        compiler_params=params(3),
+        name="learn",
+    )(*operands)
+
+
+def half_of(array, count, side):
+    blocks = array.reshape(array.shape[0], count, 2, -1)
+    return lax.dynamic_index_in_dim(blocks, side, 2, False).transpose(1, 0, 2)
+
+
+def across_groups(array):
+    count = lax.axis_size("sdata")
+    return lax.ppermute(array, "sdata", [(g, (g + 1) % count) for g in range(count)])
+
+
+def tables_of(length):
+    halfway = HEAD_DIM // 2
+    lanes = jnp.arange(LANES) % HEAD_DIM
+    frequencies = jnp.exp(-math.log(500000.0) * (2.0 / HEAD_DIM) * (lanes % halfway).astype(F32))
+    angles = jnp.arange(length).astype(F32)[:, None] * frequencies[None, :]
+    sign = jnp.where(lanes < halfway, -1.0, 1.0)
+    return jnp.cos(angles), jnp.sin(angles) * sign[None, :]
+
+
+def widened(matrix):
+    return jnp.pad(matrix, ((0, 0), (0, LANES - matrix.shape[1])))
 
 
 VMEM_SPEC = pl.BlockSpec(memory_space=pltpu.VMEM)
+ANY_SPEC = pl.BlockSpec(memory_space=pl.ANY)
 SMEM_SPEC = pl.BlockSpec(memory_space=pltpu.SMEM)
 
 
@@ -562,41 +886,6 @@
     return grad.reshape(length, breadth)
 
 
-def send_early(grad):
-    unused, client_count, group_count = axis_counts()
-    group = lax.axis_index("sdata")
-    blocks = grad.reshape(client_count, group_count, -1, grad.shape[1])
-    arrived = []
-    for d in range(1, group_count):
-        block = lax.dynamic_index_in_dim(blocks, turned(group, d, group_count), 1, False)
-        ring = [(g, (g + d) % group_count) for g in range(group_count)]
-        arrived.append(lax.ppermute(block, "sdata", ring))
-    return jnp.stack(arrived)
-
-
-def average(early, grads):
-    unused, client_count, group_count = axis_counts()
-    count = len(grads)
-    rows = grads[0].shape[0] // (client_count * group_count)
-    widths = [grad.shape[1] for grad in grads]
-    dma = pltpu.SemaphoreType.DMA
-    return pl.pallas_call(
-        partial(average_kernel, client_count, group_count, count),
-        out_shape=tuple(jax.ShapeDtypeStruct((rows, width), BF16) for width in widths),
-        in_specs=[VMEM_SPEC] * (count + 1),
-        out_specs=(VMEM_SPEC,) * count,
-        scratch_shapes=[
-            pltpu.VMEM((group_count, client_count, rows, w) if n else (16, 128), BF16)
-            for n, w in enumerate(widths)
-        ]
-        + [pltpu.VMEM((client_count, rows, w), BF16) for w in widths]
-        + [pltpu.VMEM((client_count, rows, w), BF16) for w in widths]
-        + [dma((2, count, group_count, client_count)), dma((2, count, client_count))],
-        compiler_params=params(3),
-        name="average",
-    )(early, *[grad.reshape(client_count, group_count, rows, grad.shape[1]) for grad in grads])
-
-
 def local(
     client_input,
     client_gain,
@@ -612,32 +901,35 @@
     assignment,
 ):
     client_count = lax.axis_size("client")
-    normed = normalize(client_input, client_gain[0])
-    attended, pullback = jax.vjp(
-        partial(attention_part, normed),
-        query_weight[0],
-        key_weight[0],
-        client_value_weight[0],
-        output_weight[0],
+    shared = key_weight.shape[2]
+    kv_count = shared // HEAD_DIM
+    tables = tables_of(client_input.shape[0])
+    matrices = [
+        query_weight[0], widened(key_weight[0]), widened(client_value_weight[0]), output_weight[0]
+    ]
+    normed, theirs, *saved, attended = forward(
+        client_input, client_gain, tables, matrices, kv_count, client_count
     )
+    if theirs.ndim == 2:
+        theirs = half_of(normed, client_count, 1 - lax.axis_index("sdata"))
+    far_normed = across_groups(theirs)
     ids = jnp.arange(client_count).astype(jnp.int32)
     ahead = (assignment[None, :] < assignment[:, None]) | (
         (assignment[None, :] == assignment[:, None]) & (ids[None, :] < ids[:, None])
     )
     inverse = jnp.sum(ahead.astype(jnp.int32), 1)
     group_order = jnp.sum(jnp.where(inverse[None, :] == ids[:, None], ids[None, :], 0), 1)
-    cut_rows, up_rows, up_own = relay_out(
-        group_order, attended.astype(BF16), client_input, upstream
-    )
+    cut_rows, up_rows, up_own = relay_out(group_order, attended, client_input, upstream)
+    context, cut_rows = lax.optimization_barrier((saved[3], cut_rows))
+    far_context = across_groups(context)
     pulled = server_pull(
         cut_rows, up_rows, server_gain[0], server_gate[0], server_up[0], server_down[0]
     )
     arriving_grad = relay_back(inverse, pulled, up_own)
-    query_grad, key_grad, value_grad, output_grad = pullback(arriving_grad.astype(jnp.float32))
-    output_update, query_update, key_update, value_update = average(
-        send_early(output_grad), [output_grad, query_grad, key_grad, value_grad]
+    query_update, key_update, value_update, output_update = learn(
+        arriving_grad, output_weight[0], saved, normed, far_normed, far_context, tables, kv_count
     )
-    return (query_update, key_update, value_update, output_update)
+    return (query_update, key_update[:, :shared], value_update[:, :shared], output_update)
 
 
 def solution(mesh):

time: 212 us -> 195 us (0.920)
  the two profiles are of different devices: /device:TPU:8 before, /device:TPU:0 now
where the time goes in v1:
time: 195 us; the launch traced here: 194 us
  Pallas kernels  181 us (93%)
  local copies, waits for them, and re-layouts  8.03 us (4%)
  starting transfers between devices  3.89 us (2%)
    pallas_call x1, Pallas kernels, learn(): pl.pallas_call(partial(learn_kernel, kv_count, count, aligned), out_shape...  76.9 us
    pallas_call x1, Pallas kernels, relay_out(): pl.pallas_call(partial(out_kernel, chips, client_count, group_count), out...  37.6 us
    pallas_call x1, Pallas kernels, relay_back(): pl.pallas_call(partial(back_kernel, chips, client_count, group_count), ou...  34.3 us
    pallas_call x1, Pallas kernels, server_pull(): pl.pallas_call(server_kernel, grid=(hidden // block,), out_shape=jax.Shap...  20.6 us
    pallas_call x1, Pallas kernels, forward(): pl.pallas_call(partial(forward_kernel, kv_count, sends_half), out_shape=(...  11.3 us
    unnamed x18, local copies, waits for them, and re-layouts  8.03 us
  transfers between devices with their start and end apart: 2, of which 0 were waited for; matrix products, arithmetic and copies ran while one was open for 0% of the time, Pallas kernels for 48%

profile of v1, /device:TPU:0, one launch (start us, length us, event | category | flops | bytes accessed | tf_op | source)
XLA Modules:
  0.0 194.4 jit_solution(2525146397963789909)
XLA Ops:
  0.7 0.8 fusion
  1.4 0.0 copy-start.2
  1.4 1.0 copy-done.2
  2.5 0.0 copy-start.3
  2.5 1.0 copy-done.3
  3.5 0.0 copy-start.5
  3.5 0.7 copy-done.5
  4.2 0.0 copy-start.6
  4.2 11.3 %forward.1 = (bf16[384,2048]{1,0:T(8,128)(2,1)S(1)}, bf16[4,384,256]{2,1,0:T(8,128)(2,1)S(1)}, bf16[384,512]{1,0:T(8,128)(2,1)S(1)}, bf16[384,128]{1,0:T(8,128)(...) custom-call(bf16[384,2048]{1,0:T(8,128)(2,1)} %rows_ref.1, ...), custom_call_target="tpu_custom_call" | custom-call | tf_op jit(solution)/shard_map/forward/pallas_call | solution.py:129
  15.5 0.0 copy-start
  15.5 1.2 copy-done
  16.7 3.0 %collective-permute-start = (bf16[4,384,256]{2,1,0:T(8,128)(2,1)S(1)}, bf16[4,384,256]{2,1,0:T(8,128)(2,1)S(1)}, u32[]{:S(2)}, u32[]{:S(2)}) collective-permute-start(bf16[4,384,256]{2,1,0:T(8,128)(2,1)S(1)} %get-tuple-element.28), channel_id=1, source_target_pairs={{0,1},{1,0},{2,3},{3,2},{4,5},{5,4},{6,7},{7,6},{8,9},{9,8},{10,11... | collective-permute-start | bytes 2359304 | tf_op jit(solution)/shard_map/ppermute | solution.py:800
  19.7 0.0 copy-done.6
  19.7 0.2 convert_reduce_fusion.inverse
  19.9 0.1 select_reduce_fusion.order
  20.0 0.0 copy-start.1
  20.0 1.4 copy-done.1
  21.4 0.0 copy-start.4
  21.4 37.6 %relay_out.1 = (bf16[4,96,2048]{2,1,0:T(8,128)(2,1)S(1)}, bf16[4,96,2048]{2,1,0:T(8,128)(2,1)S(1)}, bf16[4,96,512]{2,1,0:T(8,128)(2,1)S(1)}) custom-call(s32[4]{0:T(128)S(1)} %select_reduce_fusion.order, bf16[4,96,2048]{2,1,0:T(8,128)(2,1)S(1)} %bitcast.16, bf16[4,96,2048]{2,1,0:T(8,128)(2,1)} %bitcast.23, bf16[4,96,2048]{2,1,0:T(8,128)(2,1)} %bitcast.28), custom_call_target="tpu_custom_call" | custom-call | tf_op jit(solution)/shard_map/relay_out/pallas_call | solution.py:840
  59.1 0.9 collective-permute-start.1
  60.0 0.0 copy-done.4
  60.0 20.6 %server_pull.1 = bf16[384,2048]{1,0:T(8,128)(2,1)S(1)} custom-call(bf16[384,2048]{1,0:T(8,128)(2,1)S(1)} %bitcast.17, bf16[384,2048]{1,0:T(8,128)(2,1)S(1)} %bitcast.18, bf16[1,2048]{1,0:T(2,128)(2,1)S(1)} %copy-done.4, bf16[2048,1024]{1,0:T(8,128)(2,1)} %bitcast.24, bf16[2048,1024]{1,0:T(8,128)(2,1)} %bitcast.25, bf16[1024,2048]{1,0:T(8,128)(2,1)} %bitcast.26), custom_call_target="tpu_custom_call" | custom-call | tf_op jit(solution)/shard_map/server_pull/pallas_call | solution.py:206
  80.6 34.3 %relay_back.1 = bf16[4,96,2048]{2,1,0:T(8,128)(2,1)S(1)} custom-call(s32[4]{0:T(128)S(1)} %convert_reduce_fusion.inverse, bf16[4,96,2048]{2,1,0:T(8,128)(2,1)S(1)} %bitcast.15, bf16[4,96,512]{2,1,0:T(8,128)(2,1)S(1)} %get-tuple-element.22.up_own), custom_call_target="tpu_custom_call" | custom-call | tf_op jit(solution)/shard_map/relay_back/pallas_call | solution.py:872
  114.9 0.0 collective-permute-done.1.far_context
  114.9 0.0 collective-permute-done.far_normed
  114.9 76.9 %learn.1 = (bf16[256,512]{1,0:T(8,128)(2,1)S(1)}, bf16[256,128]{1,0:T(8,128)(2,1)S(1)}, bf16[256,128]{1,0:T(8,128)(2,1)S(1)}, bf16[256,512]{1,0:T(8,128)(2,1)S(1)}) custom-call(bf16[384,2048]{1,0:T(8,128)(2,1)S(1)} %bitcast.14, bf16[2048,512]{1,0:T(8,128)(2,1)} %bitcast.22, bf16[384,512]{1,0:T(8,128)(2,1)S(1)} %get-tuple-element.23.query_ref, ...), custom_call_target="tpu_custom_call" | custom-call | tf_op jit(solution)/shard_map/learn/pallas_call | solution.py:772
  191.8 0.7 copy.20
  192.5 0.6 copy.21
  193.1 0.6 copy.22
  193.7 0.7 copy.23
  (2 shorter events, 0.0 us)
Async XLA Ops:
  1.4 1.0 copy-start.2
  2.5 1.0 copy-start.3
  3.5 0.7 copy-start.5
  4.2 15.5 %copy-start.6 = (s32[4]{0:T(128)S(1)}, s32[4]{0:T(128)}, u32[]{:S(2)}) copy-start(s32[4]{0:T(128)} %param.23) | copy-start | bytes 52
  15.5 1.2 copy-start
  16.7 98.2 %collective-permute-start = (bf16[4,384,256]{2,1,0:T(8,128)(2,1)S(1)}, bf16[4,384,256]{2,1,0:T(8,128)(2,1)S(1)}, u32[]{:S(2)}, u32[]{:S(2)}) collective-permute-start(bf16[4,384,256]{2,1,0:T(8,128)(2,1)S(1)} %get-tuple-element.28), channel_id=1, source_target_pairs={{0,1},{1,0},{2,3},{3,2},{4,5},{5,4},{6,7},{7,6},{8,9},{9,8},{10,11... | collective-permute-start | bytes 2359304 | tf_op jit(solution)/shard_map/ppermute | solution.py:800
  20.0 1.4 copy-start.1
  21.4 38.6 %copy-start.4 = (bf16[1,2048]{1,0:T(2,128)(2,1)S(1)}, bf16[1,2048]{1,0:T(2,128)(2,1)}, u32[]{:S(2)}) copy-start(bf16[1,2048]{1,0:T(2,128)(2,1)} %gain_ref.3) | copy-start | bytes 12292
  59.1 55.8 %collective-permute-start.1 = (bf16[384,512]{1,0:T(8,128)(2,1)S(1)}, bf16[384,512]{1,0:T(8,128)(2,1)S(1)}, u32[]{:S(2)}, u32[]{:S(2)}) collective-permute-start(bf16[384,512]{1,0:T(8,128)(2,1)S(1)} %get-tuple-element.29.context_ref), channel_id=1, source_target_pairs={{0,1},{1,0},{2,3},{3,2},{4,5},{5,4},{6,7},{7,6},{8,9},{9,8},{10,11... | collective-permute-start | bytes 1179656 | tf_op jit(solution)/shard_map/ppermute | solution.py:800

commit v2 on v1

v2 whole, which is shorter than its diff:
```python
from functools import partial
import math

import jax
import jax.numpy as jnp
from jax import lax
from jax.experimental import pallas as pl
from jax.experimental.pallas import tpu as pltpu
from jax.sharding import PartitionSpec as P

HEAD_DIM = 64
MESH = pl.DeviceIdType.MESH
CORES = 2
LANES = 128
BF16 = jnp.bfloat16
F32 = jnp.float32


def lane_tile(flag_ref=None):
    return lax.broadcasted_iota(jnp.int32, (1, LANES), 1)


def swap_halves(tile):
    low = lax.rem(lane_tile(), HEAD_DIM) < HEAD_DIM // 2
    ahead = pltpu.roll(tile, LANES - HEAD_DIM // 2, 1)
    behind = pltpu.roll(tile, HEAD_DIM // 2, 1)
    return jnp.where(low, ahead, behind)


def paired(tile, at):
    low = lane_tile() < HEAD_DIM
    moved = pltpu.roll(tile, HEAD_DIM, 1)
    first, second = (tile, moved) if at == 0 else (moved, tile)
    zero = jnp.zeros_like(tile)
    return jnp.where(low, first, zero).astype(BF16), jnp.where(low, zero, second).astype(BF16)


CROSSED = (((1,), (1,)), ((), ()))
TALL = (((0,), (0,)), ((), ()))


VMEM_SPEC = pl.BlockSpec(memory_space=pltpu.VMEM)
ANY_SPEC = pl.BlockSpec(memory_space=pl.ANY)
SMEM_SPEC = pl.BlockSpec(memory_space=pltpu.SMEM)


def params(number):
    return pltpu.CompilerParams(
        collective_id=number, has_side_effects=True, vmem_limit_bytes=48 * 2**20
    )


def axis_counts():
    return lax.axis_size("tensor") // CORES, lax.axis_size("client"), lax.axis_size("sdata")


def greet(others):
    barrier = pltpu.get_barrier_semaphore()
    for other in others:
        pl.semaphore_signal(barrier, inc=1, device_id=other, device_id_type=MESH)
    pl.semaphore_wait(barrier, len(others))


def send(source, target, send_sem, recv_sem, device):
    copy = pltpu.make_async_remote_copy(
        src_ref=source,
        dst_ref=target,
        send_sem=send_sem,
        recv_sem=recv_sem,
        device_id=device,
        device_id_type=MESH,
    )
    copy.start()
    return copy


def place():
    tensor_at = lax.axis_index("tensor")
    return tensor_at // CORES, lax.rem(tensor_at, CORES)


def turned(index, step, count):
    return lax.rem(index + step, count)


def columns_of(chip, core, width):
    return pl.ds(pl.multiple_of((chip * CORES + core) * width, width), width)


def partners(chips, client_count, group_count):
    chip, core = place()
    client, group = lax.axis_index("client"), lax.axis_index("sdata")
    others = [{"tensor": chip * CORES + 1 - core}]
    others += [{"tensor": turned(chip, k, chips) * CORES + core} for k in range(1, chips)]
    others += [{"client": turned(client, k, client_count)} for k in range(1, client_count)]
    others += [{"sdata": turned(group, k, group_count)} for k in range(1, group_count)]
    return others


class ShareSum:
    def __init__(self, part, pair, relay, landed, sems, pieces, chips):
        self.part, self.pair, self.relay, self.landed = part, pair, relay, landed
        self.pair_send, self.pair_recv, self.chip_send, self.chip_recv = sems
        self.chips, self.width = chips, part.shape[-1] // (CORES * chips)
        self.chip, self.core = place()
        self.pair_copies = {}
        self.chip_copies = {}
        for n, (q, rows) in enumerate(pieces):
            for k in list(range(1, chips)) + [0]:
                to = turned(self.chip, k, chips)
                self.pair_copies[k, n] = send(
                    part.at[q, rows, columns_of(to, 1 - self.core, self.width)],
                    pair.at[k, q, rows],
                    self.pair_send.at[k, n],
                    self.pair_recv.at[k, n],
                    {"tensor": self.chip * CORES + 1 - self.core},
                )
        for n, (q, rows) in enumerate(pieces):
            for k in range(1, chips):
                to = turned(self.chip, k, chips)
                self.pair_copies[k, n].wait_recv()
                relay[k, q, rows] = (
                    part[q, rows, columns_of(to, self.core, self.width)].astype(F32)
                    + pair[k, q, rows].astype(F32)
                ).astype(BF16)
                self.chip_copies[k, n] = send(
                    relay.at[k, q, rows],
                    landed.at[k, q, rows],
                    self.chip_send.at[k, n],
                    self.chip_recv.at[k, n],
                    {"tensor": to * CORES + self.core},
                )

    def get(self, n, piece):
        q, rows = piece
        self.pair_copies[0, n].wait_recv()
        total = self.part[q, rows, columns_of(self.chip, self.core, self.width)].astype(
            F32
        ) + self.pair[0, q, rows].astype(F32)
        for k in range(1, self.chips):
            self.chip_copies[k, n].wait_recv()
            total = total + self.landed[k, q, rows].astype(F32)
        return total

    def finish(self):
        for copy in list(self.pair_copies.values()) + list(self.chip_copies.values()):
            copy.wait_send()


class Widen:
    def __init__(self, out, sems, chips):
        self.out, self.chips = out, chips
        self.chip_send, self.chip_recv, self.pair_send, self.pair_recv = sems
        self.chip, self.core = place()
        self.width = out.shape[-1] // (CORES * chips)
        self.forwarded, self.chip_copies = [], {}

    def spot(self, piece, k):
        q, rows = piece
        at = turned(self.chip, self.chips - k, self.chips)
        return q, rows, columns_of(at, self.core, self.width)

    def pair_copy(self, source, k, n, piece):
        self.forwarded.append(
            send(
                source,
                self.out.at[self.spot(piece, k)],
                self.pair_send.at[k, n],
                self.pair_recv.at[k, n],
                {"tensor": self.chip * CORES + 1 - self.core},
            )
        )

    def start(self, source, n, piece):
        spot = self.spot(piece, 0)
        for k in range(1, self.chips):
            self.chip_copies[k, n] = send(
                source,
                self.out.at[spot],
                self.chip_send.at[k, n],
                self.chip_recv.at[k, n],
                {"tensor": turned(self.chip, k, self.chips) * CORES + self.core},
            )
        self.pair_copy(source, 0, n, piece)
        self.out[spot] = source[...]

    def forward(self, n, piece):
        for k in range(1, self.chips):
            self.chip_copies[k, n].wait_recv()
            self.pair_copy(self.out.at[self.spot(piece, k)], k, n, piece)

    def finish(self):
        for copy in self.forwarded:
            copy.wait_recv()
        for copy in self.forwarded + list(self.chip_copies.values()):
            copy.wait_send()


PARTS = 2


def parts_of(chunk):
    parts = PARTS if chunk % (16 * PARTS) == 0 else 1
    return [slice(p * chunk // parts, (p + 1) * chunk // parts) for p in range(parts)]


def out_kernel(
    chips, client_count, group_count,
    order, part, inputs, up_at,
    cut_out, up_own,
    pair, relay, landed, cut_from, up_put, cut_put, cut_own,
    tp_sems, z_sems, y_sems, up_sems, wide_sems, *cut_at,
):
    client, group = lax.axis_index("client"), lax.axis_index("sdata")
    chip, core = place()
    share = client_count // group_count
    chunk = part.shape[1]
    width = part.shape[-1] // (CORES * chips)
    cols = columns_of(chip, core, width)
    greet(partners(chips, client_count, group_count))
    parts = parts_of(chunk)
    steps = list(range(1, client_count)) + [0]
    pieces = [(turned(client, k, client_count), rows) for rows in parts for k in steps]
    sums = ShareSum(part, pair, relay, landed, [tp_sems.at[i] for i in range(4)], pieces, chips)
    up_copies = []
    for d in range(1, group_count):
        to = turned(group, d, group_count)
        for i in range(share):
            up_put[d, i] = up_at[order[to * share + i]]
            up_copies.append(
                send(
                    up_put.at[d, i], up_own.at[group * share + i],
                    up_sems.at[0, d, i], up_sems.at[1, d, i], {"sdata": to},
                )
            )
    for i in range(share):
        up_own[group * share + i] = up_at[order[group * share + i]]
    cut_z = []
    for n, piece in enumerate(pieces):
        p, k = n // client_count, steps[n % client_count]
        to, rows = piece
        block = (sums.get(n, piece) + inputs[to, rows, cols].astype(F32)).astype(BF16)
        if k == 0:
            cut_at[p][client] = block
        else:
            cut_from[k, rows] = block
            cut_z.append(
                (
                    p,
                    send(
                        cut_from.at[k, rows], cut_at[p].at[client],
                        z_sems.at[0, p, k], z_sems.at[1, p, k], {"client": to},
                    ),
                )
            )
    widen = Widen(cut_out, [wide_sems.at[i] for i in range(4)], chips)
    rounds, y_copies = [], []

    def widen_piece(q, rows):
        widen.start(cut_own.at[q, rows], len(rounds), (q, rows))
        rounds.append((q, rows))

    for p, rows in enumerate(parts):
        for which, copy in cut_z:
            if which == p:
                copy.wait_recv()
        for d in range(1, group_count):
            to = turned(group, d, group_count)
            for i in range(share):
                cut_put[d, i, rows] = cut_at[p][order[to * share + i]]
                y_copies.append(
                    (
                        send(
                            cut_put.at[d, i, rows], cut_own.at[group * share + i, rows],
                            y_sems.at[0, p, d, i], y_sems.at[1, p, d, i], {"sdata": to},
                        ),
                        turned(group, group_count - d, group_count) * share + i,
                        rows,
                    )
                )
        for i in range(share):
            q = group * share + i
            cut_own[q, rows] = cut_at[p][order[group * share + i]]
            widen_piece(q, rows)
    for copy, q, rows in y_copies:
        copy.wait_recv()
        widen_piece(q, rows)
    for n, piece in enumerate(rounds):
        widen.forward(n, piece)
    widen.finish()
    sums.finish()
    for copy in up_copies:
        copy.wait_recv()
    for copy in up_copies + [c for unused, c in cut_z] + [c for c, unused, also in y_copies]:
        copy.wait_send()


def back_kernel(
    chips, client_count, group_count,
    inverse, part, up_own,
    grad_out,
    pair, relay, landed, y_from, z_from, own,
    tp_sems, y_sems, z_sems, wide_sems, *y_at,
):
    client, group = lax.axis_index("client"), lax.axis_index("sdata")
    share = client_count // group_count
    greet(partners(chips, client_count, group_count))
    parts = parts_of(part.shape[1])
    steps = [(d, i) for d in list(range(1, group_count)) + [0] for i in range(share)]
    pieces = [
        (turned(group, d, group_count) * share + i, rows) for rows in parts for d, i in steps
    ]
    sums = ShareSum(part, pair, relay, landed, [tp_sems.at[i] for i in range(4)], pieces, chips)
    y_copies = []
    for n, piece in enumerate(pieces):
        p, (d, i) = n // len(steps), steps[n % len(steps)]
        q, rows = piece
        block = (sums.get(n, piece) + up_own[q, rows].astype(F32)).astype(BF16)
        if d == 0:
            y_at[p][group * share + i] = block
        else:
            y_from[d, i, rows] = block
            y_copies.append(
                (
                    p,
                    send(
                        y_from.at[d, i, rows], y_at[p].at[group * share + i],
                        y_sems.at[0, p, d, i], y_sems.at[1, p, d, i],
                        {"sdata": turned(group, d, group_count)},
                    ),
                )
            )
    widen = Widen(grad_out, [wide_sems.at[i] for i in range(4)], chips)
    z_copies, rounds = [], []

    def widen_piece(q, rows):
        widen.start(own.at[q, rows], len(rounds), (q, rows))
        rounds.append((q, rows))

    for p, rows in enumerate(parts):
        for which, copy in y_copies:
            if which == p:
                copy.wait_recv()
        for k in range(1, client_count):
            to = turned(client, k, client_count)
            z_from[k, rows] = y_at[p][inverse[to]]
            z_copies.append(
                (
                    send(
                        z_from.at[k, rows], own.at[client, rows],
                        z_sems.at[0, p, k], z_sems.at[1, p, k], {"client": to},
                    ),
                    turned(client, client_count - k, client_count),
                    rows,
                )
            )
        own[client, rows] = y_at[p][inverse[client]]
        widen_piece(client, rows)
    for copy, source, rows in z_copies:
        copy.wait_recv()
        widen_piece(source, rows)
    for n, piece in enumerate(rounds):
        widen.forward(n, piece)
    widen.finish()
    sums.finish()
    for copy in [c for unused, c in y_copies] + [c for c, unused, also in z_copies]:
        copy.wait_send()


def forward_kernel(
    kv_count, sends_half, chips, count,
    rows_hbm, gain_ref, cosine_hbm, sine_hbm, upstream_hbm,
    query_hbm, key_hbm, value_hbm, output_hbm,
    normed_out, far_out, query_out, key_out, value_out, context_out, weights_out, attended_out, up_out,
    rows_ref, cosine_ref, sine_ref,
    query_mat, key_mat, value_mat, output_mat, scores, key_pair, value_turn, theirs,
    sems, z_sems, y_sems,
):
    length = rows_ref.shape[0]
    client, group = lax.axis_index("client"), lax.axis_index("sdata")
    chip, core = place()
    chunk, width = up_out.shape[1:]
    moves = (
        (rows_hbm, rows_ref), (cosine_hbm, cosine_ref), (sine_hbm, sine_ref),
        (query_hbm, query_mat), (key_hbm, key_mat), (value_hbm, value_mat), (output_hbm, output_mat),
        (upstream_hbm.at[client, :, columns_of(chip, core, width)], up_out.at[client]),
    )
    copies = []
    for i, (source, target) in enumerate(moves):
        copies.append(pltpu.make_async_copy(source, target, sems.at[i]))
        copies[-1].start()
    greet(
        [{"client": turned(client, k, count)} for k in range(1, count)]
        + ([{"sdata": 1 - group}] if sends_half else [])
    )
    sent = []
    for k in range(1, count):
        to = turned(client, k, count)
        sent.append(
            send(
                upstream_hbm.at[to, :, columns_of(chip, core, width)], up_out.at[client],
                z_sems.at[0, k], z_sems.at[1, k], {"client": to},
            )
        )
    copies[0].wait()
    rows_float = rows_ref[...].astype(F32)
    inv_rms = lax.rsqrt(jnp.mean(rows_float * rows_float, -1, keepdims=True) + 1e-05)
    normed_out[...] = (rows_float * inv_rms * gain_ref[...].astype(F32)).astype(BF16)
    if sends_half:
        wide = far_out.shape[2]
        for n in range(count // CORES):
            d = CORES * n + core
            at = pl.ds(pl.multiple_of((2 * d + 1 - group) * wide, wide), wide)
            theirs[n] = normed_out[:, at]
            sent.append(
                send(
                    theirs.at[n], far_out.at[n], y_sems.at[0, n], y_sems.at[1, n],
                    {"sdata": 1 - group},
                )
            )
    normed = normed_out[...]
    copies[1].wait()
    copies[2].wait()

    def turn(tile):
        return tile * cosine_ref[...] + swap_halves(tile) * sine_ref[...]

    copies[3].wait()
    wide = 2 * LANES
    for at in range(0, query_mat.shape[1], wide):
        part = jnp.dot(normed, query_mat[:, at : at + wide], preferred_element_type=F32)
        for side in (0, LANES):
            query_out[:, at + side : at + side + LANES] = turn(part[:, side : side + LANES]).astype(BF16)
    copies[4].wait()
    keys = turn(jnp.dot(normed, key_mat[...], preferred_element_type=F32)).astype(BF16)
    key_out[...] = keys
    copies[5].wait()
    values = jnp.dot(normed, value_mat[...], preferred_element_type=F32).astype(BF16)
    value_out[...] = values
    keys_float, values_float = keys.astype(F32), values.astype(F32)
    values_turned = values_float.T.astype(BF16)
    value_turn[...] = jnp.zeros_like(value_turn)
    for g in range(kv_count):
        key_pair[g, :length], key_pair[g, length:] = paired(keys_float, g)
        mine = values_turned[g * HEAD_DIM : (g + 1) * HEAD_DIM]
        value_turn[g, :HEAD_DIM, :length] = mine
        value_turn[g, HEAD_DIM:, length:] = mine
    tiles = query_mat.shape[1] // LANES
    step = LANES
    for t in range(tiles):
        g = t * kv_count // tiles
        scores[...] = lax.dot_general(
            key_pair[g], query_out[:, t * LANES : (t + 1) * LANES], CROSSED, preferred_element_type=F32
        )
        for head in range(2):
            base = head * length
            for i in range(0, length, step):
                deep = i + step
                block = scores[base : base + deep, i : i + step] * HEAD_DIM ** (-0.5)
                key_ids = lax.broadcasted_iota(jnp.int32, (deep, step), 0)
                query_ids = lax.broadcasted_iota(jnp.int32, (deep, step), 1) + i
                block = jnp.where(key_ids <= query_ids, block, -1e30)
                exponent = jnp.exp(block - jnp.max(block, 0, keepdims=True))
                share = 1.0 / jnp.sum(exponent, 0, keepdims=True)
                weights_out[t, base : base + deep, i : i + step] = (exponent * share).astype(BF16)
                if deep < length:
                    weights_out[t, base + deep : base + length, i : i + step] = jnp.zeros(
                        (length - deep, step), BF16
                    )
        turned_context = jnp.dot(value_turn[g], weights_out[t], preferred_element_type=F32)
        context_out[:, t * LANES : (t + 1) * LANES] = turned_context.T.astype(BF16)
    copies[6].wait()
    context = context_out[...]
    wide = next(b for b in (512, 256, 128) if attended_out.shape[1] % b == 0)
    for at in range(0, attended_out.shape[1], wide):
        attended_out[:, at : at + wide] = lax.dot_general(
            context, output_mat[at : at + wide, :], CROSSED, preferred_element_type=F32
        ).astype(BF16)
    copies[7].wait()
    for copy in sent:
        copy.wait_recv()
    for copy in sent:
        copy.wait_send()


def forward(rows_in, gain, tables, upstream, matrices, kv_count):
    chips, count, unused = axis_counts()
    length, breadth = rows_in.shape
    features, shared = matrices[0].shape[1], matrices[1].shape[1]
    tiles = features // LANES
    rows = breadth // (2 * count)
    sends_half = rows % LANES == 0
    shape = lambda *sizes: jax.ShapeDtypeStruct(sizes, BF16)
    half = (count // CORES, length, rows) if sends_half else (16, LANES)
    chunk, width = length // count, breadth // (CORES * chips)
    dma = pltpu.SemaphoreType.DMA
    return pl.pallas_call(
        partial(forward_kernel, kv_count, sends_half, chips, count),
        out_shape=(
            shape(length, breadth), shape(*half), shape(length, features), shape(length, shared),
            shape(length, shared), shape(length, features), shape(tiles, 2 * length, length),
            shape(length, breadth), shape(count, chunk, width),
        ),
        in_specs=[ANY_SPEC, VMEM_SPEC] + [ANY_SPEC] * 7,
        out_specs=(VMEM_SPEC,) * 9,
        scratch_shapes=[pltpu.VMEM(rows_in.shape, BF16)]
        + [pltpu.VMEM(table.shape, F32) for table in tables]
        + [pltpu.VMEM(m.shape, BF16) for m in matrices]
        + [
            pltpu.VMEM((2 * length, length), F32),
            pltpu.VMEM((kv_count, 2 * length, LANES), BF16),
            pltpu.VMEM((kv_count, LANES, 2 * length), BF16),
            pltpu.VMEM(half, BF16),
            dma((8,)), dma((2, count)), dma((2, count)),
        ],
        compiler_params=params(4),
        name="forward",
    )(rows_in, gain, *tables, upstream.reshape(count, chunk, breadth), *matrices)


def server_kernel(
    chips, shares,
    rows_ref, own_ref, gain_ref, context_ref, half_ref, gate_hbm, up_hbm, down_hbm,
    out_ref, far_context, far_normed,
    up_all, normed_ref, gate_value, up_value, gate_grad, up_grad, weighted_ref,
    gate_ref, up_ref, down_ref, load_sems, wide_sems, far_sems, core_sems, local_sems,
):
    length, breadth = rows_ref.shape
    hidden = gate_ref.shape[1]
    block = next(b for b in (512, 256, 128, hidden) if hidden % b == 0)
    spans = [slice(at, at + block) for at in range(0, hidden, block)]

    def loads(i, which):
        source, target = ((gate_hbm, gate_ref), (up_hbm, up_ref), (down_hbm, down_ref))[which]
        at = (spans[i], slice(None)) if which == 2 else (slice(None), spans[i])
        return pltpu.make_async_copy(source.at[at], target.at[at], load_sems.at[which, i])

    for which in range(3):
        for i in range(len(spans)):
            loads(i, which).start()
    group = lax.axis_index("sdata")
    chip, core = place()
    sibling = {"tensor": chip * CORES + 1 - core}
    greet(
        [sibling, {"sdata": 1 - group}]
        + [{"tensor": turned(chip, k, chips) * CORES + core} for k in range(1, chips)]
    )
    widen = Widen(up_all, [wide_sems.at[i] for i in range(4)], chips)
    count = own_ref.shape[0]
    for q in range(count):
        widen.start(own_ref.at[q], q, (q, slice(None)))
    others = [
        send(context_ref, far_context, far_sems.at[0], far_sems.at[1], {"sdata": 1 - group})
    ]
    kept = []
    for n in range(shares):
        d = CORES * n + core
        others.append(
            send(half_ref.at[n], far_normed.at[d], core_sems.at[0, n], core_sems.at[1, n], sibling)
        )
        kept.append(pltpu.make_async_copy(half_ref.at[n], far_normed.at[d], local_sems.at[n]))
        kept[-1].start()
    rows_float = rows_ref[...].astype(F32)
    gain = gain_ref[...].astype(F32)
    inv_rms = lax.rsqrt(jnp.mean(rows_float * rows_float, -1, keepdims=True) + 1e-05)
    normed_ref[...] = (rows_float * inv_rms * gain).astype(BF16)
    for i, span in enumerate(spans):
        loads(i, 0).wait()
        gate_value[:, span] = jnp.dot(normed_ref[...], gate_ref[:, span], preferred_element_type=F32)
        loads(i, 1).wait()
        up_value[:, span] = jnp.dot(normed_ref[...], up_ref[:, span], preferred_element_type=F32)
    for q in range(count):
        widen.forward(q, (q, slice(None)))
    widen.finish()
    upstream = up_all[...].reshape(length, breadth)
    for i, span in enumerate(spans):
        loads(i, 2).wait()
        pulled = lax.dot_general(upstream, down_ref[span], CROSSED, preferred_element_type=F32)
        gate, up = gate_value[:, span], up_value[:, span]
        sigmoid_gate = jax.nn.sigmoid(gate)
        gate_grad[:, span] = (
            pulled * up * sigmoid_gate * (1.0 + gate * (1.0 - sigmoid_gate))
        ).astype(BF16)
        up_grad[:, span] = (pulled * gate * sigmoid_gate).astype(BF16)
    step = next(b for b in (256, 128, breadth) if breadth % b == 0)
    lean = jnp.zeros((length, 1), F32)
    for at in range(0, breadth, step):
        span = slice(at, at + step)
        weighted = (
            lax.dot_general(gate_grad[...], gate_ref[span], CROSSED, preferred_element_type=F32)
            + lax.dot_general(up_grad[...], up_ref[span], CROSSED, preferred_element_type=F32)
        ) * gain_ref[:, span].astype(F32)
        weighted_ref[:, span] = weighted
        lean = lean + jnp.sum(weighted * rows_ref[:, span].astype(F32), -1, keepdims=True)
    pull = inv_rms**3 * (lean * (1.0 / breadth))
    out_ref[...] = (inv_rms * weighted_ref[...] - rows_ref[...].astype(F32) * pull).astype(BF16)
    for copy in others:
        copy.wait_recv()
    for copy in others:
        copy.wait_send()
    for copy in kept:
        copy.wait()


def server_pull(rows_in, up_own, gain, context, half, gate_matrix, up_matrix, down_matrix):
    chips, count, unused = axis_counts()
    length, breadth = rows_in.shape
    hidden = gate_matrix.shape[1]
    shares = half.shape[0] if half.ndim == 3 else 0
    full = (count,) + half.shape[1:] if shares else half.shape
    dma = pltpu.SemaphoreType.DMA
    vmem = lambda *sizes: pltpu.VMEM(sizes, BF16)
    wide = lambda *sizes: pltpu.VMEM(sizes, F32)
    return pl.pallas_call(
        partial(server_kernel, chips, shares),
        out_shape=(
            jax.ShapeDtypeStruct((length, breadth), BF16),
            jax.ShapeDtypeStruct(context.shape, BF16),
            jax.ShapeDtypeStruct(full, BF16),
        ),
        in_specs=[VMEM_SPEC] * 5 + [ANY_SPEC] * 3,
        out_specs=(VMEM_SPEC,) * 3,
        scratch_shapes=[
            vmem(count, length // count, breadth), vmem(length, breadth),
            wide(length, hidden), wide(length, hidden), vmem(length, hidden), vmem(length, hidden),
            wide(length, breadth),
            vmem(breadth, hidden), vmem(breadth, hidden), vmem(hidden, breadth),
            dma((3, hidden // LANES)), dma((4, chips, count)), dma((2,)), dma((2, count)),
            dma((count,)),
        ],
        compiler_params=params(5),
        name="server_pull",
    )(rows_in, up_own, gain[None], context, half, gate_matrix, up_matrix, down_matrix)


class Chain:
    def __init__(self, own, forth, back, sems, count):
        self.own, self.forth, self.back, self.count = own, forth, back, count
        self.sems = sems
        self.at = lax.axis_index("client")

    def copy(self, way, j, d):
        landing = self.forth if way == 0 else self.back
        to = self.at + 1 if way == 0 else self.at - 1
        return pltpu.make_async_remote_copy(
            src_ref=self.own.at[d],
            dst_ref=landing.at[j],
            send_sem=self.sems.at[2 * way, j],
            recv_sem=self.sems.at[2 * way + 1, j],
            device_id={"client": lax.rem(to + self.count, self.count)},
            device_id_type=MESH,
        )

    def legs(self):
        for j in range(self.count - 1):
            for way in (0, 1):
                d = self.count - 1 - j if way == 0 else j
                end = 0 if way == 0 else self.count - 1
                beyond = self.at < d if way == 0 else self.at > d
                yield way, j, d, end, beyond

    def open(self, d, way):
        j = self.count - 1 - d if way == 0 else d
        if j < self.count - 1:
            end = 0 if way == 0 else self.count - 1

            @pl.when(self.at == end)
            def _():
                self.copy(way, j, d).start()

    def relay(self):
        near = self.at < self.count // 2
        legs = list(self.legs())
        turns = [(leg, near) for leg in legs if leg[0] == 0]
        turns += [(leg, self.at >= 0) for leg in legs if leg[0] == 1]
        turns += [(leg, jnp.logical_not(near)) for leg in legs if leg[0] == 0]
        for (way, j, d, end, beyond), now in turns:
            landing = self.forth if way == 0 else self.back

            @pl.when(now & beyond & (self.at != end))
            def _(way=way, j=j, d=d, landing=landing):
                self.copy(way, j, d).wait_recv()
                self.own[d] = (self.own[d].astype(F32) + landing[j].astype(F32)).astype(BF16)
                self.copy(way, j, d).start()

    def total(self, out_refs):
        last = self.count - 1
        for way, end, j in ((0, 0, last - self.at), (1, last, self.at)):
            landing = self.forth if way == 0 else self.back

            @pl.when(self.at != end)
            def _(way=way, j=j, landing=landing):
                self.copy(way, j, 0).wait_recv()
                self.own[self.at] = (
                    self.own[self.at].astype(F32) + landing[j].astype(F32)
                ).astype(BF16)

        result = (self.own[self.at].astype(F32) * (1.0 / self.count)).astype(BF16)
        at = 0
        for out in out_refs:
            out[...] = result[:, at : at + out.shape[1]]
            at += out.shape[1]

    def finish(self):
        for way, j, d, end, beyond in self.legs():

            @pl.when(beyond)
            def _(way=way, j=j, d=d):
                self.copy(way, j, d).wait_send()


def learn_kernel(
    kv_count, count, aligned,
    cut_ref, output_ref, query_ref, key_ref, value_ref, context_ref, weights_ref, normed_ref,
    far_normed, far_context, cosine_ref, sine_ref, *refs,
):
    if not aligned:
        near_cut, give_cut, near_normed, refs = refs[0], refs[1], refs[2], refs[3:]
    query_out, key_out, value_out, output_out = refs[:4]
    (
        pulled, pair, key_turn, value_pair, weight_grad, score_grad, query_grad, shared_grad,
        far_cut, far_query, far_shared,
        output_own, output_forth, output_back, shared_own, shared_forth, shared_back,
        query_own, query_forth, query_back,
        cut_sems, core_sems, give_sems, output_sems, shared_sems, query_sems,
    ) = refs[4:]
    length = cut_ref.shape[0]
    rows = far_cut.shape[2]
    client, group = lax.axis_index("client"), lax.axis_index("sdata")
    tensor_at = lax.axis_index("tensor")
    core = lax.rem(tensor_at, CORES)
    sibling = {"tensor": tensor_at + 1 - 2 * core}
    across = {"sdata": 1 - group}
    ahead = {"client": lax.rem(client + 1, count)}
    behind = {"client": lax.rem(client + count - 1, count)}
    greet([sibling, across, ahead, behind])
    order = []
    for j in range((count + 1) // 2):
        order += [count - 1 - j, j]

    def columns(d, side):
        return pl.ds(pl.multiple_of((2 * d + side) * rows, rows), rows)

    def cut_copy(n, d):
        source = cut_ref.at[:, columns(d, 1 - group)] if aligned else give_cut.at[d]
        return pltpu.make_async_remote_copy(
            src_ref=source, dst_ref=far_cut.at[d],
            send_sem=cut_sems.at[0, n], recv_sem=cut_sems.at[1, n],
            device_id=across, device_id_type=MESH,
        )

    def core_copy(n, d):
        return pltpu.make_async_remote_copy(
            src_ref=far_cut.at[d], dst_ref=far_cut.at[d],
            send_sem=core_sems.at[0, n], recv_sem=core_sems.at[1, n],
            device_id=sibling, device_id_type=MESH,
        )

    halves = count // CORES
    picks = [order[CORES * n] + core * (order[CORES * n + 1] - order[CORES * n]) for n in range(halves)]
    others = [
        order[CORES * n + 1] + core * (order[CORES * n] - order[CORES * n + 1]) for n in range(halves)
    ]
    for n in range(halves):
        cut_copy(n, picks[n]).start()

    width = 2 * LANES if query_ref.shape[1] % (2 * LANES) == 0 else LANES
    for at in range(0, query_ref.shape[1], width):
        pulled[:, at : at + width] = jnp.dot(
            cut_ref[...], output_ref[:, at : at + width], preferred_element_type=F32
        ).astype(BF16)
    keys_float, values_float = key_ref[...].astype(F32), value_ref[...].astype(F32)
    keys_turned = keys_float.T.astype(BF16)
    key_turn[...] = jnp.zeros_like(key_turn)
    score_grad[...] = jnp.zeros_like(score_grad)
    for g in range(kv_count):
        value_pair[g, :length], value_pair[g, length:] = paired(values_float, g)
        mine = keys_turned[g * HEAD_DIM : (g + 1) * HEAD_DIM]
        key_turn[g, :HEAD_DIM, :length] = mine
        key_turn[g, HEAD_DIM:, length:] = mine

    def unturn(tile):
        return tile * cosine_ref[...] - swap_halves(tile) * sine_ref[...]

    tiles = query_ref.shape[1] // LANES
    low = lane_tile() < HEAD_DIM
    key_sum, value_sum = [None] * kv_count, [None] * kv_count
    for t in range(tiles):
        g = t * kv_count // tiles
        span = slice(t * LANES, (t + 1) * LANES)
        weight_grad[...] = lax.dot_general(
            value_pair[g], pulled[:, span], CROSSED, preferred_element_type=F32
        )
        for head in range(2):
            base = head * length
            for i in range(0, length, LANES):
                deep = i + LANES
                grad = weight_grad[base : base + deep, i : i + LANES].astype(BF16).astype(F32)
                weight = weights_ref[t, base : base + deep, i : i + LANES].astype(F32)
                both = grad * weight
                drift = jnp.sum(both, 0, keepdims=True)
                score_grad[base : base + deep, i : i + LANES] = (
                    (both - weight * drift) * HEAD_DIM ** (-0.5)
                ).astype(BF16)
        back_query = jnp.dot(key_turn[g], score_grad[...], preferred_element_type=F32)
        query_grad[:, span] = unturn(back_query.T.astype(BF16).astype(F32)).astype(BF16)
        back_key = jnp.dot(score_grad[...], query_ref[:, span], preferred_element_type=F32)
        back_value = jnp.dot(weights_ref[t], pulled[:, span], preferred_element_type=F32)
        first = key_sum[g] is None
        key_sum[g] = back_key if first else key_sum[g] + back_key
        value_sum[g] = back_value if first else value_sum[g] + back_value

    def folded(sums):
        whole = None
        for g, both in enumerate(sums):
            upper, lower = both[:length], both[length:]
            if g == 0:
                whole = upper + pltpu.roll(lower, HEAD_DIM, 1)
            else:
                whole = jnp.where(low, whole, pltpu.roll(upper, HEAD_DIM, 1) + lower)
        return whole.astype(BF16)

    shared_grad[:, :LANES] = unturn(folded(key_sum).astype(F32)).astype(BF16)
    shared_grad[:, LANES:] = folded(value_sum)

    def give(source, target, i):
        return pltpu.make_async_remote_copy(
            src_ref=source, dst_ref=target, send_sem=give_sems.at[0, i], recv_sem=give_sems.at[1, i],
            device_id=across, device_id_type=MESH,
        )

    gifts = [give(shared_grad, far_shared, 0), give(query_grad, far_query, 1)]
    for gift in gifts:
        gift.start()
    chains = [
        Chain(output_own, output_forth, output_back, output_sems, count),
        Chain(shared_own, shared_forth, shared_back, shared_sems, count),
        Chain(query_own, query_forth, query_back, query_sems, count),
    ]

    def near(d, from_cut):
        if aligned:
            return (cut_ref if from_cut else normed_ref)[:, columns(d, group)]
        return near_cut[d] if from_cut else near_normed[d]

    def product(chain, d, left, right, far_left, far_right):
        chain.own[d] = (
            lax.dot_general(left, right, TALL, preferred_element_type=F32)
            + lax.dot_general(far_left, far_right, TALL, preferred_element_type=F32)
        ).astype(BF16)

    for n in range(halves):
        cut_copy(n, picks[n]).wait_recv()
        core_copy(n, picks[n]).start()
        core_copy(n, others[n]).wait_recv()
        for i in range(CORES):
            d = order[CORES * n + i]
            product(chains[0], d, near(d, True), context_ref[...], far_cut[d], far_context[...])
            for way in (0, 1):
                chains[0].open(d, way)

    def spread(chain, grad, far_grad):
        for d in order:
            product(chain, d, near(d, False), grad[...], far_normed[d], far_grad[...])
            for way in (0, 1):
                chain.open(d, way)

    gifts[0].wait_recv()
    spread(chains[1], shared_grad, far_shared)
    chains[0].relay()
    gifts[1].wait_recv()
    spread(chains[2], query_grad, far_query)
    chains[1].relay()
    chains[2].relay()
    chains[0].total([output_out])
    chains[1].total([key_out, value_out])
    chains[2].total([query_out])
    for n in range(halves):
        cut_copy(n, picks[n]).wait_send()
        core_copy(n, picks[n]).wait_send()
    for gift in gifts:
        gift.wait_send()
    for chain in chains:
        chain.finish()


def learn(cut_grad, output_matrix, saved, normed, far_normed, far_context, tables, kv_count):
    unused, count, group_count = axis_counts()
    queries, keys, values, context, weights = saved
    length, breadth = cut_grad.shape
    features = queries.shape[1]
    rows = breadth // (count * group_count)
    aligned = rows % LANES == 0
    dma = pltpu.SemaphoreType.DMA
    shape = lambda *sizes: jax.ShapeDtypeStruct(sizes, BF16)
    vmem = lambda *sizes: pltpu.VMEM(sizes, BF16)
    operands = [cut_grad, output_matrix, queries, keys, values, context, weights, normed]
    operands += [far_normed, far_context, *tables]
    if not aligned:
        group = lax.axis_index("sdata")
        operands += [
            half_of(cut_grad, count, group), half_of(cut_grad, count, 1 - group),
            half_of(normed, count, group),
        ]
    chain = lambda wide: [
        vmem(count, rows, wide), vmem(count - 1, rows, wide), vmem(count - 1, rows, wide)
    ]
    return pl.pallas_call(
        partial(learn_kernel, kv_count, count, aligned),
        out_shape=(
            shape(rows, features), shape(rows, LANES), shape(rows, LANES), shape(rows, features)
        ),
        in_specs=[VMEM_SPEC] * len(operands),
        out_specs=(VMEM_SPEC,) * 4,
        scratch_shapes=[
            vmem(length, features), vmem(16, LANES), vmem(kv_count, LANES, 2 * length),
            vmem(kv_count, 2 * length, LANES), pltpu.VMEM((2 * length, length), F32),
            vmem(2 * length, length), vmem(length, features), vmem(length, 2 * LANES),
            vmem(count, length, rows), vmem(length, features), vmem(length, 2 * LANES),
        ]
        + chain(features) + chain(2 * LANES) + chain(features)
        + [dma((2, count // CORES)), dma((2, count // CORES)), dma((2, 2))]
        + [dma((4, count - 1))] * 3,
        compiler_params=params(3),
        name="learn",
    )(*operands)


def half_of(array, count, side):
    blocks = array.reshape(array.shape[0], count, 2, -1)
    return lax.dynamic_index_in_dim(blocks, side, 2, False).transpose(1, 0, 2)


def across_groups(array):
    count = lax.axis_size("sdata")
    return lax.ppermute(array, "sdata", [(g, (g + 1) % count) for g in range(count)])


def tables_of(length):
    halfway = HEAD_DIM // 2
    lanes = jnp.arange(LANES) % HEAD_DIM
    frequencies = jnp.exp(-math.log(500000.0) * (2.0 / HEAD_DIM) * (lanes % halfway).astype(F32))
    angles = jnp.arange(length).astype(F32)[:, None] * frequencies[None, :]
    sign = jnp.where(lanes < halfway, -1.0, 1.0)
    return jnp.cos(angles), jnp.sin(angles) * sign[None, :]


def widened(matrix):
    return jnp.pad(matrix, ((0, 0), (0, LANES - matrix.shape[1])))


def relay_out(order, attended, rows_in, up_at):
    chips, client_count, group_count = axis_counts()
    length, breadth = rows_in.shape
    chunk, width = length // client_count, breadth // (CORES * chips)
    share = client_count // group_count
    parts = len(parts_of(chunk))
    full = (client_count, chunk, breadth)
    own = (client_count, chunk, width)
    dma = pltpu.SemaphoreType.DMA
    vmem = lambda shape: pltpu.VMEM(shape, BF16)
    cut, up_own = pl.pallas_call(
        partial(out_kernel, chips, client_count, group_count),
        out_shape=(jax.ShapeDtypeStruct(full, BF16), jax.ShapeDtypeStruct(own, BF16)),
        in_specs=[SMEM_SPEC, VMEM_SPEC, VMEM_SPEC, VMEM_SPEC],
        out_specs=(VMEM_SPEC,) * 2,
        scratch_shapes=[
            vmem((chips,) + own), vmem((chips,) + own), vmem((chips,) + own), vmem(own),
            vmem((group_count, share, chunk, width)), vmem((group_count, share, chunk, width)),
            vmem(own),
            dma((4, chips, parts * client_count)), dma((2, parts, client_count)),
            dma((2, parts, group_count, share)), dma((2, group_count, share)),
            dma((4, chips, parts * client_count)),
        ]
        + [vmem((client_count, chunk // parts, width))] * parts,
        compiler_params=params(1),
        name="relay_out",
    )(order, attended.reshape(full), rows_in.reshape(full), up_at)
    return cut.reshape(length, breadth), up_own


def relay_back(inverse, pulled, up_own):
    chips, client_count, group_count = axis_counts()
    length, breadth = pulled.shape
    chunk, width = length // client_count, breadth // (CORES * chips)
    share = client_count // group_count
    parts = len(parts_of(chunk))
    full = (client_count, chunk, breadth)
    own = (client_count, chunk, width)
    dma = pltpu.SemaphoreType.DMA
    vmem = lambda shape: pltpu.VMEM(shape, BF16)
    grad = pl.pallas_call(
        partial(back_kernel, chips, client_count, group_count),
        out_shape=jax.ShapeDtypeStruct(full, BF16),
        in_specs=[SMEM_SPEC, VMEM_SPEC, VMEM_SPEC],
        out_specs=VMEM_SPEC,
        scratch_shapes=[
            vmem((chips,) + own), vmem((chips,) + own), vmem((chips,) + own),
            vmem((group_count, share, chunk, width)), vmem(own), vmem(own),
            dma((4, chips, parts * client_count)), dma((2, parts, group_count, share)),
            dma((2, parts, client_count)), dma((4, chips, parts * client_count)),
        ]
        + [vmem((client_count, chunk // parts, width))] * parts,
        compiler_params=params(2),
        name="relay_back",
    )(inverse, pulled.reshape(full), up_own)
    return grad.reshape(length, breadth)


def local(
    client_input,
    client_gain,
    query_weight,
    key_weight,
    client_value_weight,
    output_weight,
    server_gain,
    server_gate,
    server_up,
    server_down,
    upstream,
    assignment,
):
    client_count = lax.axis_size("client")
    shared = key_weight.shape[2]
    kv_count = shared // HEAD_DIM
    tables = tables_of(client_input.shape[0])
    matrices = [
        query_weight[0], widened(key_weight[0]), widened(client_value_weight[0]), output_weight[0]
    ]
    normed, half, *saved, attended, up_at = forward(
        client_input, client_gain, tables, upstream, matrices, kv_count
    )
    ids = jnp.arange(client_count).astype(jnp.int32)
    ahead = (assignment[None, :] < assignment[:, None]) | (
        (assignment[None, :] == assignment[:, None]) & (ids[None, :] < ids[:, None])
    )
    inverse = jnp.sum(ahead.astype(jnp.int32), 1)
    group_order = jnp.sum(jnp.where(inverse[None, :] == ids[:, None], ids[None, :], 0), 1)
    cut_rows, up_own = relay_out(group_order, attended, client_input, up_at)
    pulled, far_context, far_normed = server_pull(
        cut_rows, up_own, server_gain[0], saved[3], half,
        server_gate[0], server_up[0], server_down[0],
    )
    if half.ndim == 2:
        far_normed = across_groups(half_of(normed, client_count, 1 - lax.axis_index("sdata")))
    arriving_grad = relay_back(inverse, pulled, up_own)
    query_update, key_update, value_update, output_update = learn(
        arriving_grad, output_weight[0], saved, normed, far_normed, far_context, tables, kv_count
    )
    return (query_update, key_update[:, :shared], value_update[:, :shared], output_update)


def solution(mesh):
    placed = (
        P(("client", "sdata"), None),
        P("client", None),
        P("client", None, "tensor"),
        P("client", None, "tensor"),
        P("client", None, "tensor"),
        P("client", None, "tensor"),
        P("sdata", None),
        P("sdata", None, "tensor"),
        P("sdata", None, "tensor"),
        P("sdata", "tensor", None),
        P(("client", "sdata"), None),
        P(),
    )
    return jax.shard_map(
        local,
        mesh=mesh,
        in_specs=placed,
        out_specs=(
            P(("client", "sdata"), "tensor"),
            P(("client", "sdata"), "tensor"),
            P(("client", "sdata"), "tensor"),
            P(("client", "sdata"), "tensor"),
        ),
        check_vma=False,
    )
```

time: 195 us -> 170 us (0.87)
  the two profiles are of different devices: /device:TPU:0 before, /device:TPU:8 now
where the time goes in v2:
time: 170 us
  Pallas kernels  159 us (94%)
  local copies, waits for them, and re-layouts  8 us (5%)
  other arithmetic  1.81 us (1%)
    pallas_call x1, Pallas kernels, learn(): pl.pallas_call(partial(learn_kernel, kv_count, count, aligned), out_shape...  65.8 us
    pallas_call x1, Pallas kernels, relay_back(): pl.pallas_call(partial(back_kernel, chips, client_count, group_count), ou...  29.3 us
    pallas_call x1, Pallas kernels, relay_out(): pl.pallas_call(partial(out_kernel, chips, client_count, group_count), out...  28.3 us
    pallas_call x1, Pallas kernels, server_pull(): pl.pallas_call(partial(server_kernel, chips, shares), out_shape=(jax.Shap...  19.4 us
    pallas_call x1, Pallas kernels, forward(): pl.pallas_call(partial(forward_kernel, kv_count, sends_half, chips, count...  16.2 us
    unnamed x18, local copies, waits for them, and re-layouts  8 us

profile of v2, /device:TPU:8, one launch (start us, length us, event | category | flops | bytes accessed | tf_op | source)
XLA Modules:
  0.0 169.5 jit_solution(16084955025170311029)
XLA Ops:
  0.6 0.9 convert_reduce_fusion.inverse
  1.5 0.1 select_reduce_fusion.order
  1.7 0.8 fusion
  2.5 0.0 copy-start.3
  2.5 1.0 copy-done.3
  3.5 0.0 copy-start.4
  3.5 1.0 copy-done.4
  4.5 0.0 copy-start.6
  4.5 0.7 copy-done.6
  5.2 0.0 copy-start
  5.2 16.2 %forward.1 = (bf16[384,2048]{1,0:T(8,128)(2,1)S(1)}, bf16[2,384,256]{2,1,0:T(8,128)(2,1)S(1)}, bf16[384,512]{1,0:T(8,128)(2,1)S(1)}, bf16[384,128]{1,0:T(8,128)(...) custom-call(bf16[384,2048]{1,0:T(8,128)(2,1)} %rows_hbm.1, ...), custom_call_target="tpu_custom_call" | custom-call | tf_op jit(solution)/shard_map/forward/pallas_call | solution.py:497
  21.5 0.0 copy-start.1
  21.5 1.1 copy-done.1
  22.6 0.0 copy-done
  22.6 0.0 copy-start.2
  22.6 1.4 copy-done.2
  24.0 0.0 copy-start.5
  24.0 28.3 %relay_out.1 = (bf16[4,96,2048]{2,1,0:T(8,128)(2,1)S(1)}, bf16[4,96,512]{2,1,0:T(8,128)(2,1)S(1)}) custom-call(s32[4]{0:T(128)S(1)} %select_reduce_fusion.order, bf16[4,96,2048]{2,1,0:T(8,128)(2,1)S(1)} %bitcast.16, bf16[4,96,2048]{2,1,0:T(8,128)(2,1)S(1)} %bitcast.13, bf16[4,96,512]{2,1,0:T(8,128)(2,1)S(1)} %get-tuple-element.19.up_at), custom_call_target="tpu_custom_call" | custom-call | tf_op jit(solution)/shard_map/relay_out/pallas_call | solution.py:962
  52.3 0.0 copy-done.5
  52.3 19.4 %server_pull.1 = (bf16[384,2048]{1,0:T(8,128)(2,1)S(1)}, bf16[384,512]{1,0:T(8,128)(2,1)S(1)}, bf16[4,384,256]{2,1,0:T(8,128)(2,1)S(1)}) custom-call(bf16[384,2048]{1,0:T(8,128)(2,1)S(1)} %bitcast.15, bf16[4,96,512]{2,1,0:T(8,128)(2,1)S(1)} %get-tuple-element.21.own_ref.up_own, bf16[1,2048]{1,0:T(2,128)(2,1)S(1)} %copy-done.5, ...), custom_call_target="tpu_custom_call" | custom-call | tf_op jit(solution)/shard_map/server_pull/pallas_call | solution.py:614
  71.7 29.3 %relay_back.1 = bf16[4,96,2048]{2,1,0:T(8,128)(2,1)S(1)} custom-call(s32[4]{0:T(128)S(1)} %convert_reduce_fusion.inverse, bf16[4,96,2048]{2,1,0:T(8,128)(2,1)S(1)} %bitcast.17, bf16[4,96,512]{2,1,0:T(8,128)(2,1)S(1)} %get-tuple-element.21.own_ref.up_own), custom_call_target="tpu_custom_call" | custom-call | tf_op jit(solution)/shard_map/relay_back/pallas_call | solution.py:992
  101.0 65.8 %learn.1 = (bf16[256,512]{1,0:T(8,128)(2,1)S(1)}, bf16[256,128]{1,0:T(8,128)(2,1)S(1)}, bf16[256,128]{1,0:T(8,128)(2,1)S(1)}, bf16[256,512]{1,0:T(8,128)(2,1)S(1)}) custom-call(bf16[384,2048]{1,0:T(8,128)(2,1)S(1)} %bitcast.14, bf16[2048,512]{1,0:T(8,128)(2,1)} %bitcast.21, bf16[384,512]{1,0:T(8,128)(2,1)S(1)} %get-tuple-element.25.query_ref, ...), custom_call_target="tpu_custom_call" | custom-call | tf_op jit(solution)/shard_map/learn/pallas_call | solution.py:908
  166.8 0.7 copy.20
  167.5 0.6 copy.21
  168.2 0.6 copy.22
  168.8 0.7 copy.23
  (2 shorter events, 0.0 us)
Async XLA Ops:
  2.5 1.0 copy-start.3
  3.5 1.0 copy-start.4
  4.5 0.7 copy-start.6
  5.2 17.4 %copy-start = (bf16[384,2048]{1,0:T(8,128)(2,1)S(1)}, bf16[384,2048]{1,0:T(8,128)(2,1)}, u32[]{:S(2)}) copy-start(bf16[384,2048]{1,0:T(8,128)(2,1)} %rows_hbm.1) | copy-start | bytes 4718596
  21.5 1.2 copy-start.1
  22.6 1.4 copy-start.2
  24.0 28.3 %copy-start.5 = (bf16[1,2048]{1,0:T(2,128)(2,1)S(1)}, bf16[1,2048]{1,0:T(2,128)(2,1)}, u32[]{:S(2)}) copy-start(bf16[1,2048]{1,0:T(2,128)(2,1)} %gain_ref.3) | copy-start | bytes 12292

commit v3 on v2

--- a/solution.py
+++ b/solution.py
@@ -3,6 +3,7 @@
 
 import jax
 import jax.numpy as jnp
+import numpy as np
 from jax import lax
 from jax.experimental import pallas as pl
 from jax.experimental.pallas import tpu as pltpu
@@ -27,6 +28,13 @@
     return jnp.where(low, ahead, behind)
 
 
+def unfold(table, cosine_ref, sine_ref):
+    low = lane_tile() < HEAD_DIM
+    moved = pltpu.roll(table, HEAD_DIM, 1)
+    cosine_ref[...] = jnp.where(low, table, moved)
+    sine_ref[...] = jnp.where(low, moved, table)
+
+
 def paired(tile, at):
     low = lane_tile() < HEAD_DIM
     moved = pltpu.roll(tile, HEAD_DIM, 1)
@@ -40,13 +48,13 @@
 
 
 VMEM_SPEC = pl.BlockSpec(memory_space=pltpu.VMEM)
-ANY_SPEC = pl.BlockSpec(memory_space=pl.ANY)
+HBM_SPEC = pl.BlockSpec(memory_space=pltpu.HBM)
 SMEM_SPEC = pl.BlockSpec(memory_space=pltpu.SMEM)
 
 
-def params(number):
+def params(number, mebibytes):
     return pltpu.CompilerParams(
-        collective_id=number, has_side_effects=True, vmem_limit_bytes=48 * 2**20
+        collective_id=number, has_side_effects=True, vmem_limit_bytes=mebibytes * 2**20
     )
 
 
@@ -206,40 +214,41 @@
 
 def out_kernel(
     chips, client_count, group_count,
-    order, part, inputs, up_at,
-    cut_out, up_own,
+    order, sent, part, inputs, up_at,
+    cut_out, up_own, up_all,
     pair, relay, landed, cut_from, up_put, cut_put, cut_own,
-    tp_sems, z_sems, y_sems, up_sems, wide_sems, *cut_at,
+    tp_sems, z_sems, y_sems, up_sems, wide_sems, kept_sems, *cut_at,
 ):
     client, group = lax.axis_index("client"), lax.axis_index("sdata")
-    chip, core = place()
     share = client_count // group_count
     chunk = part.shape[1]
-    width = part.shape[-1] // (CORES * chips)
-    cols = columns_of(chip, core, width)
-    greet(partners(chips, client_count, group_count))
     parts = parts_of(chunk)
     steps = list(range(1, client_count)) + [0]
     pieces = [(turned(client, k, client_count), rows) for rows in parts for k in steps]
     sums = ShareSum(part, pair, relay, landed, [tp_sems.at[i] for i in range(4)], pieces, chips)
+    for copy in sent:
+        copy.wait_recv()
     up_copies = []
     for d in range(1, group_count):
         to = turned(group, d, group_count)
         for i in range(share):
-            up_put[d, i] = up_at[order[to * share + i]]
+            up_put[d, i] = up_at[order(to * share + i)]
             up_copies.append(
                 send(
                     up_put.at[d, i], up_own.at[group * share + i],
                     up_sems.at[0, d, i], up_sems.at[1, d, i], {"sdata": to},
                 )
             )
+    kept = Widen(up_all, [kept_sems.at[i] for i in range(4)], chips)
     for i in range(share):
-        up_own[group * share + i] = up_at[order[group * share + i]]
+        q = group * share + i
+        up_own[q] = up_at[order(q)]
+        kept.start(up_own.at[q], i, (q, slice(None)))
     cut_z = []
     for n, piece in enumerate(pieces):
         p, k = n // client_count, steps[n % client_count]
         to, rows = piece
-        block = (sums.get(n, piece) + inputs[to, rows, cols].astype(F32)).astype(BF16)
+        block = (sums.get(n, piece) + inputs[to, rows].astype(F32)).astype(BF16)
         if k == 0:
             cut_at[p][client] = block
         else:
@@ -267,7 +276,7 @@
         for d in range(1, group_count):
             to = turned(group, d, group_count)
             for i in range(share):
-                cut_put[d, i, rows] = cut_at[p][order[to * share + i]]
+                cut_put[d, i, rows] = cut_at[p][order(to * share + i)]
                 y_copies.append(
                     (
                         send(
@@ -280,24 +289,97 @@
                 )
         for i in range(share):
             q = group * share + i
-            cut_own[q, rows] = cut_at[p][order[group * share + i]]
+            cut_own[q, rows] = cut_at[p][order(group * share + i)]
             widen_piece(q, rows)
     for copy, q, rows in y_copies:
         copy.wait_recv()
         widen_piece(q, rows)
+    for i in range(share):
+        kept.forward(i, (group * share + i, slice(None)))
     for n, piece in enumerate(rounds):
         widen.forward(n, piece)
     widen.finish()
+    kept.finish()
     sums.finish()
     for copy in up_copies:
         copy.wait_recv()
-    for copy in up_copies + [c for unused, c in cut_z] + [c for c, unused, also in y_copies]:
+    for copy in sent + up_copies + [c for unused, c in cut_z] + [c for c, unused, also in y_copies]:
         copy.wait_send()
+
+
+def ranked(assigned, c, at):
+    total = 0
+    for j in range(c):
+        before = (assigned[j] < assigned[at]) | ((assigned[j] == assigned[at]) & (j < at))
+        total = total + jnp.where(before, 1, 0)
+    return total
+
+
+def depart_kernel(kv_count, sends_half, chips, count, groups, assigned, *refs):
+    ins, outs = refs[:9], refs[9:16]
+    cut_out, up_own, up_all = refs[16:19]
+    attended, up_at, inputs = refs[19:22]
+    fore, rest = refs[22:38], refs[38:]
+    sent = forward_kernel(
+        kv_count, sends_half, chips, count, *ins, *outs, attended, up_at, inputs, *fore
+    )
+    ranks = [ranked(assigned, count, c) for c in range(count)]
+
+    def order(at):
+        return sum(jnp.where(rank == at, c, 0) for c, rank in enumerate(ranks))
+
+    out_kernel(
+        chips, count, groups, order, sent, attended, inputs, up_at, cut_out, up_own, up_all, *rest
+    )
+
+
+def depart(assigned, rows_in, gain, table, upstream, matrices, kv_count):
+    chips, count, groups = axis_counts()
+    length, breadth = rows_in.shape
+    features, shared = matrices[0].shape[1], matrices[1].shape[1]
+    tiles = features // LANES
+    rows = breadth // (2 * count)
+    sends_half = rows % LANES == 0
+    shape = lambda *sizes: jax.ShapeDtypeStruct(sizes, BF16)
+    half = (count // CORES, length, rows) if sends_half else (16, LANES)
+    chunk, width = length // count, breadth // (CORES * chips)
+    share, parts = count // groups, len(parts_of(chunk))
+    full, own = (count, chunk, breadth), (count, chunk, width)
+    dma = pltpu.SemaphoreType.DMA
+    vmem = lambda sizes: pltpu.VMEM(sizes, BF16)
+    return pl.pallas_call(
+        partial(depart_kernel, kv_count, sends_half, chips, count, groups),
+        out_shape=(
+            shape(length, breadth), shape(*half), shape(length, features), shape(length, shared),
+            shape(length, shared), shape(length, features), shape(tiles, 2 * length, length),
+            shape(*full), shape(*own), shape(*full),
+        ),
+        in_specs=[SMEM_SPEC] + [HBM_SPEC] * 9,
+        out_specs=(VMEM_SPEC,) * 10,
+        scratch_shapes=[vmem(full), vmem(own), vmem(own), vmem(rows_in.shape), vmem(gain.shape)]
+        + [pltpu.VMEM(table.shape, F32)] * 3
+        + [vmem(m.shape) for m in matrices]
+        + [
+            pltpu.VMEM((2, 2 * length, length), F32), vmem((kv_count, 2 * length, LANES)),
+            vmem((kv_count, LANES, 2 * length)), vmem(half),
+            dma((9,)), dma((2, count)), dma((2, count)),
+            vmem((chips,) + own), vmem((chips,) + own), vmem((chips,) + own), vmem(own),
+            vmem((groups, share, chunk, width)), vmem((groups, share, chunk, width)), vmem(own),
+            dma((4, chips, parts * count)), dma((2, parts, count)),
+            dma((2, parts, groups, share)), dma((2, groups, share)),
+            dma((4, chips, parts * count)), dma((4, chips, share)),
+        ]
+        + [vmem((count, chunk // parts, width))] * parts,
+        compiler_params=params(1, 52),
+        name="depart",
+    )(
+        assigned, rows_in, gain, table, upstream.reshape(full), rows_in.reshape(full), *matrices
+    )
 
 
 def back_kernel(
     chips, client_count, group_count,
-    inverse, part, up_own,
+    assigned, part, up_own,
     grad_out,
     pair, relay, landed, y_from, z_from, own,
     tp_sems, y_sems, z_sems, wide_sems, *y_at,
@@ -311,39 +393,36 @@
         (turned(group, d, group_count) * share + i, rows) for rows in parts for d, i in steps
     ]
     sums = ShareSum(part, pair, relay, landed, [tp_sems.at[i] for i in range(4)], pieces, chips)
-    y_copies = []
-    for n, piece in enumerate(pieces):
-        p, (d, i) = n // len(steps), steps[n % len(steps)]
-        q, rows = piece
-        block = (sums.get(n, piece) + up_own[q, rows].astype(F32)).astype(BF16)
-        if d == 0:
-            y_at[p][group * share + i] = block
-        else:
-            y_from[d, i, rows] = block
-            y_copies.append(
-                (
-                    p,
+    widen = Widen(grad_out, [wide_sems.at[i] for i in range(4)], chips)
+    y_copies, z_copies, rounds = [], [], []
+
+    def widen_piece(q, rows):
+        widen.start(own.at[q, rows], len(rounds), (q, rows))
+        rounds.append((q, rows))
+
+    for p, rows in enumerate(parts):
+        arrivals = []
+        for at, (d, i) in enumerate(steps):
+            n = p * len(steps) + at
+            q = pieces[n][0]
+            block = (sums.get(n, (q, rows)) + up_own[q, rows].astype(F32)).astype(BF16)
+            if d == 0:
+                y_at[p][group * share + i] = block
+            else:
+                y_from[d, i, rows] = block
+                arrivals.append(
                     send(
                         y_from.at[d, i, rows], y_at[p].at[group * share + i],
                         y_sems.at[0, p, d, i], y_sems.at[1, p, d, i],
                         {"sdata": turned(group, d, group_count)},
-                    ),
+                    )
                 )
-            )
-    widen = Widen(grad_out, [wide_sems.at[i] for i in range(4)], chips)
-    z_copies, rounds = [], []
-
-    def widen_piece(q, rows):
-        widen.start(own.at[q, rows], len(rounds), (q, rows))
-        rounds.append((q, rows))
-
-    for p, rows in enumerate(parts):
-        for which, copy in y_copies:
-            if which == p:
-                copy.wait_recv()
+        for copy in arrivals:
+            copy.wait_recv()
+        y_copies += arrivals
         for k in range(1, client_count):
             to = turned(client, k, client_count)
-            z_from[k, rows] = y_at[p][inverse[to]]
+            z_from[k, rows] = y_at[p][ranked(assigned, client_count, to)]
             z_copies.append(
                 (
                     send(
@@ -354,7 +433,7 @@
                     rows,
                 )
             )
-        own[client, rows] = y_at[p][inverse[client]]
+        own[client, rows] = y_at[p][ranked(assigned, client_count, client)]
         widen_piece(client, rows)
     for copy, source, rows in z_copies:
         copy.wait_recv()
@@ -363,16 +442,17 @@
         widen.forward(n, piece)
     widen.finish()
     sums.finish()
-    for copy in [c for unused, c in y_copies] + [c for c, unused, also in z_copies]:
+    for copy in y_copies + [c for c, unused, also in z_copies]:
         copy.wait_send()
 
 
 def forward_kernel(
     kv_count, sends_half, chips, count,
-    rows_hbm, gain_ref, cosine_hbm, sine_hbm, upstream_hbm,
+    rows_hbm, gain_hbm, table_hbm, upstream_hbm, inputs_hbm,
     query_hbm, key_hbm, value_hbm, output_hbm,
-    normed_out, far_out, query_out, key_out, value_out, context_out, weights_out, attended_out, up_out,
-    rows_ref, cosine_ref, sine_ref,
+    normed_out, far_out, query_out, key_out, value_out, context_out, weights_out,
+    attended_out, up_out, inputs_out,
+    rows_ref, gain_ref, table_ref, cosine_ref, sine_ref,
     query_mat, key_mat, value_mat, output_mat, scores, key_pair, value_turn, theirs,
     sems, z_sems, y_sems,
 ):
@@ -381,18 +461,16 @@
     chip, core = place()
     chunk, width = up_out.shape[1:]
     moves = (
-        (rows_hbm, rows_ref), (cosine_hbm, cosine_ref), (sine_hbm, sine_ref),
+        (rows_hbm, rows_ref), (table_hbm, table_ref), (gain_hbm, gain_ref),
         (query_hbm, query_mat), (key_hbm, key_mat), (value_hbm, value_mat), (output_hbm, output_mat),
         (upstream_hbm.at[client, :, columns_of(chip, core, width)], up_out.at[client]),
+        (inputs_hbm.at[:, :, columns_of(chip, core, width)], inputs_out),
     )
     copies = []
     for i, (source, target) in enumerate(moves):
         copies.append(pltpu.make_async_copy(source, target, sems.at[i]))
         copies[-1].start()
-    greet(
-        [{"client": turned(client, k, count)} for k in range(1, count)]
-        + ([{"sdata": 1 - group}] if sends_half else [])
-    )
+    greet(partners(chips, count, lax.axis_size("sdata")))
     sent = []
     for k in range(1, count):
         to = turned(client, k, count)
@@ -403,6 +481,7 @@
             )
         )
     copies[0].wait()
+    copies[2].wait()
     rows_float = rows_ref[...].astype(F32)
     inv_rms = lax.rsqrt(jnp.mean(rows_float * rows_float, -1, keepdims=True) + 1e-05)
     normed_out[...] = (rows_float * inv_rms * gain_ref[...].astype(F32)).astype(BF16)
@@ -420,7 +499,7 @@
             )
     normed = normed_out[...]
     copies[1].wait()
-    copies[2].wait()
+    unfold(table_ref[...], cosine_ref, sine_ref)
 
     def turn(tile):
         return tile * cosine_ref[...] + swap_halves(tile) * sine_ref[...]
@@ -449,14 +528,14 @@
     step = LANES
     for t in range(tiles):
         g = t * kv_count // tiles
-        scores[...] = lax.dot_general(
+        scores[t % 2] = lax.dot_general(
             key_pair[g], query_out[:, t * LANES : (t + 1) * LANES], CROSSED, preferred_element_type=F32
         )
         for head in range(2):
             base = head * length
             for i in range(0, length, step):
                 deep = i + step
-                block = scores[base : base + deep, i : i + step] * HEAD_DIM ** (-0.5)
+                block = scores[t % 2, base : base + deep, i : i + step] * HEAD_DIM ** (-0.5)
                 key_ids = lax.broadcasted_iota(jnp.int32, (deep, step), 0)
                 query_ids = lax.broadcasted_iota(jnp.int32, (deep, step), 1) + i
                 block = jnp.where(key_ids <= query_ids, block, -1e30)
@@ -471,59 +550,27 @@
         context_out[:, t * LANES : (t + 1) * LANES] = turned_context.T.astype(BF16)
     copies[6].wait()
     context = context_out[...]
-    wide = next(b for b in (512, 256, 128) if attended_out.shape[1] % b == 0)
-    for at in range(0, attended_out.shape[1], wide):
-        attended_out[:, at : at + wide] = lax.dot_general(
-            context, output_mat[at : at + wide, :], CROSSED, preferred_element_type=F32
-        ).astype(BF16)
+    breadth = attended_out.shape[2]
+    wide = next(b for b in (512, 256, 128) if breadth % b == 0)
+    for at in range(0, breadth, wide):
+        attended_out[:, :, at : at + wide] = (
+            lax.dot_general(
+                context, output_mat[at : at + wide, :], CROSSED, preferred_element_type=F32
+            )
+            .reshape(count, chunk, wide)
+            .astype(BF16)
+        )
     copies[7].wait()
-    for copy in sent:
-        copy.wait_recv()
-    for copy in sent:
-        copy.wait_send()
-
-
-def forward(rows_in, gain, tables, upstream, matrices, kv_count):
-    chips, count, unused = axis_counts()
-    length, breadth = rows_in.shape
-    features, shared = matrices[0].shape[1], matrices[1].shape[1]
-    tiles = features // LANES
-    rows = breadth // (2 * count)
-    sends_half = rows % LANES == 0
-    shape = lambda *sizes: jax.ShapeDtypeStruct(sizes, BF16)
-    half = (count // CORES, length, rows) if sends_half else (16, LANES)
-    chunk, width = length // count, breadth // (CORES * chips)
-    dma = pltpu.SemaphoreType.DMA
-    return pl.pallas_call(
-        partial(forward_kernel, kv_count, sends_half, chips, count),
-        out_shape=(
-            shape(length, breadth), shape(*half), shape(length, features), shape(length, shared),
-            shape(length, shared), shape(length, features), shape(tiles, 2 * length, length),
-            shape(length, breadth), shape(count, chunk, width),
-        ),
-        in_specs=[ANY_SPEC, VMEM_SPEC] + [ANY_SPEC] * 7,
-        out_specs=(VMEM_SPEC,) * 9,
-        scratch_shapes=[pltpu.VMEM(rows_in.shape, BF16)]
-        + [pltpu.VMEM(table.shape, F32) for table in tables]
-        + [pltpu.VMEM(m.shape, BF16) for m in matrices]
-        + [
-            pltpu.VMEM((2 * length, length), F32),
-            pltpu.VMEM((kv_count, 2 * length, LANES), BF16),
-            pltpu.VMEM((kv_count, LANES, 2 * length), BF16),
-            pltpu.VMEM(half, BF16),
-            dma((8,)), dma((2, count)), dma((2, count)),
-        ],
-        compiler_params=params(4),
-        name="forward",
-    )(rows_in, gain, *tables, upstream.reshape(count, chunk, breadth), *matrices)
+    copies[8].wait()
+    return sent
 
 
 def server_kernel(
-    chips, shares,
-    rows_ref, own_ref, gain_ref, context_ref, half_ref, gate_hbm, up_hbm, down_hbm,
+    chips, groups, shares,
+    rows_ref, own_ref, part_ref, gain_hbm, context_ref, half_ref, gate_hbm, up_hbm, down_hbm,
     out_ref, far_context, far_normed,
     up_all, normed_ref, gate_value, up_value, gate_grad, up_grad, weighted_ref,
-    gate_ref, up_ref, down_ref, load_sems, wide_sems, far_sems, core_sems, local_sems,
+    gain_ref, gate_ref, up_ref, down_ref, load_sems, wide_sems, far_sems, core_sems, local_sems,
 ):
     length, breadth = rows_ref.shape
     hidden = gate_ref.shape[1]
@@ -535,6 +582,8 @@
         at = (spans[i], slice(None)) if which == 2 else (slice(None), spans[i])
         return pltpu.make_async_copy(source.at[at], target.at[at], load_sems.at[which, i])
 
+    gain_load = pltpu.make_async_copy(gain_hbm, gain_ref, load_sems.at[3, 0])
+    gain_load.start()
     for which in range(3):
         for i in range(len(spans)):
             loads(i, which).start()
@@ -547,8 +596,14 @@
     )
     widen = Widen(up_all, [wide_sems.at[i] for i in range(4)], chips)
     count = own_ref.shape[0]
-    for q in range(count):
-        widen.start(own_ref.at[q], q, (q, slice(None)))
+    share = count // groups
+    missing = [
+        (turned(group, d, groups) * share + i, slice(None))
+        for d in range(1, groups)
+        for i in range(share)
+    ]
+    for n, piece in enumerate(missing):
+        widen.start(own_ref.at[piece[0]], n, piece)
     others = [
         send(context_ref, far_context, far_sems.at[0], far_sems.at[1], {"sdata": 1 - group})
     ]
@@ -561,6 +616,7 @@
         kept.append(pltpu.make_async_copy(half_ref.at[n], far_normed.at[d], local_sems.at[n]))
         kept[-1].start()
     rows_float = rows_ref[...].astype(F32)
+    gain_load.wait()
     gain = gain_ref[...].astype(F32)
     inv_rms = lax.rsqrt(jnp.mean(rows_float * rows_float, -1, keepdims=True) + 1e-05)
     normed_ref[...] = (rows_float * inv_rms * gain).astype(BF16)
@@ -569,8 +625,10 @@
         gate_value[:, span] = jnp.dot(normed_ref[...], gate_ref[:, span], preferred_element_type=F32)
         loads(i, 1).wait()
         up_value[:, span] = jnp.dot(normed_ref[...], up_ref[:, span], preferred_element_type=F32)
-    for q in range(count):
-        widen.forward(q, (q, slice(None)))
+    for i in range(share):
+        up_all[group * share + i] = part_ref[group * share + i]
+    for n, piece in enumerate(missing):
+        widen.forward(n, piece)
     widen.finish()
     upstream = up_all[...].reshape(length, breadth)
     for i, span in enumerate(spans):
@@ -602,8 +660,8 @@
         copy.wait()
 
 
-def server_pull(rows_in, up_own, gain, context, half, gate_matrix, up_matrix, down_matrix):
-    chips, count, unused = axis_counts()
+def server_pull(rows_in, up_own, up_part, gain, context, half, gate_matrix, up_matrix, down_matrix):
+    chips, count, groups = axis_counts()
     length, breadth = rows_in.shape
     hidden = gate_matrix.shape[1]
     shares = half.shape[0] if half.ndim == 3 else 0
@@ -612,25 +670,25 @@
     vmem = lambda *sizes: pltpu.VMEM(sizes, BF16)
     wide = lambda *sizes: pltpu.VMEM(sizes, F32)
     return pl.pallas_call(
-        partial(server_kernel, chips, shares),
+        partial(server_kernel, chips, groups, shares),
         out_shape=(
             jax.ShapeDtypeStruct((length, breadth), BF16),
             jax.ShapeDtypeStruct(context.shape, BF16),
             jax.ShapeDtypeStruct(full, BF16),
         ),
-        in_specs=[VMEM_SPEC] * 5 + [ANY_SPEC] * 3,
+        in_specs=[VMEM_SPEC] * 3 + [HBM_SPEC] + [VMEM_SPEC] * 2 + [HBM_SPEC] * 3,
         out_specs=(VMEM_SPEC,) * 3,
         scratch_shapes=[
             vmem(count, length // count, breadth), vmem(length, breadth),
             wide(length, hidden), wide(length, hidden), vmem(length, hidden), vmem(length, hidden),
             wide(length, breadth),
-            vmem(breadth, hidden), vmem(breadth, hidden), vmem(hidden, breadth),
-            dma((3, hidden // LANES)), dma((4, chips, count)), dma((2,)), dma((2, count)),
+            vmem(1, breadth), vmem(breadth, hidden), vmem(breadth, hidden), vmem(hidden, breadth),
+            dma((4, hidden // LANES)), dma((4, chips, count)), dma((2,)), dma((2, count)),
             dma((count,)),
         ],
-        compiler_params=params(5),
+        compiler_params=params(5, 50),
         name="server_pull",
-    )(rows_in, up_own, gain[None], context, half, gate_matrix, up_matrix, down_matrix)
+    )(rows_in, up_own, up_part, gain[None], context, half, gate_matrix, up_matrix, down_matrix)
 
 
 class Chain:
@@ -661,12 +719,17 @@
 
     def open(self, d, way):
         j = self.count - 1 - d if way == 0 else d
-        if j < self.count - 1:
-            end = 0 if way == 0 else self.count - 1
+        end = 0 if way == 0 else self.count - 1
+        if abs(d - end) > 1:
 
             @pl.when(self.at == end)
             def _():
                 self.copy(way, j, d).start()
+
+    def add(self, way, j, d):
+        landing = self.forth if way == 0 else self.back
+        self.copy(way, j, d).wait_recv()
+        self.own[d] = (self.own[d].astype(F32) + landing[j].astype(F32)).astype(BF16)
 
     def relay(self):
         near = self.at < self.count // 2
@@ -675,13 +738,31 @@
         turns += [(leg, self.at >= 0) for leg in legs if leg[0] == 1]
         turns += [(leg, jnp.logical_not(near)) for leg in legs if leg[0] == 0]
         for (way, j, d, end, beyond), now in turns:
-            landing = self.forth if way == 0 else self.back
-
-            @pl.when(now & beyond & (self.at != end))
-            def _(way=way, j=j, d=d, landing=landing):
-                self.copy(way, j, d).wait_recv()
-                self.own[d] = (self.own[d].astype(F32) + landing[j].astype(F32)).astype(BF16)
+            if abs(d - end) < 3:
+                continue
+            far = self.at < d - 1 if way == 0 else self.at > d + 1
+
+            @pl.when(now & far & (self.at != end))
+            def _(way=way, j=j, d=d):
+                self.add(way, j, d)
                 self.copy(way, j, d).start()
+
+    def close(self, ends):
+        last = self.count - 1
+        for way, end, d in ((0, 0, self.at + 1), (1, last, self.at - 1)):
+            j = last - d if way == 0 else d
+            if ends:
+
+                @pl.when(self.at == end)
+                def _(way=way, j=j, d=d):
+                    self.copy(way, j, d).start()
+
+            else:
+
+                @pl.when((self.at > 0) & (self.at < last))
+                def _(way=way, j=j, d=d):
+                    self.add(way, j, d)
+                    self.copy(way, j, d).start()
 
     def total(self, out_refs):
         last = self.count - 1
@@ -712,7 +793,7 @@
 def learn_kernel(
     kv_count, count, aligned,
     cut_ref, output_ref, query_ref, key_ref, value_ref, context_ref, weights_ref, normed_ref,
-    far_normed, far_context, cosine_ref, sine_ref, *refs,
+    far_normed, far_context, table_ref, *refs,
 ):
     if not aligned:
         near_cut, give_cut, near_normed, refs = refs[0], refs[1], refs[2], refs[3:]
@@ -722,6 +803,7 @@
         far_cut, far_query, far_shared,
         output_own, output_forth, output_back, shared_own, shared_forth, shared_back,
         query_own, query_forth, query_back,
+        cosine_ref, sine_ref,
         cut_sems, core_sems, give_sems, output_sems, shared_sems, query_sems,
     ) = refs[4:]
     length = cut_ref.shape[0]
@@ -779,6 +861,8 @@
         key_turn[g, :HEAD_DIM, :length] = mine
         key_turn[g, HEAD_DIM:, length:] = mine
 
+    unfold(table_ref[...], cosine_ref, sine_ref)
+
     def unturn(tile):
         return tile * cosine_ref[...] - swap_halves(tile) * sine_ref[...]
 
@@ -788,23 +872,23 @@
     for t in range(tiles):
         g = t * kv_count // tiles
         span = slice(t * LANES, (t + 1) * LANES)
-        weight_grad[...] = lax.dot_general(
+        weight_grad[t % 2] = lax.dot_general(
             value_pair[g], pulled[:, span], CROSSED, preferred_element_type=F32
         )
         for head in range(2):
             base = head * length
             for i in range(0, length, LANES):
                 deep = i + LANES
-                grad = weight_grad[base : base + deep, i : i + LANES].astype(BF16).astype(F32)
+                grad = weight_grad[t % 2, base : base + deep, i : i + LANES].astype(BF16).astype(F32)
                 weight = weights_ref[t, base : base + deep, i : i + LANES].astype(F32)
                 both = grad * weight
                 drift = jnp.sum(both, 0, keepdims=True)
-                score_grad[base : base + deep, i : i + LANES] = (
+                score_grad[t % 2, base : base + deep, i : i + LANES] = (
                     (both - weight * drift) * HEAD_DIM ** (-0.5)
                 ).astype(BF16)
-        back_query = jnp.dot(key_turn[g], score_grad[...], preferred_element_type=F32)
+        back_query = jnp.dot(key_turn[g], score_grad[t % 2], preferred_element_type=F32)
         query_grad[:, span] = unturn(back_query.T.astype(BF16).astype(F32)).astype(BF16)
-        back_key = jnp.dot(score_grad[...], query_ref[:, span], preferred_element_type=F32)
+        back_key = jnp.dot(score_grad[t % 2], query_ref[:, span], preferred_element_type=F32)
         back_value = jnp.dot(weights_ref[t], pulled[:, span], preferred_element_type=F32)
         first = key_sum[g] is None
         key_sum[g] = back_key if first else key_sum[g] + back_key
@@ -870,8 +954,12 @@
     chains[0].relay()
     gifts[1].wait_recv()
     spread(chains[2], query_grad, far_query)
-    chains[1].relay()
-    chains[2].relay()
+    for chain in chains:
+        chain.close(True)
+    chains[0].close(False)
+    for chain in chains[1:]:
+        chain.relay()
+        chain.close(False)
     chains[0].total([output_out])
     chains[1].total([key_out, value_out])
     chains[2].total([query_out])
@@ -884,7 +972,7 @@
         chain.finish()
 
 
-def learn(cut_grad, output_matrix, saved, normed, far_normed, far_context, tables, kv_count):
+def learn(cut_grad, output_matrix, saved, normed, far_normed, far_context, table, kv_count):
     unused, count, group_count = axis_counts()
     queries, keys, values, context, weights = saved
     length, breadth = cut_grad.shape
@@ -895,7 +983,7 @@
     shape = lambda *sizes: jax.ShapeDtypeStruct(sizes, BF16)
     vmem = lambda *sizes: pltpu.VMEM(sizes, BF16)
     operands = [cut_grad, output_matrix, queries, keys, values, context, weights, normed]
-    operands += [far_normed, far_context, *tables]
+    operands += [far_normed, far_context, table]
     if not aligned:
         group = lax.axis_index("sdata")
         operands += [
@@ -914,16 +1002,41 @@
         out_specs=(VMEM_SPEC,) * 4,
         scratch_shapes=[
             vmem(length, features), vmem(16, LANES), vmem(kv_count, LANES, 2 * length),
-            vmem(kv_count, 2 * length, LANES), pltpu.VMEM((2 * length, length), F32),
-            vmem(2 * length, length), vmem(length, features), vmem(length, 2 * LANES),
+            vmem(kv_count, 2 * length, LANES), pltpu.VMEM((2, 2 * length, length), F32),
+            vmem(2, 2 * length, length), vmem(length, features), vmem(length, 2 * LANES),
             vmem(count, length, rows), vmem(length, features), vmem(length, 2 * LANES),
         ]
         + chain(features) + chain(2 * LANES) + chain(features)
+        + [pltpu.VMEM(table.shape, F32)] * 2
         + [dma((2, count // CORES)), dma((2, count // CORES)), dma((2, 2))]
         + [dma((4, count - 1))] * 3,
-        compiler_params=params(3),
+        compiler_params=params(3, 28),
         name="learn",
     )(*operands)
+
+
+def emit_kernel(count, *refs):
+    sems = refs[2 * count]
+    copies = [
+        pltpu.make_async_copy(refs[i], refs[count + i], sems.at[i]) for i in range(count)
+    ]
+    for copy in copies:
+        copy.start()
+    for copy in copies:
+        copy.wait()
+
+
+def emit(*arrays):
+    count = len(arrays)
+    return pl.pallas_call(
+        partial(emit_kernel, count),
+        out_shape=tuple(jax.ShapeDtypeStruct(a.shape, a.dtype) for a in arrays),
+        in_specs=[VMEM_SPEC] * count,
+        out_specs=(HBM_SPEC,) * count,
+        scratch_shapes=[pltpu.SemaphoreType.DMA((count,))],
+        compiler_params=pltpu.CompilerParams(vmem_limit_bytes=4 * 2**20),
+        name="emit",
+    )(*arrays)
 
 
 def half_of(array, count, side):
@@ -936,50 +1049,20 @@
     return lax.ppermute(array, "sdata", [(g, (g + 1) % count) for g in range(count)])
 
 
-def tables_of(length):
+def table_of(length):
     halfway = HEAD_DIM // 2
-    lanes = jnp.arange(LANES) % HEAD_DIM
-    frequencies = jnp.exp(-math.log(500000.0) * (2.0 / HEAD_DIM) * (lanes % halfway).astype(F32))
-    angles = jnp.arange(length).astype(F32)[:, None] * frequencies[None, :]
-    sign = jnp.where(lanes < halfway, -1.0, 1.0)
-    return jnp.cos(angles), jnp.sin(angles) * sign[None, :]
+    lanes = np.arange(HEAD_DIM)
+    frequencies = np.exp(-math.log(500000.0) * (2.0 / HEAD_DIM) * (lanes % halfway))
+    angles = np.arange(length)[:, None] * frequencies[None, :]
+    sign = np.where(lanes < halfway, -1.0, 1.0)
+    return jnp.asarray(np.concatenate([np.cos(angles), np.sin(angles) * sign], 1), F32)
 
 
 def widened(matrix):
     return jnp.pad(matrix, ((0, 0), (0, LANES - matrix.shape[1])))
 
 
-def relay_out(order, attended, rows_in, up_at):
-    chips, client_count, group_count = axis_counts()
-    length, breadth = rows_in.shape
-    chunk, width = length // client_count, breadth // (CORES * chips)
-    share = client_count // group_count
-    parts = len(parts_of(chunk))
-    full = (client_count, chunk, breadth)
-    own = (client_count, chunk, width)
-    dma = pltpu.SemaphoreType.DMA
-    vmem = lambda shape: pltpu.VMEM(shape, BF16)
-    cut, up_own = pl.pallas_call(
-        partial(out_kernel, chips, client_count, group_count),
-        out_shape=(jax.ShapeDtypeStruct(full, BF16), jax.ShapeDtypeStruct(own, BF16)),
-        in_specs=[SMEM_SPEC, VMEM_SPEC, VMEM_SPEC, VMEM_SPEC],
-        out_specs=(VMEM_SPEC,) * 2,
-        scratch_shapes=[
-            vmem((chips,) + own), vmem((chips,) + own), vmem((chips,) + own), vmem(own),
-            vmem((group_count, share, chunk, width)), vmem((group_count, share, chunk, width)),
-            vmem(own),
-            dma((4, chips, parts * client_count)), dma((2, parts, client_count)),
-            dma((2, parts, group_count, share)), dma((2, group_count, share)),
-            dma((4, chips, parts * client_count)),
-        ]
-        + [vmem((client_count, chunk // parts, width))] * parts,
-        compiler_params=params(1),
-        name="relay_out",
-    )(order, attended.reshape(full), rows_in.reshape(full), up_at)
-    return cut.reshape(length, breadth), up_own
-
-
-def relay_back(inverse, pulled, up_own):
+def relay_back(assigned, pulled, up_own):
     chips, client_count, group_count = axis_counts()
     length, breadth = pulled.shape
     chunk, width = length // client_count, breadth // (CORES * chips)
@@ -1001,9 +1084,9 @@
             dma((2, parts, client_count)), dma((4, chips, parts * client_count)),
         ]
         + [vmem((client_count, chunk // parts, width))] * parts,
-        compiler_params=params(2),
+        compiler_params=params(2, 14),
         name="relay_back",
-    )(inverse, pulled.reshape(full), up_own)
+    )(assigned, pulled.reshape(full), up_own)
     return grad.reshape(length, breadth)
 
 
@@ -1024,29 +1107,26 @@
     client_count = lax.axis_size("client")
     shared = key_weight.shape[2]
     kv_count = shared // HEAD_DIM
-    tables = tables_of(client_input.shape[0])
+    table = table_of(client_input.shape[0])
     matrices = [
         query_weight[0], widened(key_weight[0]), widened(client_value_weight[0]), output_weight[0]
     ]
-    normed, half, *saved, attended, up_at = forward(
-        client_input, client_gain, tables, upstream, matrices, kv_count
+    normed, half, *saved, cut_rows, up_own, up_part = depart(
+        assignment, client_input, client_gain, table, upstream, matrices, kv_count
     )
-    ids = jnp.arange(client_count).astype(jnp.int32)
-    ahead = (assignment[None, :] < assignment[:, None]) | (
-        (assignment[None, :] == assignment[:, None]) & (ids[None, :] < ids[:, None])
-    )
-    inverse = jnp.sum(ahead.astype(jnp.int32), 1)
-    group_order = jnp.sum(jnp.where(inverse[None, :] == ids[:, None], ids[None, :], 0), 1)
-    cut_rows, up_own = relay_out(group_order, attended, client_input, up_at)
+    cut_rows = cut_rows.reshape(client_input.shape)
     pulled, far_context, far_normed = server_pull(
-        cut_rows, up_own, server_gain[0], saved[3], half,
+        cut_rows, up_own, up_part, server_gain[0], saved[3], half,
         server_gate[0], server_up[0], server_down[0],
     )
     if half.ndim == 2:
         far_normed = across_groups(half_of(normed, client_count, 1 - lax.axis_index("sdata")))
-    arriving_grad = relay_back(inverse, pulled, up_own)
-    query_update, key_update, value_update, output_update = learn(
-        arriving_grad, output_weight[0], saved, normed, far_normed, far_context, tables, kv_count
+    arriving_grad = relay_back(assignment, pulled, up_own)
+    query_update, key_update, value_update, output_update = emit(
+        *learn(
+            arriving_grad, output_weight[0], saved, normed, far_normed, far_context, table,
+            kv_count,
+        )
     )
     return (query_update, key_update[:, :shared], value_update[:, :shared], output_update)
 

time: 170 us -> 144 us (0.85)
  Pallas kernels: 159 us -> 140 us
  local copies, waits for them, and re-layouts: 8 us -> 2.31 us
  other arithmetic: 1.81 us -> 0 us
    pallas_call x1, Pallas kernels: 65.8 us -> 54.4 us  [learn(): pl.pallas_call(partial(learn_kernel, kv_count, count, aligned), out_shape...]
    unnamed x18, local copies, waits for them, and re-layouts: 8 us -> 2.31 us
    pallas_call x3, Pallas kernels: 63.8 us -> 59.2 us  [the longest x1 40.9 us: depart(): pl.pallas_call(partial(depart_kernel, kv_count, sends_half, chips, count,...]
    pallas_call x1, Pallas kernels: 29.3 us -> 26.5 us  [relay_back(): pl.pallas_call(partial(back_kernel, chips, client_count, group_count), ou...]
where the time goes in v3:
time: 144 us; the launch traced here: 143 us
  Pallas kernels  140 us (97%)
  local copies, waits for them, and re-layouts  2.31 us (2%)
    pallas_call x1, Pallas kernels, learn(): pl.pallas_call(partial(learn_kernel, kv_count, count, aligned), out_shape...  54.4 us
    pallas_call x1, Pallas kernels, depart(): pl.pallas_call(partial(depart_kernel, kv_count, sends_half, chips, count,...  40.9 us
    pallas_call x1, Pallas kernels, relay_back(): pl.pallas_call(partial(back_kernel, chips, client_count, group_count), ou...  26.5 us
    pallas_call x1, Pallas kernels, server_pull(): pl.pallas_call(partial(server_kernel, chips, groups, shares), out_shape=(...  17.4 us

profile of v3, /device:TPU:8, one launch (start us, length us, event | category | flops | bytes accessed | tf_op | source)
XLA Modules:
  0.0 143.3 jit_solution(1150380932643486076)
XLA Ops:
  0.6 0.0 copy-start.3
  0.6 0.9 copy-done.3
  1.6 0.0 copy-start.6
  1.6 0.7 copy-done.6
  2.3 0.0 copy-start.7
  2.3 0.7 copy-done.7
  2.9 0.0 copy-start.5
  2.9 40.9 %depart.1 = (bf16[384,2048]{1,0:T(8,128)(2,1)}, bf16[2,384,256]{2,1,0:T(8,128)(2,1)S(1)}, bf16[384,512]{1,0:T(8,128)(2,1)S(1)}, bf16[384,128]{1,0:T(8,128)(2,1)S...) custom-call(s32[4]{0:T(128)S(1)} %copy-done.7, ...), custom_call_target="tpu_custom_call" | custom-call | tf_op jit(solution)/shard_map/depart/pallas_call | solution.py:350
  43.8 0.0 copy-done.5
  43.8 0.0 copy-start.8
  43.8 0.0 copy-start.1
  43.8 0.0 copy-start.2
  43.9 17.4 %server_pull.1 = (bf16[384,2048]{1,0:T(8,128)(2,1)S(1)}, bf16[384,512]{1,0:T(8,128)(2,1)S(1)}, bf16[4,384,256]{2,1,0:T(8,128)(2,1)S(1)}) custom-call(bf16[384,2048]{1,0:T(8,128)(2,1)} %bitcast.22, bf16[4,96,512]{2,1,0:T(8,128)(2,1)S(1)} %get-tuple-element.22.own_ref.up_own, bf16[4,96,2048]{2,1,0:T(8,128)(2,1)} %get-tuple-element.23.part_ref, ...), custom_call_target="tpu_custom_call" | custom-call | tf_op jit(solution)/shard_map/server_pull/pallas_call | solution.py:672
  61.3 0.0 copy-done.8
  61.3 0.0 copy-start
  61.3 0.0 copy-start.4
  61.3 26.5 %relay_back.1 = bf16[4,96,2048]{2,1,0:T(8,128)(2,1)S(1)} custom-call(s32[4]{0:T(128)S(1)} %copy-done.8, bf16[4,96,2048]{2,1,0:T(8,128)(2,1)S(1)} %bitcast.15, bf16[4,96,512]{2,1,0:T(8,128)(2,1)S(1)} %get-tuple-element.22.own_ref.up_own), custom_call_target="tpu_custom_call" | custom-call | tf_op jit(solution)/shard_map/relay_back/pallas_call | solution.py:1075
  87.8 0.0 copy-done.1
  87.9 0.0 copy-done.2
  87.9 0.0 copy-done
  87.9 0.0 copy-done.4
  87.9 54.4 %learn.1 = (bf16[256,512]{1,0:T(8,128)(2,1)S(1)}, bf16[256,128]{1,0:T(8,128)(2,1)S(1)}, bf16[256,128]{1,0:T(8,128)(2,1)S(1)}, bf16[256,512]{1,0:T(8,128)(2,1)S(1)}) custom-call(bf16[384,2048]{1,0:T(8,128)(2,1)S(1)} %bitcast.14, bf16[2048,512]{1,0:T(8,128)(2,1)S(1)} %bitcast.13, bf16[384,512]{1,0:T(8,128)(2,1)S(1)} %get-tuple-element.27.query_ref, ...), custom_call_target="tpu_custom_call" | custom-call | tf_op jit(solution)/shard_map/learn/pallas_call | solution.py:996
  142.3 0.9 emit.1
Async XLA Ops:
  0.6 0.9 copy-start.3
  1.6 0.7 copy-start.6
  2.3 0.7 copy-start.7
  2.9 40.9 %copy-start.5 = (bf16[1,2048]{1,0:T(2,128)(2,1)S(1)}, bf16[1,2048]{1,0:T(2,128)(2,1)}, u32[]{:S(2)}) copy-start(bf16[1,2048]{1,0:T(2,128)(2,1)} %gain_hbm.1) | copy-start | bytes 12292
  43.8 17.4 %copy-start.8 = (s32[4]{0:T(128)S(1)}, s32[4]{0:T(128)}, u32[]{:S(2)}) copy-start(s32[4]{0:T(128)} %assigned.3) | copy-start | bytes 52
  43.8 44.0 %copy-start.1 = (bf16[4,768,384]{2,1,0:T(8,128)(2,1)S(1)}, bf16[4,768,384]{2,1,0:T(8,128)(2,1)}, u32[]{:S(2)}) copy-start(bf16[4,768,384]{2,1,0:T(8,128)(2,1)} %get-tuple-element.30.weights_ref) | copy-start | bytes 7077892
  43.8 44.0 %copy-start.2 = (bf16[384,2048]{1,0:T(8,128)(2,1)S(1)}, bf16[384,2048]{1,0:T(8,128)(2,1)}, u32[]{:S(2)}) copy-start(bf16[384,2048]{1,0:T(8,128)(2,1)} %get-tuple-element.31.normed_ref) | copy-start | bytes 4718596
  61.3 26.6 %copy-start = (bf16[1,2048,512]{2,1,0:T(8,128)(2,1)S(1)}, bf16[1,2048,512]{2,1,0:T(8,128)(2,1)}, u32[]{:S(2)}) copy-start(bf16[1,2048,512]{2,1,0:T(8,128)(2,1)} %param.18) | copy-start | bytes 6291460
  61.3 26.6 %copy-start.4 = (f32[384,128]{1,0:T(8,128)S(1)}, f32[384,128]{1,0:T(8,128)}, u32[]{:S(2)}) copy-start(f32[384,128]{1,0:T(8,128)} %constant.1.clone.refs_2_.table_ref) | copy-start | bytes 589828

commit v4 on v3

--- a/solution.py
+++ b/solution.py
@@ -113,31 +113,45 @@
         self.chip, self.core = place()
         self.pair_copies = {}
         self.chip_copies = {}
-        for n, (q, rows) in enumerate(pieces):
-            for k in list(range(1, chips)) + [0]:
-                to = turned(self.chip, k, chips)
-                self.pair_copies[k, n] = send(
-                    part.at[q, rows, columns_of(to, 1 - self.core, self.width)],
-                    pair.at[k, q, rows],
-                    self.pair_send.at[k, n],
-                    self.pair_recv.at[k, n],
-                    {"tensor": self.chip * CORES + 1 - self.core},
-                )
-        for n, (q, rows) in enumerate(pieces):
-            for k in range(1, chips):
-                to = turned(self.chip, k, chips)
-                self.pair_copies[k, n].wait_recv()
-                relay[k, q, rows] = (
-                    part[q, rows, columns_of(to, self.core, self.width)].astype(F32)
-                    + pair[k, q, rows].astype(F32)
-                ).astype(BF16)
-                self.chip_copies[k, n] = send(
-                    relay.at[k, q, rows],
-                    landed.at[k, q, rows],
-                    self.chip_send.at[k, n],
-                    self.chip_recv.at[k, n],
-                    {"tensor": to * CORES + self.core},
-                )
+        self.pieces = pieces
+
+    def give(self, k):
+        to = turned(self.chip, k, self.chips)
+        for n, (q, rows) in enumerate(self.pieces):
+            self.pair_copies[k, n] = send(
+                self.part.at[q, rows, columns_of(to, 1 - self.core, self.width)],
+                self.pair.at[k, q, rows],
+                self.pair_send.at[k, n],
+                self.pair_recv.at[k, n],
+                {"tensor": self.chip * CORES + 1 - self.core},
+            )
+
+    def hand_on(self, k):
+        to = turned(self.chip, k, self.chips)
+        for n, (q, rows) in enumerate(self.pieces):
+            self.pair_copies[k, n].wait_recv()
+            self.relay[k, q, rows] = (
+                self.part[q, rows, columns_of(to, self.core, self.width)].astype(F32)
+                + self.pair[k, q, rows].astype(F32)
+            ).astype(BF16)
+            self.chip_copies[k, n] = send(
+                self.relay.at[k, q, rows],
+                self.landed.at[k, q, rows],
+                self.chip_send.at[k, n],
+                self.chip_recv.at[k, n],
+                {"tensor": to * CORES + self.core},
+            )
+
+    def fill(self, make):
+        for k in range(1, self.chips):
+            make(turned(self.chip, k, self.chips), 1 - self.core)
+            self.give(k)
+        for k in range(1, self.chips):
+            make(turned(self.chip, k, self.chips), self.core)
+            self.hand_on(k)
+        make(self.chip, 1 - self.core)
+        self.give(0)
+        make(self.chip, self.core)
 
     def get(self, n, piece):
         q, rows = piece
@@ -214,7 +228,7 @@
 
 def out_kernel(
     chips, client_count, group_count,
-    order, sent, part, inputs, up_at,
+    order, sent, copies, project, part, inputs, up_at,
     cut_out, up_own, up_all,
     pair, relay, landed, cut_from, up_put, cut_put, cut_own,
     tp_sems, z_sems, y_sems, up_sems, wide_sems, kept_sems, *cut_at,
@@ -226,6 +240,9 @@
     steps = list(range(1, client_count)) + [0]
     pieces = [(turned(client, k, client_count), rows) for rows in parts for k in steps]
     sums = ShareSum(part, pair, relay, landed, [tp_sems.at[i] for i in range(4)], pieces, chips)
+    sums.fill(project)
+    for copy in copies:
+        copy.wait()
     for copy in sent:
         copy.wait_recv()
     up_copies = []
@@ -320,7 +337,7 @@
     cut_out, up_own, up_all = refs[16:19]
     attended, up_at, inputs = refs[19:22]
     fore, rest = refs[22:38], refs[38:]
-    sent = forward_kernel(
+    sent, copies, project = forward_kernel(
         kv_count, sends_half, chips, count, *ins, *outs, attended, up_at, inputs, *fore
     )
     ranks = [ranked(assigned, count, c) for c in range(count)]
@@ -329,7 +346,7 @@
         return sum(jnp.where(rank == at, c, 0) for c, rank in enumerate(ranks))
 
     out_kernel(
-        chips, count, groups, order, sent, attended, inputs, up_at, cut_out, up_own, up_all, *rest
+        chips, count, groups, order, sent, copies, project, attended, inputs, up_at, cut_out, up_own, up_all, *rest
     )
 
 
@@ -378,7 +395,7 @@
 
 
 def back_kernel(
-    chips, client_count, group_count,
+    chips, client_count, group_count, pull,
     assigned, part, up_own,
     grad_out,
     pair, relay, landed, y_from, z_from, own,
@@ -386,13 +403,13 @@
 ):
     client, group = lax.axis_index("client"), lax.axis_index("sdata")
     share = client_count // group_count
-    greet(partners(chips, client_count, group_count))
     parts = parts_of(part.shape[1])
     steps = [(d, i) for d in list(range(1, group_count)) + [0] for i in range(share)]
     pieces = [
         (turned(group, d, group_count) * share + i, rows) for rows in parts for d, i in steps
     ]
     sums = ShareSum(part, pair, relay, landed, [tp_sems.at[i] for i in range(4)], pieces, chips)
+    sums.fill(pull)
     widen = Widen(grad_out, [wide_sems.at[i] for i in range(4)], chips)
     y_copies, z_copies, rounds = [], [], []
 
@@ -550,27 +567,24 @@
         context_out[:, t * LANES : (t + 1) * LANES] = turned_context.T.astype(BF16)
     copies[6].wait()
     context = context_out[...]
-    breadth = attended_out.shape[2]
-    wide = next(b for b in (512, 256, 128) if breadth % b == 0)
-    for at in range(0, breadth, wide):
-        attended_out[:, :, at : at + wide] = (
-            lax.dot_general(
-                context, output_mat[at : at + wide, :], CROSSED, preferred_element_type=F32
-            )
-            .reshape(count, chunk, wide)
+
+    def project(to, side):
+        cols = columns_of(to, side, width)
+        attended_out[:, :, cols] = (
+            lax.dot_general(context, output_mat[cols, :], CROSSED, preferred_element_type=F32)
+            .reshape(count, chunk, width)
             .astype(BF16)
         )
-    copies[7].wait()
-    copies[8].wait()
-    return sent
+
+    return sent, copies[7:], project
 
 
 def server_kernel(
     chips, groups, shares,
     rows_ref, own_ref, part_ref, gain_hbm, context_ref, half_ref, gate_hbm, up_hbm, down_hbm,
-    out_ref, far_context, far_normed,
-    up_all, normed_ref, gate_value, up_value, gate_grad, up_grad, weighted_ref,
-    gain_ref, gate_ref, up_ref, down_ref, load_sems, wide_sems, far_sems, core_sems, local_sems,
+    assigned, grad_out, far_context, far_normed,
+    up_all, normed_ref, gate_value, up_value, gate_grad, up_grad, pulled_ref,
+    gain_ref, gate_ref, up_ref, down_ref, load_sems, wide_sems, far_sems, core_sems, local_sems, *rest,
 ):
     length, breadth = rows_ref.shape
     hidden = gate_ref.shape[1]
@@ -590,10 +604,7 @@
     group = lax.axis_index("sdata")
     chip, core = place()
     sibling = {"tensor": chip * CORES + 1 - core}
-    greet(
-        [sibling, {"sdata": 1 - group}]
-        + [{"tensor": turned(chip, k, chips) * CORES + core} for k in range(1, chips)]
-    )
+    greet(partners(chips, lax.axis_size("client"), groups))
     widen = Widen(up_all, [wide_sems.at[i] for i in range(4)], chips)
     count = own_ref.shape[0]
     share = count // groups
@@ -631,27 +642,38 @@
         widen.forward(n, piece)
     widen.finish()
     upstream = up_all[...].reshape(length, breadth)
+    lean = jnp.zeros((length, 1), F32)
     for i, span in enumerate(spans):
         loads(i, 2).wait()
         pulled = lax.dot_general(upstream, down_ref[span], CROSSED, preferred_element_type=F32)
         gate, up = gate_value[:, span], up_value[:, span]
         sigmoid_gate = jax.nn.sigmoid(gate)
-        gate_grad[:, span] = (
+        gate_part = (
             pulled * up * sigmoid_gate * (1.0 + gate * (1.0 - sigmoid_gate))
         ).astype(BF16)
-        up_grad[:, span] = (pulled * gate * sigmoid_gate).astype(BF16)
-    step = next(b for b in (256, 128, breadth) if breadth % b == 0)
-    lean = jnp.zeros((length, 1), F32)
-    for at in range(0, breadth, step):
-        span = slice(at, at + step)
-        weighted = (
-            lax.dot_general(gate_grad[...], gate_ref[span], CROSSED, preferred_element_type=F32)
-            + lax.dot_general(up_grad[...], up_ref[span], CROSSED, preferred_element_type=F32)
-        ) * gain_ref[:, span].astype(F32)
-        weighted_ref[:, span] = weighted
-        lean = lean + jnp.sum(weighted * rows_ref[:, span].astype(F32), -1, keepdims=True)
-    pull = inv_rms**3 * (lean * (1.0 / breadth))
-    out_ref[...] = (inv_rms * weighted_ref[...] - rows_ref[...].astype(F32) * pull).astype(BF16)
+        up_part = (pulled * gate * sigmoid_gate).astype(BF16)
+        gate_grad[:, span], up_grad[:, span] = gate_part, up_part
+        lean = lean + jnp.sum(
+            gate_part.astype(F32) * gate + up_part.astype(F32) * up, -1, keepdims=True
+        )
+    lean = inv_rms**2 * (lean * (1.0 / breadth))
+    width = own_ref.shape[2]
+    chunk = own_ref.shape[1]
+    step = min(256, width)
+
+    def pull(to, side):
+        for at in range(0, width, step):
+            span = pl.ds(pl.multiple_of((to * CORES + side) * width + at, step), step)
+            weighted = (
+                lax.dot_general(gate_grad[...], gate_ref[span, :], CROSSED, preferred_element_type=F32)
+                + lax.dot_general(up_grad[...], up_ref[span, :], CROSSED, preferred_element_type=F32)
+            ) * gain_ref[:, span].astype(F32)
+            mine = inv_rms * weighted - rows_ref[:, span].astype(F32) * lean
+            pulled_ref[:, :, span] = mine.reshape(count, chunk, step).astype(BF16)
+
+    back_kernel(
+        chips, lax.axis_size("client"), groups, pull, assigned, pulled_ref, own_ref, grad_out, *rest
+    )
     for copy in others:
         copy.wait_recv()
     for copy in others:
@@ -660,35 +682,46 @@
         copy.wait()
 
 
-def server_pull(rows_in, up_own, up_part, gain, context, half, gate_matrix, up_matrix, down_matrix):
+def serve(assigned, rows_in, up_own, up_part, gain, context, half, gate_matrix, up_matrix, down_matrix):
     chips, count, groups = axis_counts()
     length, breadth = rows_in.shape
     hidden = gate_matrix.shape[1]
     shares = half.shape[0] if half.ndim == 3 else 0
-    full = (count,) + half.shape[1:] if shares else half.shape
+    far = (count,) + half.shape[1:] if shares else half.shape
+    chunk, width = length // count, breadth // (CORES * chips)
+    share, parts = count // groups, len(parts_of(chunk))
+    full, own = (count, chunk, breadth), (count, chunk, width)
     dma = pltpu.SemaphoreType.DMA
     vmem = lambda *sizes: pltpu.VMEM(sizes, BF16)
     wide = lambda *sizes: pltpu.VMEM(sizes, F32)
     return pl.pallas_call(
         partial(server_kernel, chips, groups, shares),
         out_shape=(
-            jax.ShapeDtypeStruct((length, breadth), BF16),
+            jax.ShapeDtypeStruct(full, BF16),
             jax.ShapeDtypeStruct(context.shape, BF16),
-            jax.ShapeDtypeStruct(full, BF16),
+            jax.ShapeDtypeStruct(far, BF16),
         ),
-        in_specs=[VMEM_SPEC] * 3 + [HBM_SPEC] + [VMEM_SPEC] * 2 + [HBM_SPEC] * 3,
+        in_specs=[VMEM_SPEC] * 3 + [HBM_SPEC] + [VMEM_SPEC] * 2 + [HBM_SPEC] * 3 + [SMEM_SPEC],
         out_specs=(VMEM_SPEC,) * 3,
         scratch_shapes=[
-            vmem(count, length // count, breadth), vmem(length, breadth),
+            vmem(*full), vmem(length, breadth),
             wide(length, hidden), wide(length, hidden), vmem(length, hidden), vmem(length, hidden),
-            wide(length, breadth),
+            vmem(*full),
             vmem(1, breadth), vmem(breadth, hidden), vmem(breadth, hidden), vmem(hidden, breadth),
             dma((4, hidden // LANES)), dma((4, chips, count)), dma((2,)), dma((2, count)),
             dma((count,)),
-        ],
+            vmem(chips, *own), vmem(chips, *own), vmem(chips, *own),
+            vmem(groups, share, chunk, width), vmem(*own), vmem(*own),
+            dma((4, chips, parts * count)), dma((2, parts, groups, share)),
+            dma((2, parts, count)), dma((4, chips, parts * count)),
+        ]
+        + [vmem(count, chunk // parts, width)] * parts,
         compiler_params=params(5, 50),
-        name="server_pull",
-    )(rows_in, up_own, up_part, gain[None], context, half, gate_matrix, up_matrix, down_matrix)
+        name="serve",
+    )(
+        rows_in, up_own, up_part, gain[None], context, half, gate_matrix, up_matrix, down_matrix,
+        assigned,
+    )
 
 
 class Chain:
@@ -1062,34 +1095,6 @@
     return jnp.pad(matrix, ((0, 0), (0, LANES - matrix.shape[1])))
 
 
-def relay_back(assigned, pulled, up_own):
-    chips, client_count, group_count = axis_counts()
-    length, breadth = pulled.shape
-    chunk, width = length // client_count, breadth // (CORES * chips)
-    share = client_count // group_count
-    parts = len(parts_of(chunk))
-    full = (client_count, chunk, breadth)
-    own = (client_count, chunk, width)
-    dma = pltpu.SemaphoreType.DMA
-    vmem = lambda shape: pltpu.VMEM(shape, BF16)
-    grad = pl.pallas_call(
-        partial(back_kernel, chips, client_count, group_count),
-        out_shape=jax.ShapeDtypeStruct(full, BF16),
-        in_specs=[SMEM_SPEC, VMEM_SPEC, VMEM_SPEC],
-        out_specs=VMEM_SPEC,
-        scratch_shapes=[
-            vmem((chips,) + own), vmem((chips,) + own), vmem((chips,) + own),
-            vmem((group_count, share, chunk, width)), vmem(own), vmem(own),
-            dma((4, chips, parts * client_count)), dma((2, parts, group_count, share)),
-            dma((2, parts, client_count)), dma((4, chips, parts * client_count)),
-        ]
-        + [vmem((client_count, chunk // parts, width))] * parts,
-        compiler_params=params(2, 14),
-        name="relay_back",
-    )(assigned, pulled.reshape(full), up_own)
-    return grad.reshape(length, breadth)
-
-
 def local(
     client_input,
     client_gain,
@@ -1115,13 +1120,13 @@
         assignment, client_input, client_gain, table, upstream, matrices, kv_count
     )
     cut_rows = cut_rows.reshape(client_input.shape)
-    pulled, far_context, far_normed = server_pull(
-        cut_rows, up_own, up_part, server_gain[0], saved[3], half,
+    arriving_grad, far_context, far_normed = serve(
+        assignment, cut_rows, up_own, up_part, server_gain[0], saved[3], half,
         server_gate[0], server_up[0], server_down[0],
     )
+    arriving_grad = arriving_grad.reshape(client_input.shape)
     if half.ndim == 2:
         far_normed = across_groups(half_of(normed, client_count, 1 - lax.axis_index("sdata")))
-    arriving_grad = relay_back(assignment, pulled, up_own)
     query_update, key_update, value_update, output_update = emit(
         *learn(
             arriving_grad, output_weight[0], saved, normed, far_normed, far_context, table,

time: 144 us -> 139 us (0.965)
  Pallas kernels: 140 us -> 135 us
    pallas_call x2 -> x1, Pallas kernels: 43.9 us -> 39.4 us  [serve(): pl.pallas_call(partial(server_kernel, chips, groups, shares), out_shape=(...]
where the time goes in v4:
time: 139 us
  Pallas kernels  135 us (97%)
  local copies, waits for them, and re-layouts  2.3 us (2%)
    pallas_call x1, Pallas kernels, learn(): pl.pallas_call(partial(learn_kernel, kv_count, count, aligned), out_shape...  54.5 us
    pallas_call x1, Pallas kernels, depart(): pl.pallas_call(partial(depart_kernel, kv_count, sends_half, chips, count,...  40.6 us
    pallas_call x1, Pallas kernels, serve(): pl.pallas_call(partial(server_kernel, chips, groups, shares), out_shape=(...  39.4 us

profile of v4, /device:TPU:8, one launch (start us, length us, event | category | flops | bytes accessed | tf_op | source)
XLA Modules:
  0.0 138.5 jit_solution(934005478200048734)
XLA Ops:
  0.6 0.0 copy-start.3
  0.6 0.9 copy-done.3
  1.6 0.0 copy-start.6
  1.6 0.7 copy-done.6
  2.3 0.0 copy-start.7
  2.3 0.7 copy-done.7
  2.9 0.0 copy-start.5
  2.9 0.0 copy-start.8
  2.9 40.6 %depart.1 = (bf16[384,2048]{1,0:T(8,128)(2,1)}, bf16[2,384,256]{2,1,0:T(8,128)(2,1)S(1)}, bf16[384,512]{1,0:T(8,128)(2,1)S(1)}, bf16[384,128]{1,0:T(8,128)(2,1)S...) custom-call(s32[4]{0:T(128)S(1)} %copy-done.7, ...), custom_call_target="tpu_custom_call" | custom-call | tf_op jit(solution)/shard_map/depart/pallas_call | solution.py:367
  43.5 0.0 copy-done.5
  43.5 0.0 copy-done.8
  43.5 0.0 copy-start
  43.6 0.0 copy-start.1
  43.6 0.0 copy-start.2
  43.6 0.0 copy-start.4
  43.6 39.4 %serve.1 = (bf16[4,96,2048]{2,1,0:T(8,128)(2,1)S(1)}, bf16[384,512]{1,0:T(8,128)(2,1)S(1)}, bf16[4,384,256]{2,1,0:T(8,128)(2,1)S(1)}) custom-call(bf16[384,2048]{1,0:T(8,128)(2,1)} %bitcast.19, bf16[4,96,512]{2,1,0:T(8,128)(2,1)S(1)} %get-tuple-element.22.own_ref, bf16[4,96,2048]{2,1,0:T(8,128)(2,1)} %get-tuple-element.23.part_ref, ...), custom_call_target="tpu_custom_call" | custom-call | tf_op jit(solution)/shard_map/serve/pallas_call | solution.py:697
  83.0 0.0 copy-done
  83.0 0.0 copy-done.1
  83.0 0.0 copy-done.2
  83.0 0.0 copy-done.4
  83.0 54.5 %learn.1 = (bf16[256,512]{1,0:T(8,128)(2,1)S(1)}, bf16[256,128]{1,0:T(8,128)(2,1)S(1)}, bf16[256,128]{1,0:T(8,128)(2,1)S(1)}, bf16[256,512]{1,0:T(8,128)(2,1)S(1)}) custom-call(bf16[384,2048]{1,0:T(8,128)(2,1)S(1)} %bitcast.13, bf16[2048,512]{1,0:T(8,128)(2,1)S(1)} %bitcast.12, bf16[384,512]{1,0:T(8,128)(2,1)S(1)} %get-tuple-element.27.query_ref, ...), custom_call_target="tpu_custom_call" | custom-call | tf_op jit(solution)/shard_map/learn/pallas_call | solution.py:1029
  137.5 0.9 emit.1
Async XLA Ops:
  0.6 0.9 copy-start.3
  1.6 0.7 copy-start.6
  2.3 0.7 copy-start.7
  2.9 40.6 %copy-start.5 = (bf16[1,2048]{1,0:T(2,128)(2,1)S(1)}, bf16[1,2048]{1,0:T(2,128)(2,1)}, u32[]{:S(2)}) copy-start(bf16[1,2048]{1,0:T(2,128)(2,1)} %gain_hbm.1) | copy-start | bytes 12292
  2.9 40.6 %copy-start.8 = (s32[4]{0:T(128)S(1)}, s32[4]{0:T(128)}, u32[]{:S(2)}) copy-start(s32[4]{0:T(128)} %assigned.3) | copy-start | bytes 52
  43.5 39.4 %copy-start = (bf16[1,2048,512]{2,1,0:T(8,128)(2,1)S(1)}, bf16[1,2048,512]{2,1,0:T(8,128)(2,1)}, u32[]{:S(2)}) copy-start(bf16[1,2048,512]{2,1,0:T(8,128)(2,1)} %param.18) | copy-start | bytes 6291460
  43.6 39.4 %copy-start.1 = (bf16[4,768,384]{2,1,0:T(8,128)(2,1)S(1)}, bf16[4,768,384]{2,1,0:T(8,128)(2,1)}, u32[]{:S(2)}) copy-start(bf16[4,768,384]{2,1,0:T(8,128)(2,1)} %get-tuple-element.30.weights_ref) | copy-start | bytes 7077892
  43.6 39.4 %copy-start.2 = (bf16[384,2048]{1,0:T(8,128)(2,1)S(1)}, bf16[384,2048]{1,0:T(8,128)(2,1)}, u32[]{:S(2)}) copy-start(bf16[384,2048]{1,0:T(8,128)(2,1)} %get-tuple-element.31.normed_ref) | copy-start | bytes 4718596
  43.6 39.4 %copy-start.4 = (f32[384,128]{1,0:T(8,128)S(1)}, f32[384,128]{1,0:T(8,128)}, u32[]{:S(2)}) copy-start(f32[384,128]{1,0:T(8,128)} %constant.1.clone.refs_2_.table_ref) | copy-start | bytes 589828

commit v5 on v4

--- a/solution.py
+++ b/solution.py
@@ -588,7 +588,7 @@
 ):
     length, breadth = rows_ref.shape
     hidden = gate_ref.shape[1]
-    block = next(b for b in (512, 256, 128, hidden) if hidden % b == 0)
+    block = next(b for b in (1024, 512, 256, 128, hidden) if hidden % b == 0)
     spans = [slice(at, at + block) for at in range(0, hidden, block)]
 
     def loads(i, which):

time: 139 us -> 139 us (level)
  no operation moved by 1% of the time
where the time goes in v5:
time: 139 us; the launch traced here: 138 us
  Pallas kernels  135 us (97%)
  local copies, waits for them, and re-layouts  2.3 us (2%)
    pallas_call x1, Pallas kernels, learn(): pl.pallas_call(partial(learn_kernel, kv_count, count, aligned), out_shape...  54.5 us
    pallas_call x1, Pallas kernels, depart(): pl.pallas_call(partial(depart_kernel, kv_count, sends_half, chips, count,...  40.6 us
    pallas_call x1, Pallas kernels, serve(): pl.pallas_call(partial(server_kernel, chips, groups, shares), out_shape=(...  38.8 us

profile of v5, /device:TPU:8, one launch (start us, length us, event | category | flops | bytes accessed | tf_op | source)
XLA Modules:
  0.0 138.0 jit_solution(7907093316992753316)
XLA Ops:
  0.6 0.0 copy-start.3
  0.6 0.9 copy-done.3
  1.6 0.0 copy-start.6
  1.6 0.7 copy-done.6
  2.3 0.0 copy-start.7
  2.3 0.7 copy-done.7
  2.9 0.0 copy-start.5
  2.9 0.0 copy-start.8
  2.9 40.6 %depart.1 = (bf16[384,2048]{1,0:T(8,128)(2,1)}, bf16[2,384,256]{2,1,0:T(8,128)(2,1)S(1)}, bf16[384,512]{1,0:T(8,128)(2,1)S(1)}, bf16[384,128]{1,0:T(8,128)(2,1)S...) custom-call(s32[4]{0:T(128)S(1)} %copy-done.7, ...), custom_call_target="tpu_custom_call" | custom-call | tf_op jit(solution)/shard_map/depart/pallas_call | solution.py:367
  43.5 0.0 copy-done.5
  43.5 0.0 copy-done.8
  43.5 0.0 copy-start
  43.6 0.0 copy-start.1
  43.6 0.0 copy-start.2
  43.6 0.0 copy-start.4
  43.6 38.8 %serve.1 = (bf16[4,96,2048]{2,1,0:T(8,128)(2,1)S(1)}, bf16[384,512]{1,0:T(8,128)(2,1)S(1)}, bf16[4,384,256]{2,1,0:T(8,128)(2,1)S(1)}) custom-call(bf16[384,2048]{1,0:T(8,128)(2,1)} %bitcast.19, bf16[4,96,512]{2,1,0:T(8,128)(2,1)S(1)} %get-tuple-element.22.own_ref, bf16[4,96,2048]{2,1,0:T(8,128)(2,1)} %get-tuple-element.23.part_ref, ...), custom_call_target="tpu_custom_call" | custom-call | tf_op jit(solution)/shard_map/serve/pallas_call | solution.py:697
  82.4 0.0 copy-done
  82.4 0.0 copy-done.1
  82.4 0.0 copy-done.2
  82.4 0.0 copy-done.4
  82.5 54.5 %learn.1 = (bf16[256,512]{1,0:T(8,128)(2,1)S(1)}, bf16[256,128]{1,0:T(8,128)(2,1)S(1)}, bf16[256,128]{1,0:T(8,128)(2,1)S(1)}, bf16[256,512]{1,0:T(8,128)(2,1)S(1)}) custom-call(bf16[384,2048]{1,0:T(8,128)(2,1)S(1)} %bitcast.13, bf16[2048,512]{1,0:T(8,128)(2,1)S(1)} %bitcast.12, bf16[384,512]{1,0:T(8,128)(2,1)S(1)} %get-tuple-element.27.query_ref, ...), custom_call_target="tpu_custom_call" | custom-call | tf_op jit(solution)/shard_map/learn/pallas_call | solution.py:1029
  136.9 0.9 emit.1
Async XLA Ops:
  0.6 0.9 copy-start.3
  1.6 0.7 copy-start.6
  2.3 0.7 copy-start.7
  2.9 40.6 %copy-start.5 = (bf16[1,2048]{1,0:T(2,128)(2,1)S(1)}, bf16[1,2048]{1,0:T(2,128)(2,1)}, u32[]{:S(2)}) copy-start(bf16[1,2048]{1,0:T(2,128)(2,1)} %gain_hbm.1) | copy-start | bytes 12292
  2.9 40.6 %copy-start.8 = (s32[4]{0:T(128)S(1)}, s32[4]{0:T(128)}, u32[]{:S(2)}) copy-start(s32[4]{0:T(128)} %assigned.3) | copy-start | bytes 52
  43.5 38.9 %copy-start = (bf16[1,2048,512]{2,1,0:T(8,128)(2,1)S(1)}, bf16[1,2048,512]{2,1,0:T(8,128)(2,1)}, u32[]{:S(2)}) copy-start(bf16[1,2048,512]{2,1,0:T(8,128)(2,1)} %param.18) | copy-start | bytes 6291460
  43.6 38.9 %copy-start.1 = (bf16[4,768,384]{2,1,0:T(8,128)(2,1)S(1)}, bf16[4,768,384]{2,1,0:T(8,128)(2,1)}, u32[]{:S(2)}) copy-start(bf16[4,768,384]{2,1,0:T(8,128)(2,1)} %get-tuple-element.30.weights_ref) | copy-start | bytes 7077892
  43.6 38.9 %copy-start.2 = (bf16[384,2048]{1,0:T(8,128)(2,1)S(1)}, bf16[384,2048]{1,0:T(8,128)(2,1)}, u32[]{:S(2)}) copy-start(bf16[384,2048]{1,0:T(8,128)(2,1)} %get-tuple-element.31.normed_ref) | copy-start | bytes 4718596
  43.6 38.9 %copy-start.4 = (f32[384,128]{1,0:T(8,128)S(1)}, f32[384,128]{1,0:T(8,128)}, u32[]{:S(2)}) copy-start(f32[384,128]{1,0:T(8,128)} %constant.1.clone.refs_2_.table_ref) | copy-start | bytes 589828
